TPU v7x, 32 devices: a whole 2x2x4 slice. The times are simulated.
32 devices in a mesh: rep: 2 (over x), dp: 16 (over y, z, core).
Axes of the slice: x: 2, y: 2, z: 4, core: 2. Of those that a mesh axis runs over, the one named last changes fastest.
Arguments:
- x: bfloat16 [32, 2048, 640], P(('rep', 'dp')), parts along dimension 0
- dy: bfloat16 [32, 2048, 640], P(('rep', 'dp')), parts along dimension 0
- w_gate: bfloat16 [2, 640, 2048], replicated
- w_up: bfloat16 [2, 640, 2048], replicated
- w_down: bfloat16 [2, 2048, 640], replicated
- m_w_gate: float32 [2, 640, 2048], P(None, 'dp')
- m_w_up: float32 [2, 640, 2048], P(None, 'dp')
- m_w_down: float32 [2, 2048, 640], P(None, 'dp')
- v_w_gate: float32 [2, 640, 2048], P(None, 'dp')
- v_w_up: float32 [2, 640, 2048], P(None, 'dp')
- v_w_down: float32 [2, 2048, 640], P(None, 'dp')
Outputs:
- output 1: bfloat16 [4, 640, 2048], P('rep'), parts along dimension 0
- output 2: bfloat16 [4, 640, 2048], P('rep'), parts along dimension 0
- output 3: bfloat16 [4, 2048, 640], P('rep'), parts along dimension 0
- output 4: float32 [4, 640, 2048], P('rep', 'dp'), parts along dimension 0
- output 5: float32 [4, 640, 2048], P('rep', 'dp'), parts along dimension 0
- output 6: float32 [4, 2048, 640], P('rep', 'dp'), parts along dimension 0
- output 7: float32 [4, 640, 2048], P('rep', 'dp'), parts along dimension 0
- output 8: float32 [4, 640, 2048], P('rep', 'dp'), parts along dimension 0
- output 9: float32 [4, 2048, 640], P('rep', 'dp'), parts along dimension 0
There are 2 independent parts. A program takes and returns all parts, laid end to end along the dimension named above; an argument that names none is the same for every part.
All inputs are finite; a program needn't handle non-finite values.
Results may differ from a plain program's by a relative error of at most 0.022.
Values are sent between devices in bfloat16 or wider.
A program may use at most 2 GiB of HBM per device.

v0:
```python
import jax
import jax.numpy as jnp
from jax import lax

NAMES = ("w_gate", "w_up", "w_down")


def matmul(a, w):
    return jnp.dot(a, w, preferred_element_type=jnp.float32).astype(jnp.bfloat16)


def normed(h):
    wide = h.astype(jnp.float32)
    scale = lax.rsqrt(jnp.mean(wide**2, -1, keepdims=True) + 1e-6)
    return (wide * scale).astype(jnp.bfloat16)


def layer(h, w):
    a = normed(h)
    gate = jnp.dot(a, w["w_gate"], preferred_element_type=jnp.float32)
    up = jnp.dot(a, w["w_up"], preferred_element_type=jnp.float32)
    return h + matmul((jax.nn.silu(gate) * up).astype(jnp.bfloat16), w["w_down"])


def adamw(w, m, v, g):
    m = 0.9 * m + 0.1 * g
    v = 0.95 * v + 0.05 * g * g
    step = m * lax.rsqrt(v + 1e-8) + 0.1 * w
    return (w - 0.02 * step).astype(jnp.bfloat16), m, v


def clipped(gradients, sum_of_squares, count):
    factor = jnp.minimum(1.0, 0.5 * lax.rsqrt(sum_of_squares / count + 1e-30))
    return [g * factor for g in gradients]


def stack(weights, h):
    for number in range(weights["w_gate"].shape[0]):
        h = layer(h, {name: w[number] for name, w in weights.items()})
    return h


def solution(mesh):
    groups = mesh.shape["rep"]

    def step(x, dy, *arrays):
        weights, m, v = (arrays[i : i + 3] for i in (0, 3, 6))
        x, dy = (t.reshape(groups, -1, *t.shape[1:]) for t in (x, dy))

        def of_a_group(x, dy):
            _, back = jax.vjp(lambda w: stack(w, x), dict(zip(NAMES, weights, strict=True)))
            by_weights = back(dy)[0]
            gradients = [by_weights[name].astype(jnp.float32) for name in NAMES]
            gradients = clipped(gradients, sum(jnp.sum(g * g) for g in gradients), sum(g.size for g in gradients))
            new = [adamw(w.astype(jnp.float32), m, v, g) for w, m, v, g in zip(weights, m, v, gradients, strict=True)]
            return tuple(one[which] for which in range(3) for one in new)

        return tuple(t.reshape(-1, *t.shape[2:]) for t in jax.vmap(of_a_group)(x, dy))

    return step
```

profile of v0, /device:TPU:0, one launch (start us, length us, event | category | flops | bytes accessed | tf_op | source)
XLA Modules:
  0.0 1124.0 jit_solution(6360464328116078352)
XLA Ops:
  16.7 11.3 %convolution_convert_fusion.1 = bf16[2048,2048]{1,0:T(8,128)(2,1)} fusion(bf16[1,2048,640]{2,1,0:T(8,128)(2,1)} %param.17, bf16[2,2048,640]{2,1,0:T(8,128)(2,1)} %param.16), kind=kOutput, calls=%fused_computation.205 | convolution fusion | flops 5372903424 | bytes 13631488 | tf_op jit(solution)/vmap(transpose(jvp()))/dot_general | solution.py:9
  28.1 11.6 %fusion.198 = f32[2048,2048]{1,0:T(8,128)} fusion(bf16[2,640,2048]{2,1,0:T(8,128)(2,1)} %param.12, bf16[1,2048,640]{2,1,0:T(8,128)(2,1)S(1)} %copy-done.14, f32[2048]{0:T(1024)S(1)} %add_rsqrt_fusion), kind=kOutput, calls=%fused_computation.238 | convolution fusion | flops 5372641280 | bytes 22028288 | tf_op jit(solution)/vmap(jvp())/dot_general | solution.py:20
  39.6 18.6 %fusion.156 = (bf16[1,1,2048,2048]{3,2,1,0:T(8,128)(2,1)}, f32[2048,2048]{1,0:T(8,128)}) fusion(f32[2048,2048]{1,0:T(8,128)} %fusion.198, bf16[2,640,2048]{2,1,0:T(8,128)(2,1)} %param.15, bf16[1,2048,640]{2,1,0:T(8,128)(2,1)S(1)} %copy-done.14, f32[2048]{0:T(1024)S(1)} %add_rsqrt_fusion), kind=kOutput, calls=%fused_computation.191 | convolution fusion | flops 5397807104 | bytes 47194112 | tf_op jit(solution)/vmap(jvp())/dot_general | solution.py:21
  58.3 12.4 %copy.4 = bf16[1,1,2048,2048]{2,3,1,0:T(8,128)(2,1)} copy(bf16[1,1,2048,2048]{3,2,1,0:T(8,128)(2,1)} %get-tuple-element.263) | data formatting | bytes 16777216
  70.6 9.5 fusion.166
  81.0 13.0 %fusion.187 = f32[2048,2048]{1,0:T(8,128)} fusion(bf16[1,1,2048,640]{2,3,1,0:T(8,128)(2,1)S(1)} %fusion.167, bf16[2,640,2048]{2,1,0:T(8,128)(2,1)} %param.15), kind=kOutput, calls=%fused_computation.227 | convolution fusion | flops 5368709120 | bytes 22020096 | tf_op jit(solution)/vmap(jvp())/dot_general | solution.py:21
  94.0 21.1 %fusion.145 = (bf16[1,1,2048,2048]{3,2,1,0:T(8,128)(2,1)S(1)}, bf16[1,1,2048,2048]{3,2,1,0:T(8,128)(2,1)S(1)}, f32[2048,2048]{1,0:T(8,128)}) fusion(f32[2048,2048]{1,0:T(8,128)} %fusion.187, bf16[2048,2048]{1,0:T(8,128)(2,1)} %convolution_convert_fusion.1, bf16[2,640,2048]{2,1,0:T(8,128)(2,1)} %param.12, bf16[1,1,2048,640]{2,3,1,0:T(8,128)(2,1)S(1)} %fusion.167), kind=kOutput, calls=%fused_computation.175 | convolution fusion | flops 5431623680 | bytes 63963136 | tf_op jit(solution)/vmap(jvp())/dot_general | solution.py:20
  115.1 8.4 fusion.172
  123.5 19.1 %fusion.168 = (f32[2048]{0:T(1024)S(1)}, bf16[2048,640]{0,1:T(8,128)(2,1)S(1)}) fusion(bf16[1,1,2048,640]{2,3,1,0:T(8,128)(2,1)S(1)} %get-tuple-element.266, bf16[2048,640]{0,1:T(8,128)(2,1)S(1)} %fusion.172, bf16[2,640,2048]{2,1,0:T(8,128)(2,1)} %param.12, bf16[1,1,2048,2048]{3,2,1,0:T(8,128)(2,1)S(1)} %get-tuple-element.544), kind=kOutput, calls=%fused_computation.215 | convolution fusion | flops 5375260672 | bytes 18882560 | tf_op jit(solution)/vmap(transpose(jvp()))/dot_general | solution.py:20
  149.3 107.2 %while.17 = (bf16[1,1,2048,2048]{2,3,1,0:T(8,128)(2,1)}, bf16[1,1,2048,640]{3,2,1,0:T(8,128)(2,1)S(1)}, f32[1,128,640]{2,1,0:T(8,128)S(1)}, f32[1,128,640]{2,1,0...) while((bf16[1,1,2048,2048]{2,3,1,0:T(8,128)(2,1)}, ...), condition=%wide.windowed_dot_general_cond_rs.5.clone, body=%wide.windowed_dot_general_body_rs.5.clone.sunk | while | flops 1346863104 | bytes 67371648 | solution.py:9
  150.7 5.0 collective-permute-start.21
  167.4 7.1 collective-permute-done.22
  188.9 4.7 collective-permute-start.23
  194.6 6.5 collective-permute-done.22
  216.4 4.7 collective-permute-start.23
  222.0 6.5 collective-permute-done.22
  243.5 4.7 collective-permute-start.23
  249.2 6.5 collective-permute-done.22
  256.5 15.0 %fusion.155 = bf16[1,1,2048,2048]{3,2,1,0:T(8,128)(2,1)} fusion(f32[2048,2048]{1,0:T(8,128)} %fusion.187, f32[2048,2048]{1,0:T(8,128)} %get-tuple-element.267), kind=kLoop, calls=%fused_computation.189 | loop fusion | flops 25165824 | bytes 41943040 | tf_op jit(solution)/vmap(jvp())/convert_element_type | solution.py:22
  271.5 12.4 %copy.2 = bf16[1,1,2048,2048]{2,3,1,0:T(8,128)(2,1)} copy(bf16[1,1,2048,2048]{3,2,1,0:T(8,128)(2,1)} %fusion.155) | data formatting | bytes 16777216
  287.1 107.7 %while.16 = (bf16[1,1,2048,2048]{2,3,1,0:T(8,128)(2,1)}, bf16[1,1,2048,640]{3,2,1,0:T(8,128)(2,1)S(1)}, f32[1,128,640]{2,1,0:T(8,128)S(1)}, f32[1,128,640]{2,1,0...) while((bf16[1,1,2048,2048]{2,3,1,0:T(8,128)(2,1)}, ...), condition=%wide.windowed_dot_general_cond_rs.4.clone, body=%wide.windowed_dot_general_body_rs.4.clone.sunk | while | flops 1346863104 | bytes 67371648 | solution.py:9
  300.2 4.7 collective-permute-start.19
  305.8 6.5 collective-permute-done.18
  326.9 4.7 collective-permute-start.19
  332.5 6.5 collective-permute-done.18
  354.2 4.7 collective-permute-start.19
  359.9 6.5 collective-permute-done.18
  381.7 4.7 collective-permute-start.19
  387.4 6.5 collective-permute-done.18
  398.9 22.1 %convert_multiply_fusion = (bf16[1,1,2048,2048]{3,2,1,0:T(8,128)(2,1)}, bf16[1,1,2048,2048]{3,2,1,0:T(8,128)(2,1)}) fusion(f32[2048,2048]{1,0:T(8,128)} %fusion.198, f32[2048,2048]{1,0:T(8,128)} %get-tuple-element.264, bf16[2,2048,640]{2,1,0:T(8,128)(2,1)} %param.16, bf16[1,1,2048,640]{2,3,1,0:T(8,128)(2,1)S(1)} %copy-done.13), kind=kOutput, calls=%fused_computation.170 | convolution fusion | flops 5435817984 | bytes 55574528 | tf_op jit(solution)/vmap(transpose(jvp()))/dot_general | solution.py:9
  421.0 113.1 %while.15 = (bf16[1,1,2048,640]{2,3,1,0:T(8,128)(2,1)}, bf16[1,1,2048,2048]{3,2,1,0:T(8,128)(2,1)}, f32[1,40,2048]{2,1,0:T(8,128)S(1)}, f32[1,40,2048]{2,1,0:T(8...) while((bf16[1,1,2048,640]{2,3,1,0:T(8,128)(2,1)}, ...), condition=%wide.windowed_dot_general_cond_rs.3.clone, body=%wide.windowed_dot_general_body_rs.3.clone.sunk | while | flops 1343979520 | bytes 69468848 | solution.py:21
  428.9 5.3 fusion.335
  441.8 5.5 collective-permute-done.14
  457.1 5.3 fusion.335
  485.5 5.3 fusion.335
  513.9 5.3 fusion.335
  534.8 118.6 %while.14 = (bf16[1,1,2048,640]{2,3,1,0:T(8,128)(2,1)S(1)}, bf16[1,1,2048,2048]{3,2,1,0:T(8,128)(2,1)}, f32[1,40,2048]{2,1,0:T(8,128)}, f32[1,40,2048]{2,1,0:T(8...) while((bf16[1,1,2048,640]{2,3,1,0:T(8,128)(2,1)S(1)}, ...), condition=%wide.windowed_dot_general_cond_rs.2.clone, body=%wide.windowed_dot_general_body_rs.2.clone.sunk | while | flops 1343979520 | bytes 58983060 | solution.py:21
  543.5 5.1 fusion.327
  557.1 5.0 collective-permute-done.10
  574.5 5.1 fusion.327
  586.9 4.7 collective-permute-done.10
  604.6 5.1 fusion.327
  617.0 4.7 collective-permute-done.10
  634.7 5.1 fusion.327
  647.1 4.7 collective-permute-done.10
  653.4 115.3 %while.13 = (bf16[1,1,2048,640]{2,3,1,0:T(8,128)(2,1)}, bf16[1,1,2048,2048]{3,2,1,0:T(8,128)(2,1)}, f32[1,40,2048]{2,1,0:T(8,128)S(1)}, f32[1,40,2048]{2,1,0:T(8...) while((bf16[1,1,2048,640]{2,3,1,0:T(8,128)(2,1)}, ...), condition=%wide.windowed_dot_general_cond_rs.1.clone, body=%wide.windowed_dot_general_body_rs.1.clone.sunk | while | flops 1343979520 | bytes 69468848 | solution.py:20
  661.8 5.3 fusion.319
  691.1 5.3 fusion.319
  720.4 5.3 fusion.319
  749.7 5.3 fusion.319
  768.7 112.7 %while.12 = (bf16[1,1,2048,640]{2,3,1,0:T(8,128)(2,1)S(1)}, bf16[1,1,2048,2048]{3,2,1,0:T(8,128)(2,1)}, f32[1,40,2048]{2,1,0:T(8,128)S(1)}, f32[1,40,2048]{2,1,0...) while((bf16[1,1,2048,640]{2,3,1,0:T(8,128)(2,1)S(1)}, ...), condition=%wide.windowed_dot_general_cond_rs.clone, body=%wide.windowed_dot_general_body_rs.clone.sunk | while | flops 1343979520 | bytes 58983060 | solution.py:20
  777.1 5.1 fusion.311
  789.4 4.8 collective-permute-done.2
  805.8 5.1 fusion.311
  818.1 4.8 collective-permute-done.2
  834.5 5.1 fusion.311
  846.8 4.8 collective-permute-done.2
  863.2 5.1 fusion.311
  875.5 4.8 collective-permute-done.2
  900.6 30.6 %all-reduce.10 = f32[1]{0:T(128)} all-reduce(f32[1]{0:T(128)} %bitcast.39), channel_id=13, replica_groups=mesh['rep'=2,'dp'=16] {'dp'}, use_global_device_ids=true, to_apply=%region_3.4.clone | all-reduce | flops 1 | bytes 8 | tf_op jit(solution)/vmap()/reduce_sum | solution.py:54
  940.4 51.0 %all-gather.14.cloned.1.call-done = bf16[1,2,2048,640]{3,2,1,0:T(8,128)(2,1)} async-done(((bf16[1,2,128,640]{3,2,1,0:T(8,128)(2,1)}), bf16[1,2,2048,640]{3,2,1,0:T(8,128)(2,1)}) %all-gather.14.cloned.1.call-update) | async-done | bytes 5242896 | tf_op jit(solution)/reshape | solution.py:58
  991.5 57.4 %all-gather.12.cloned.1.call-done = bf16[1,2,640,2048]{3,2,1,0:T(8,128)(2,1)} async-done(((bf16[1,2,40,2048]{3,2,1,0:T(8,128)(2,1)}), bf16[1,2,640,2048]{3,2,1,0:T(8,128)(2,1)}) %all-gather.12.cloned.1.call-update) | async-done | bytes 5242896 | tf_op jit(solution)/reshape | solution.py:58
  1048.9 57.4 %all-gather.10.cloned.1.call-done = bf16[1,2,640,2048]{3,2,1,0:T(8,128)(2,1)} async-done(((bf16[1,2,40,2048]{3,2,1,0:T(8,128)(2,1)}), bf16[1,2,640,2048]{3,2,1,0:T(8,128)(2,1)}) %all-gather.10.cloned.1.call-update) | async-done | bytes 5242896 | tf_op jit(solution)/reshape | solution.py:58
  1106.3 6.2 copy.63
  (529 shorter events, 467.1 us)
Async XLA Ops:
  7.2 984.3 %all-gather.14.cloned.1.call-start = ((), (), s32[]{:S(2)}) async-start(), calls=%async_computation.2 | async-start | bytes 5570560 | tf_op jit(solution)/reshape | solution.py:58
  161.9 12.5 %collective-permute-start.22 = (f32[1,128,640]{2,1,0:T(8,128)S(1)}, f32[1,128,640]{2,1,0:T(8,128)S(1)}, u32[]{:S(2)}, u32[]{:S(2)}) collective-permute-start(f32[1,128,640]{2,1,0:T(8,128)S(1)} %get-tuple-element.500), channel_id=37, source_target_pairs={{0,1},{1,2},{2,3},{3,4},{4,5},{5,6},{6,7},{7,8},{8,9},{9,10},{10,1... | collective-permute-start | bytes 983048 | tf_op jit(solution)/vmap(transpose(jvp()))/dot_general | solution.py:9
  188.8 12.3 %collective-permute-start.22 = (f32[1,128,640]{2,1,0:T(8,128)S(1)}, f32[1,128,640]{2,1,0:T(8,128)S(1)}, u32[]{:S(2)}, u32[]{:S(2)}) collective-permute-start(f32[1,128,640]{2,1,0:T(8,128)S(1)} %get-tuple-element.500), channel_id=37, source_target_pairs={{0,1},{1,2},{2,3},{3,4},{4,5},{5,6},{6,7},{7,8},{8,9},{9,10},{10,1... | collective-permute-start | bytes 983048 | tf_op jit(solution)/vmap(transpose(jvp()))/dot_general | solution.py:9
  188.9 12.6 %collective-permute-start.23 = (f32[1,128,640]{2,1,0:T(8,128)S(1)}, f32[1,128,640]{2,1,0:T(8,128)S(1)}, u32[]{:S(2)}, u32[]{:S(2)}) collective-permute-start(f32[1,128,640]{2,1,0:T(8,128)S(1)} %get-tuple-element.501), channel_id=36, source_target_pairs={{0,15},{1,0},{2,1},{3,2},{4,3},{5,4},{6,5},{7,6},{8,7},{9,8},{10,9... | collective-permute-start | bytes 983048 | tf_op jit(solution)/vmap(transpose(jvp()))/dot_general | solution.py:9
  216.3 12.3 %collective-permute-start.22 = (f32[1,128,640]{2,1,0:T(8,128)S(1)}, f32[1,128,640]{2,1,0:T(8,128)S(1)}, u32[]{:S(2)}, u32[]{:S(2)}) collective-permute-start(f32[1,128,640]{2,1,0:T(8,128)S(1)} %get-tuple-element.500), channel_id=37, source_target_pairs={{0,1},{1,2},{2,3},{3,4},{4,5},{5,6},{6,7},{7,8},{8,9},{9,10},{10,1... | collective-permute-start | bytes 983048 | tf_op jit(solution)/vmap(transpose(jvp()))/dot_general | solution.py:9
  216.4 12.3 %collective-permute-start.23 = (f32[1,128,640]{2,1,0:T(8,128)S(1)}, f32[1,128,640]{2,1,0:T(8,128)S(1)}, u32[]{:S(2)}, u32[]{:S(2)}) collective-permute-start(f32[1,128,640]{2,1,0:T(8,128)S(1)} %get-tuple-element.501), channel_id=36, source_target_pairs={{0,15},{1,0},{2,1},{3,2},{4,3},{5,4},{6,5},{7,6},{8,7},{9,8},{10,9... | collective-permute-start | bytes 983048 | tf_op jit(solution)/vmap(transpose(jvp()))/dot_general | solution.py:9
  243.5 12.3 %collective-permute-start.22 = (f32[1,128,640]{2,1,0:T(8,128)S(1)}, f32[1,128,640]{2,1,0:T(8,128)S(1)}, u32[]{:S(2)}, u32[]{:S(2)}) collective-permute-start(f32[1,128,640]{2,1,0:T(8,128)S(1)} %get-tuple-element.500), channel_id=37, source_target_pairs={{0,1},{1,2},{2,3},{3,4},{4,5},{5,6},{6,7},{7,8},{8,9},{9,10},{10,1... | collective-permute-start | bytes 983048 | tf_op jit(solution)/vmap(transpose(jvp()))/dot_general | solution.py:9
  243.5 12.2 %collective-permute-start.23 = (f32[1,128,640]{2,1,0:T(8,128)S(1)}, f32[1,128,640]{2,1,0:T(8,128)S(1)}, u32[]{:S(2)}, u32[]{:S(2)}) collective-permute-start(f32[1,128,640]{2,1,0:T(8,128)S(1)} %get-tuple-element.501), channel_id=36, source_target_pairs={{0,15},{1,0},{2,1},{3,2},{4,3},{5,4},{6,5},{7,6},{8,7},{9,8},{10,9... | collective-permute-start | bytes 983048 | tf_op jit(solution)/vmap(transpose(jvp()))/dot_general | solution.py:9
  256.5 626.2 %collective-permute-start.29 = (f32[1,128,640]{2,1,0:T(8,128)}, f32[1,128,640]{2,1,0:T(8,128)}, u32[]{:S(2)}, u32[]{:S(2)}) collective-permute-start(f32[1,128,640]{2,1,0:T(8,128)} %get-tuple-element.47), channel_id=38, source_target_pairs={{0,1},{1,2},{2,3},{3,4},{4,5},{5,6},{6,7},{7,8},{8,9},{9,10},{10,1... | collective-permute-start | bytes 983048 | tf_op jit(solution)/vmap(transpose(jvp()))/dot_general | solution.py:9
  300.1 12.3 %collective-permute-start.18 = (f32[1,128,640]{2,1,0:T(8,128)S(1)}, f32[1,128,640]{2,1,0:T(8,128)S(1)}, u32[]{:S(2)}, u32[]{:S(2)}) collective-permute-start(f32[1,128,640]{2,1,0:T(8,128)S(1)} %get-tuple-element.491), channel_id=31, source_target_pairs={{0,1},{1,2},{2,3},{3,4},{4,5},{5,6},{6,7},{7,8},{8,9},{9,10},{10,1... | collective-permute-start | bytes 983048 | tf_op jit(solution)/vmap(transpose(jvp()))/dot_general | solution.py:9
  300.2 12.2 %collective-permute-start.19 = (f32[1,128,640]{2,1,0:T(8,128)S(1)}, f32[1,128,640]{2,1,0:T(8,128)S(1)}, u32[]{:S(2)}, u32[]{:S(2)}) collective-permute-start(f32[1,128,640]{2,1,0:T(8,128)S(1)} %get-tuple-element.492), channel_id=30, source_target_pairs={{0,15},{1,0},{2,1},{3,2},{4,3},{5,4},{6,5},{7,6},{8,7},{9,8},{10,9... | collective-permute-start | bytes 983048 | tf_op jit(solution)/vmap(transpose(jvp()))/dot_general | solution.py:9
  326.8 12.3 %collective-permute-start.18 = (f32[1,128,640]{2,1,0:T(8,128)S(1)}, f32[1,128,640]{2,1,0:T(8,128)S(1)}, u32[]{:S(2)}, u32[]{:S(2)}) collective-permute-start(f32[1,128,640]{2,1,0:T(8,128)S(1)} %get-tuple-element.491), channel_id=31, source_target_pairs={{0,1},{1,2},{2,3},{3,4},{4,5},{5,6},{6,7},{7,8},{8,9},{9,10},{10,1... | collective-permute-start | bytes 983048 | tf_op jit(solution)/vmap(transpose(jvp()))/dot_general | solution.py:9
  326.9 12.5 %collective-permute-start.19 = (f32[1,128,640]{2,1,0:T(8,128)S(1)}, f32[1,128,640]{2,1,0:T(8,128)S(1)}, u32[]{:S(2)}, u32[]{:S(2)}) collective-permute-start(f32[1,128,640]{2,1,0:T(8,128)S(1)} %get-tuple-element.492), channel_id=30, source_target_pairs={{0,15},{1,0},{2,1},{3,2},{4,3},{5,4},{6,5},{7,6},{8,7},{9,8},{10,9... | collective-permute-start | bytes 983048 | tf_op jit(solution)/vmap(transpose(jvp()))/dot_general | solution.py:9
  354.2 12.3 %collective-permute-start.18 = (f32[1,128,640]{2,1,0:T(8,128)S(1)}, f32[1,128,640]{2,1,0:T(8,128)S(1)}, u32[]{:S(2)}, u32[]{:S(2)}) collective-permute-start(f32[1,128,640]{2,1,0:T(8,128)S(1)} %get-tuple-element.491), channel_id=31, source_target_pairs={{0,1},{1,2},{2,3},{3,4},{4,5},{5,6},{6,7},{7,8},{8,9},{9,10},{10,1... | collective-permute-start | bytes 983048 | tf_op jit(solution)/vmap(transpose(jvp()))/dot_general | solution.py:9
  354.2 12.6 %collective-permute-start.19 = (f32[1,128,640]{2,1,0:T(8,128)S(1)}, f32[1,128,640]{2,1,0:T(8,128)S(1)}, u32[]{:S(2)}, u32[]{:S(2)}) collective-permute-start(f32[1,128,640]{2,1,0:T(8,128)S(1)} %get-tuple-element.492), channel_id=30, source_target_pairs={{0,15},{1,0},{2,1},{3,2},{4,3},{5,4},{6,5},{7,6},{8,7},{9,8},{10,9... | collective-permute-start | bytes 983048 | tf_op jit(solution)/vmap(transpose(jvp()))/dot_general | solution.py:9
  381.7 12.3 %collective-permute-start.18 = (f32[1,128,640]{2,1,0:T(8,128)S(1)}, f32[1,128,640]{2,1,0:T(8,128)S(1)}, u32[]{:S(2)}, u32[]{:S(2)}) collective-permute-start(f32[1,128,640]{2,1,0:T(8,128)S(1)} %get-tuple-element.491), channel_id=31, source_target_pairs={{0,1},{1,2},{2,3},{3,4},{4,5},{5,6},{6,7},{7,8},{8,9},{9,10},{10,1... | collective-permute-start | bytes 983048 | tf_op jit(solution)/vmap(transpose(jvp()))/dot_general | solution.py:9
  381.7 12.2 %collective-permute-start.19 = (f32[1,128,640]{2,1,0:T(8,128)S(1)}, f32[1,128,640]{2,1,0:T(8,128)S(1)}, u32[]{:S(2)}, u32[]{:S(2)}) collective-permute-start(f32[1,128,640]{2,1,0:T(8,128)S(1)} %get-tuple-element.492), channel_id=30, source_target_pairs={{0,15},{1,0},{2,1},{3,2},{4,3},{5,4},{6,5},{7,6},{8,7},{9,8},{10,9... | collective-permute-start | bytes 983048 | tf_op jit(solution)/vmap(transpose(jvp()))/dot_general | solution.py:9
  394.7 489.2 %collective-permute-start.28 = (f32[1,128,640]{2,1,0:T(8,128)}, f32[1,128,640]{2,1,0:T(8,128)}, u32[]{:S(2)}, u32[]{:S(2)}) collective-permute-start(f32[1,128,640]{2,1,0:T(8,128)} %get-tuple-element.45), channel_id=32, source_target_pairs={{0,1},{1,2},{2,3},{3,4},{4,5},{5,6},{6,7},{7,8},{8,9},{9,10},{10,1... | collective-permute-start | bytes 983048 | tf_op jit(solution)/vmap(transpose(jvp()))/dot_general | solution.py:9
  421.1 13.1 %collective-permute-start.12 = (f32[1,40,2048]{2,1,0:T(8,128)S(1)}, f32[1,40,2048]{2,1,0:T(8,128)}, u32[]{:S(2)}, u32[]{:S(2)}) collective-permute-start(f32[1,40,2048]{2,1,0:T(8,128)S(1)} %broadcast_select_fusion.30), channel_id=22, source_target_pairs={{0,1},{1,2},{2,3},{3,4},{4,5},{5,6},{6,7},{7,8},{8,9},{9,10},{10,1... | collective-permute-start | bytes 983048 | tf_op jit(solution)/vmap(transpose(jvp()))/dot_general | solution.py:21
  421.9 12.3 %collective-permute-start.13 = (f32[1,40,2048]{2,1,0:T(8,128)}, f32[1,40,2048]{2,1,0:T(8,128)S(1)}, u32[]{:S(2)}, u32[]{:S(2)}) collective-permute-start(f32[1,40,2048]{2,1,0:T(8,128)} %broadcast_select_fusion.31), channel_id=21, source_target_pairs={{0,15},{1,0},{2,1},{3,2},{4,3},{5,4},{6,5},{7,6},{8,7},{9,8},{10,9... | collective-permute-start | bytes 983048 | tf_op jit(solution)/vmap(transpose(jvp()))/dot_general | solution.py:21
  449.1 13.3 %collective-permute-start.12 = (f32[1,40,2048]{2,1,0:T(8,128)S(1)}, f32[1,40,2048]{2,1,0:T(8,128)}, u32[]{:S(2)}, u32[]{:S(2)}) collective-permute-start(f32[1,40,2048]{2,1,0:T(8,128)S(1)} %broadcast_select_fusion.30), channel_id=22, source_target_pairs={{0,1},{1,2},{2,3},{3,4},{4,5},{5,6},{6,7},{7,8},{8,9},{9,10},{10,1... | collective-permute-start | bytes 983048 | tf_op jit(solution)/vmap(transpose(jvp()))/dot_general | solution.py:21
  450.0 12.5 %collective-permute-start.13 = (f32[1,40,2048]{2,1,0:T(8,128)}, f32[1,40,2048]{2,1,0:T(8,128)S(1)}, u32[]{:S(2)}, u32[]{:S(2)}) collective-permute-start(f32[1,40,2048]{2,1,0:T(8,128)} %broadcast_select_fusion.31), channel_id=21, source_target_pairs={{0,15},{1,0},{2,1},{3,2},{4,3},{5,4},{6,5},{7,6},{8,7},{9,8},{10,9... | collective-permute-start | bytes 983048 | tf_op jit(solution)/vmap(transpose(jvp()))/dot_general | solution.py:21
  477.5 13.3 %collective-permute-start.12 = (f32[1,40,2048]{2,1,0:T(8,128)S(1)}, f32[1,40,2048]{2,1,0:T(8,128)}, u32[]{:S(2)}, u32[]{:S(2)}) collective-permute-start(f32[1,40,2048]{2,1,0:T(8,128)S(1)} %broadcast_select_fusion.30), channel_id=22, source_target_pairs={{0,1},{1,2},{2,3},{3,4},{4,5},{5,6},{6,7},{7,8},{8,9},{9,10},{10,1... | collective-permute-start | bytes 983048 | tf_op jit(solution)/vmap(transpose(jvp()))/dot_general | solution.py:21
  478.3 12.5 %collective-permute-start.13 = (f32[1,40,2048]{2,1,0:T(8,128)}, f32[1,40,2048]{2,1,0:T(8,128)S(1)}, u32[]{:S(2)}, u32[]{:S(2)}) collective-permute-start(f32[1,40,2048]{2,1,0:T(8,128)} %broadcast_select_fusion.31), channel_id=21, source_target_pairs={{0,15},{1,0},{2,1},{3,2},{4,3},{5,4},{6,5},{7,6},{8,7},{9,8},{10,9... | collective-permute-start | bytes 983048 | tf_op jit(solution)/vmap(transpose(jvp()))/dot_general | solution.py:21
  505.9 13.3 %collective-permute-start.12 = (f32[1,40,2048]{2,1,0:T(8,128)S(1)}, f32[1,40,2048]{2,1,0:T(8,128)}, u32[]{:S(2)}, u32[]{:S(2)}) collective-permute-start(f32[1,40,2048]{2,1,0:T(8,128)S(1)} %broadcast_select_fusion.30), channel_id=22, source_target_pairs={{0,1},{1,2},{2,3},{3,4},{4,5},{5,6},{6,7},{7,8},{8,9},{9,10},{10,1... | collective-permute-start | bytes 983048 | tf_op jit(solution)/vmap(transpose(jvp()))/dot_general | solution.py:21
  506.7 12.5 %collective-permute-start.13 = (f32[1,40,2048]{2,1,0:T(8,128)}, f32[1,40,2048]{2,1,0:T(8,128)S(1)}, u32[]{:S(2)}, u32[]{:S(2)}) collective-permute-start(f32[1,40,2048]{2,1,0:T(8,128)} %broadcast_select_fusion.31), channel_id=21, source_target_pairs={{0,15},{1,0},{2,1},{3,2},{4,3},{5,4},{6,5},{7,6},{8,7},{9,8},{10,9... | collective-permute-start | bytes 983048 | tf_op jit(solution)/vmap(transpose(jvp()))/dot_general | solution.py:21
  520.8 12.5 %collective-permute-start.15 = (f32[1,40,2048]{2,1,0:T(8,128)S(1)}, f32[1,40,2048]{2,1,0:T(8,128)S(1)}, u32[]{:S(2)}, u32[]{:S(2)}) collective-permute-start(f32[1,40,2048]{2,1,0:T(8,128)S(1)} %get-tuple-element.483), channel_id=23, source_target_pairs={{0,15},{1,0},{2,1},{3,2},{4,3},{5,4},{6,5},{7,6},{8,7},{9,8},{10,9... | collective-permute-start | bytes 983048 | tf_op jit(solution)/vmap(transpose(jvp()))/dot_general | solution.py:21
  534.1 351.7 %collective-permute-start.27 = (f32[1,40,2048]{2,1,0:T(8,128)}, f32[1,40,2048]{2,1,0:T(8,128)}, u32[]{:S(2)}, u32[]{:S(2)}) collective-permute-start(f32[1,40,2048]{2,1,0:T(8,128)} %get-tuple-element.43), channel_id=25, source_target_pairs={{0,1},{1,2},{2,3},{3,4},{4,5},{5,6},{6,7},{7,8},{8,9},{9,10},{10,1... | collective-permute-start | bytes 983048 | tf_op jit(solution)/vmap(transpose(jvp()))/dot_general | solution.py:21
  535.8 14.0 %collective-permute-start.8 = (f32[1,40,2048]{2,1,0:T(8,128)}, f32[1,40,2048]{2,1,0:T(8,128)}, u32[]{:S(2)}, u32[]{:S(2)}) collective-permute-start(f32[1,40,2048]{2,1,0:T(8,128)} %broadcast_select_fusion.28), channel_id=16, source_target_pairs={{0,1},{1,2},{2,3},{3,4},{4,5},{5,6},{6,7},{7,8},{8,9},{9,10},{10,1... | collective-permute-start | bytes 983048 | tf_op jit(solution)/vmap(transpose(jvp()))/dot_general | solution.py:21
  536.5 13.3 %collective-permute-start.9 = (f32[1,40,2048]{2,1,0:T(8,128)}, f32[1,40,2048]{2,1,0:T(8,128)}, u32[]{:S(2)}, u32[]{:S(2)}) collective-permute-start(f32[1,40,2048]{2,1,0:T(8,128)} %broadcast_select_fusion.29), channel_id=15, source_target_pairs={{0,15},{1,0},{2,1},{3,2},{4,3},{5,4},{6,5},{7,6},{8,7},{9,8},{10,9... | collective-permute-start | bytes 983048 | tf_op jit(solution)/vmap(transpose(jvp()))/dot_general | solution.py:21
  551.0 12.2 %collective-permute-start.11 = (f32[1,40,2048]{2,1,0:T(8,128)S(1)}, f32[1,40,2048]{2,1,0:T(8,128)S(1)}, u32[]{:S(2)}, u32[]{:S(2)}) collective-permute-start(f32[1,40,2048]{2,1,0:T(8,128)S(1)} %get-tuple-element.474), channel_id=17, source_target_pairs={{0,15},{1,0},{2,1},{3,2},{4,3},{5,4},{6,5},{7,6},{8,7},{9,8},{10,9... | collective-permute-start | bytes 983048 | tf_op jit(solution)/vmap(transpose(jvp()))/dot_general | solution.py:21
  565.9 13.8 %collective-permute-start.8 = (f32[1,40,2048]{2,1,0:T(8,128)}, f32[1,40,2048]{2,1,0:T(8,128)}, u32[]{:S(2)}, u32[]{:S(2)}) collective-permute-start(f32[1,40,2048]{2,1,0:T(8,128)} %broadcast_select_fusion.28), channel_id=16, source_target_pairs={{0,1},{1,2},{2,3},{3,4},{4,5},{5,6},{6,7},{7,8},{8,9},{9,10},{10,1... | collective-permute-start | bytes 983048 | tf_op jit(solution)/vmap(transpose(jvp()))/dot_general | solution.py:21
  567.6 12.0 %collective-permute-start.9 = (f32[1,40,2048]{2,1,0:T(8,128)}, f32[1,40,2048]{2,1,0:T(8,128)}, u32[]{:S(2)}, u32[]{:S(2)}) collective-permute-start(f32[1,40,2048]{2,1,0:T(8,128)} %broadcast_select_fusion.29), channel_id=15, source_target_pairs={{0,15},{1,0},{2,1},{3,2},{4,3},{5,4},{6,5},{7,6},{8,7},{9,8},{10,9... | collective-permute-start | bytes 983048 | tf_op jit(solution)/vmap(transpose(jvp()))/dot_general | solution.py:21
  580.9 12.5 %collective-permute-start.11 = (f32[1,40,2048]{2,1,0:T(8,128)S(1)}, f32[1,40,2048]{2,1,0:T(8,128)S(1)}, u32[]{:S(2)}, u32[]{:S(2)}) collective-permute-start(f32[1,40,2048]{2,1,0:T(8,128)S(1)} %get-tuple-element.474), channel_id=17, source_target_pairs={{0,15},{1,0},{2,1},{3,2},{4,3},{5,4},{6,5},{7,6},{8,7},{9,8},{10,9... | collective-permute-start | bytes 983048 | tf_op jit(solution)/vmap(transpose(jvp()))/dot_general | solution.py:21
  595.9 13.8 %collective-permute-start.8 = (f32[1,40,2048]{2,1,0:T(8,128)}, f32[1,40,2048]{2,1,0:T(8,128)}, u32[]{:S(2)}, u32[]{:S(2)}) collective-permute-start(f32[1,40,2048]{2,1,0:T(8,128)} %broadcast_select_fusion.28), channel_id=16, source_target_pairs={{0,1},{1,2},{2,3},{3,4},{4,5},{5,6},{6,7},{7,8},{8,9},{9,10},{10,1... | collective-permute-start | bytes 983048 | tf_op jit(solution)/vmap(transpose(jvp()))/dot_general | solution.py:21
  597.7 12.0 %collective-permute-start.9 = (f32[1,40,2048]{2,1,0:T(8,128)}, f32[1,40,2048]{2,1,0:T(8,128)}, u32[]{:S(2)}, u32[]{:S(2)}) collective-permute-start(f32[1,40,2048]{2,1,0:T(8,128)} %broadcast_select_fusion.29), channel_id=15, source_target_pairs={{0,15},{1,0},{2,1},{3,2},{4,3},{5,4},{6,5},{7,6},{8,7},{9,8},{10,9... | collective-permute-start | bytes 983048 | tf_op jit(solution)/vmap(transpose(jvp()))/dot_general | solution.py:21
  610.9 12.5 %collective-permute-start.11 = (f32[1,40,2048]{2,1,0:T(8,128)S(1)}, f32[1,40,2048]{2,1,0:T(8,128)S(1)}, u32[]{:S(2)}, u32[]{:S(2)}) collective-permute-start(f32[1,40,2048]{2,1,0:T(8,128)S(1)} %get-tuple-element.474), channel_id=17, source_target_pairs={{0,15},{1,0},{2,1},{3,2},{4,3},{5,4},{6,5},{7,6},{8,7},{9,8},{10,9... | collective-permute-start | bytes 983048 | tf_op jit(solution)/vmap(transpose(jvp()))/dot_general | solution.py:21
  626.0 13.8 %collective-permute-start.8 = (f32[1,40,2048]{2,1,0:T(8,128)}, f32[1,40,2048]{2,1,0:T(8,128)}, u32[]{:S(2)}, u32[]{:S(2)}) collective-permute-start(f32[1,40,2048]{2,1,0:T(8,128)} %broadcast_select_fusion.28), channel_id=16, source_target_pairs={{0,1},{1,2},{2,3},{3,4},{4,5},{5,6},{6,7},{7,8},{8,9},{9,10},{10,1... | collective-permute-start | bytes 983048 | tf_op jit(solution)/vmap(transpose(jvp()))/dot_general | solution.py:21
  627.7 12.0 %collective-permute-start.9 = (f32[1,40,2048]{2,1,0:T(8,128)}, f32[1,40,2048]{2,1,0:T(8,128)}, u32[]{:S(2)}, u32[]{:S(2)}) collective-permute-start(f32[1,40,2048]{2,1,0:T(8,128)} %broadcast_select_fusion.29), channel_id=15, source_target_pairs={{0,15},{1,0},{2,1},{3,2},{4,3},{5,4},{6,5},{7,6},{8,7},{9,8},{10,9... | collective-permute-start | bytes 983048 | tf_op jit(solution)/vmap(transpose(jvp()))/dot_general | solution.py:21
  654.2 12.9 %collective-permute-start.4 = (f32[1,40,2048]{2,1,0:T(8,128)}, f32[1,40,2048]{2,1,0:T(8,128)}, u32[]{:S(2)}, u32[]{:S(2)}) collective-permute-start(f32[1,40,2048]{2,1,0:T(8,128)} %broadcast_select_fusion.26), channel_id=9, source_target_pairs={{0,1},{1,2},{2,3},{3,4},{4,5},{5,6},{6,7},{7,8},{8,9},{9,10},{10,1... | collective-permute-start | bytes 983048 | tf_op jit(solution)/vmap(transpose(jvp()))/dot_general | solution.py:20
  654.9 12.1 %collective-permute-start.5 = (f32[1,40,2048]{2,1,0:T(8,128)}, f32[1,40,2048]{2,1,0:T(8,128)S(1)}, u32[]{:S(2)}, u32[]{:S(2)}) collective-permute-start(f32[1,40,2048]{2,1,0:T(8,128)} %broadcast_select_fusion.27), channel_id=8, source_target_pairs={{0,15},{1,0},{2,1},{3,2},{4,3},{5,4},{6,5},{7,6},{8,7},{9,8},{10,9... | collective-permute-start | bytes 983048 | tf_op jit(solution)/vmap(transpose(jvp()))/dot_general | solution.py:20
  668.6 12.3 %collective-permute-start.7 = (f32[1,40,2048]{2,1,0:T(8,128)S(1)}, f32[1,40,2048]{2,1,0:T(8,128)S(1)}, u32[]{:S(2)}, u32[]{:S(2)}) collective-permute-start(f32[1,40,2048]{2,1,0:T(8,128)S(1)} %get-tuple-element.465), channel_id=10, source_target_pairs={{0,15},{1,0},{2,1},{3,2},{4,3},{5,4},{6,5},{7,6},{8,7},{9,8},{10,9... | collective-permute-start | bytes 983048 | tf_op jit(solution)/vmap(transpose(jvp()))/dot_general | solution.py:20
  683.5 12.9 %collective-permute-start.4 = (f32[1,40,2048]{2,1,0:T(8,128)}, f32[1,40,2048]{2,1,0:T(8,128)}, u32[]{:S(2)}, u32[]{:S(2)}) collective-permute-start(f32[1,40,2048]{2,1,0:T(8,128)} %broadcast_select_fusion.26), channel_id=9, source_target_pairs={{0,1},{1,2},{2,3},{3,4},{4,5},{5,6},{6,7},{7,8},{8,9},{9,10},{10,1... | collective-permute-start | bytes 983048 | tf_op jit(solution)/vmap(transpose(jvp()))/dot_general | solution.py:20
  684.2 12.1 %collective-permute-start.5 = (f32[1,40,2048]{2,1,0:T(8,128)}, f32[1,40,2048]{2,1,0:T(8,128)S(1)}, u32[]{:S(2)}, u32[]{:S(2)}) collective-permute-start(f32[1,40,2048]{2,1,0:T(8,128)} %broadcast_select_fusion.27), channel_id=8, source_target_pairs={{0,15},{1,0},{2,1},{3,2},{4,3},{5,4},{6,5},{7,6},{8,7},{9,8},{10,9... | collective-permute-start | bytes 983048 | tf_op jit(solution)/vmap(transpose(jvp()))/dot_general | solution.py:20
  697.9 12.3 %collective-permute-start.7 = (f32[1,40,2048]{2,1,0:T(8,128)S(1)}, f32[1,40,2048]{2,1,0:T(8,128)S(1)}, u32[]{:S(2)}, u32[]{:S(2)}) collective-permute-start(f32[1,40,2048]{2,1,0:T(8,128)S(1)} %get-tuple-element.465), channel_id=10, source_target_pairs={{0,15},{1,0},{2,1},{3,2},{4,3},{5,4},{6,5},{7,6},{8,7},{9,8},{10,9... | collective-permute-start | bytes 983048 | tf_op jit(solution)/vmap(transpose(jvp()))/dot_general | solution.py:20
  712.8 12.9 %collective-permute-start.4 = (f32[1,40,2048]{2,1,0:T(8,128)}, f32[1,40,2048]{2,1,0:T(8,128)}, u32[]{:S(2)}, u32[]{:S(2)}) collective-permute-start(f32[1,40,2048]{2,1,0:T(8,128)} %broadcast_select_fusion.26), channel_id=9, source_target_pairs={{0,1},{1,2},{2,3},{3,4},{4,5},{5,6},{6,7},{7,8},{8,9},{9,10},{10,1... | collective-permute-start | bytes 983048 | tf_op jit(solution)/vmap(transpose(jvp()))/dot_general | solution.py:20
  713.5 12.1 %collective-permute-start.5 = (f32[1,40,2048]{2,1,0:T(8,128)}, f32[1,40,2048]{2,1,0:T(8,128)S(1)}, u32[]{:S(2)}, u32[]{:S(2)}) collective-permute-start(f32[1,40,2048]{2,1,0:T(8,128)} %broadcast_select_fusion.27), channel_id=8, source_target_pairs={{0,15},{1,0},{2,1},{3,2},{4,3},{5,4},{6,5},{7,6},{8,7},{9,8},{10,9... | collective-permute-start | bytes 983048 | tf_op jit(solution)/vmap(transpose(jvp()))/dot_general | solution.py:20
  727.2 12.3 %collective-permute-start.7 = (f32[1,40,2048]{2,1,0:T(8,128)S(1)}, f32[1,40,2048]{2,1,0:T(8,128)S(1)}, u32[]{:S(2)}, u32[]{:S(2)}) collective-permute-start(f32[1,40,2048]{2,1,0:T(8,128)S(1)} %get-tuple-element.465), channel_id=10, source_target_pairs={{0,15},{1,0},{2,1},{3,2},{4,3},{5,4},{6,5},{7,6},{8,7},{9,8},{10,9... | collective-permute-start | bytes 983048 | tf_op jit(solution)/vmap(transpose(jvp()))/dot_general | solution.py:20
  742.1 12.9 %collective-permute-start.4 = (f32[1,40,2048]{2,1,0:T(8,128)}, f32[1,40,2048]{2,1,0:T(8,128)}, u32[]{:S(2)}, u32[]{:S(2)}) collective-permute-start(f32[1,40,2048]{2,1,0:T(8,128)} %broadcast_select_fusion.26), channel_id=9, source_target_pairs={{0,1},{1,2},{2,3},{3,4},{4,5},{5,6},{6,7},{7,8},{8,9},{9,10},{10,1... | collective-permute-start | bytes 983048 | tf_op jit(solution)/vmap(transpose(jvp()))/dot_general | solution.py:20
  742.9 12.1 %collective-permute-start.5 = (f32[1,40,2048]{2,1,0:T(8,128)}, f32[1,40,2048]{2,1,0:T(8,128)S(1)}, u32[]{:S(2)}, u32[]{:S(2)}) collective-permute-start(f32[1,40,2048]{2,1,0:T(8,128)} %broadcast_select_fusion.27), channel_id=8, source_target_pairs={{0,15},{1,0},{2,1},{3,2},{4,3},{5,4},{6,5},{7,6},{8,7},{9,8},{10,9... | collective-permute-start | bytes 983048 | tf_op jit(solution)/vmap(transpose(jvp()))/dot_general | solution.py:20
  769.5 12.7 %collective-permute-start = (f32[1,40,2048]{2,1,0:T(8,128)}, f32[1,40,2048]{2,1,0:T(8,128)}, u32[]{:S(2)}, u32[]{:S(2)}) collective-permute-start(f32[1,40,2048]{2,1,0:T(8,128)} %broadcast_select_fusion.24), channel_id=3, source_target_pairs={{0,1},{1,2},{2,3},{3,4},{4,5},{5,6},{6,7},{7,8},{8,9},{9,10},{10,1... | collective-permute-start | bytes 983048 | tf_op jit(solution)/vmap(transpose(jvp()))/dot_general | solution.py:20
  770.2 12.0 %collective-permute-start.1 = (f32[1,40,2048]{2,1,0:T(8,128)}, f32[1,40,2048]{2,1,0:T(8,128)S(1)}, u32[]{:S(2)}, u32[]{:S(2)}) collective-permute-start(f32[1,40,2048]{2,1,0:T(8,128)} %broadcast_select_fusion.25), channel_id=2, source_target_pairs={{0,15},{1,0},{2,1},{3,2},{4,3},{5,4},{6,5},{7,6},{8,7},{9,8},{10,9... | collective-permute-start | bytes 983048 | tf_op jit(solution)/vmap(transpose(jvp()))/dot_general | solution.py:20
  783.3 12.3 %collective-permute-start.3 = (f32[1,40,2048]{2,1,0:T(8,128)S(1)}, f32[1,40,2048]{2,1,0:T(8,128)S(1)}, u32[]{:S(2)}, u32[]{:S(2)}) collective-permute-start(f32[1,40,2048]{2,1,0:T(8,128)S(1)} %get-tuple-element.456), channel_id=4, source_target_pairs={{0,15},{1,0},{2,1},{3,2},{4,3},{5,4},{6,5},{7,6},{8,7},{9,8},{10,9... | collective-permute-start | bytes 983048 | tf_op jit(solution)/vmap(transpose(jvp()))/dot_general | solution.py:20
  798.2 12.7 %collective-permute-start = (f32[1,40,2048]{2,1,0:T(8,128)}, f32[1,40,2048]{2,1,0:T(8,128)}, u32[]{:S(2)}, u32[]{:S(2)}) collective-permute-start(f32[1,40,2048]{2,1,0:T(8,128)} %broadcast_select_fusion.24), channel_id=3, source_target_pairs={{0,1},{1,2},{2,3},{3,4},{4,5},{5,6},{6,7},{7,8},{8,9},{9,10},{10,1... | collective-permute-start | bytes 983048 | tf_op jit(solution)/vmap(transpose(jvp()))/dot_general | solution.py:20
  799.0 12.0 %collective-permute-start.1 = (f32[1,40,2048]{2,1,0:T(8,128)}, f32[1,40,2048]{2,1,0:T(8,128)S(1)}, u32[]{:S(2)}, u32[]{:S(2)}) collective-permute-start(f32[1,40,2048]{2,1,0:T(8,128)} %broadcast_select_fusion.25), channel_id=2, source_target_pairs={{0,15},{1,0},{2,1},{3,2},{4,3},{5,4},{6,5},{7,6},{8,7},{9,8},{10,9... | collective-permute-start | bytes 983048 | tf_op jit(solution)/vmap(transpose(jvp()))/dot_general | solution.py:20
  812.0 12.3 %collective-permute-start.3 = (f32[1,40,2048]{2,1,0:T(8,128)S(1)}, f32[1,40,2048]{2,1,0:T(8,128)S(1)}, u32[]{:S(2)}, u32[]{:S(2)}) collective-permute-start(f32[1,40,2048]{2,1,0:T(8,128)S(1)} %get-tuple-element.456), channel_id=4, source_target_pairs={{0,15},{1,0},{2,1},{3,2},{4,3},{5,4},{6,5},{7,6},{8,7},{9,8},{10,9... | collective-permute-start | bytes 983048 | tf_op jit(solution)/vmap(transpose(jvp()))/dot_general | solution.py:20
  826.9 12.7 %collective-permute-start = (f32[1,40,2048]{2,1,0:T(8,128)}, f32[1,40,2048]{2,1,0:T(8,128)}, u32[]{:S(2)}, u32[]{:S(2)}) collective-permute-start(f32[1,40,2048]{2,1,0:T(8,128)} %broadcast_select_fusion.24), channel_id=3, source_target_pairs={{0,1},{1,2},{2,3},{3,4},{4,5},{5,6},{6,7},{7,8},{8,9},{9,10},{10,1... | collective-permute-start | bytes 983048 | tf_op jit(solution)/vmap(transpose(jvp()))/dot_general | solution.py:20
  827.7 12.0 %collective-permute-start.1 = (f32[1,40,2048]{2,1,0:T(8,128)}, f32[1,40,2048]{2,1,0:T(8,128)S(1)}, u32[]{:S(2)}, u32[]{:S(2)}) collective-permute-start(f32[1,40,2048]{2,1,0:T(8,128)} %broadcast_select_fusion.25), channel_id=2, source_target_pairs={{0,15},{1,0},{2,1},{3,2},{4,3},{5,4},{6,5},{7,6},{8,7},{9,8},{10,9... | collective-permute-start | bytes 983048 | tf_op jit(solution)/vmap(transpose(jvp()))/dot_general | solution.py:20
  840.8 12.3 %collective-permute-start.3 = (f32[1,40,2048]{2,1,0:T(8,128)S(1)}, f32[1,40,2048]{2,1,0:T(8,128)S(1)}, u32[]{:S(2)}, u32[]{:S(2)}) collective-permute-start(f32[1,40,2048]{2,1,0:T(8,128)S(1)} %get-tuple-element.456), channel_id=4, source_target_pairs={{0,15},{1,0},{2,1},{3,2},{4,3},{5,4},{6,5},{7,6},{8,7},{9,8},{10,9... | collective-permute-start | bytes 983048 | tf_op jit(solution)/vmap(transpose(jvp()))/dot_general | solution.py:20
  855.6 12.7 %collective-permute-start = (f32[1,40,2048]{2,1,0:T(8,128)}, f32[1,40,2048]{2,1,0:T(8,128)}, u32[]{:S(2)}, u32[]{:S(2)}) collective-permute-start(f32[1,40,2048]{2,1,0:T(8,128)} %broadcast_select_fusion.24), channel_id=3, source_target_pairs={{0,1},{1,2},{2,3},{3,4},{4,5},{5,6},{6,7},{7,8},{8,9},{9,10},{10,1... | collective-permute-start | bytes 983048 | tf_op jit(solution)/vmap(transpose(jvp()))/dot_general | solution.py:20
  856.4 12.0 %collective-permute-start.1 = (f32[1,40,2048]{2,1,0:T(8,128)}, f32[1,40,2048]{2,1,0:T(8,128)S(1)}, u32[]{:S(2)}, u32[]{:S(2)}) collective-permute-start(f32[1,40,2048]{2,1,0:T(8,128)} %broadcast_select_fusion.25), channel_id=2, source_target_pairs={{0,15},{1,0},{2,1},{3,2},{4,3},{5,4},{6,5},{7,6},{8,7},{9,8},{10,9... | collective-permute-start | bytes 983048 | tf_op jit(solution)/vmap(transpose(jvp()))/dot_general | solution.py:20
  882.8 15.1 %collective-permute-start.24 = (f32[1,40,2048]{2,1,0:T(8,128)}, f32[1,40,2048]{2,1,0:T(8,128)S(1)}, u32[]{:S(2)}, u32[]{:S(2)}) collective-permute-start(f32[1,40,2048]{2,1,0:T(8,128)} %get-tuple-element.37), channel_id=6, source_target_pairs={{0,1},{1,2},{2,3},{3,4},{4,5},{5,6},{6,7},{7,8},{8,9},{9,10},{10,1... | collective-permute-start | bytes 983048 | tf_op jit(solution)/vmap(transpose(jvp()))/dot_general | solution.py:20
  934.5 114.4 %all-gather.12.cloned.1.call-start = ((), (), s32[]{:S(2)}) async-start(), calls=%async_computation.1 | async-start | bytes 5570560 | tf_op jit(solution)/reshape | solution.py:58
  937.5 168.8 %all-gather.10.cloned.1.call-start = ((), (), s32[]{:S(2)}) async-start(), calls=%async_computation | async-start | bytes 5570560 | tf_op jit(solution)/reshape | solution.py:58
  (109 other events, 1459.3 us)
Sparse Core Ops, SparseCore 0:
  934.6 56.8 all-gather.13
  994.3 54.5 all-gather.11
  1051.7 54.5 all-gather.9
where the time goes:
time: 1140 us; the launch traced here: 1120 us
  waiting for transfers between devices  338 us (30%)
  matrix products  270 us (24%)
  starting transfers between devices  222 us (19%)
  other arithmetic  137 us (12%)
  local copies, waits for them, and re-layouts  64.2 us (6%)
  loops' own time  44.9 us (4%)
  blocking collectives  30.6 us (3%)
  between operations  17.7 us (2%)
    reshape x3, waiting for transfers between devices, step(): t.reshape(-1, *t.shape[2:])  166 us
    dot_general x19, matrix products, layer(): gate = jnp.dot(a, w['w_gate'], preferred_element_type=jnp.float32)  106 us
    dot_general x19, matrix products, layer(): up = jnp.dot(a, w['w_up'], preferred_element_type=jnp.float32)  94.3 us
    dot_general x34, starting transfers between devices, matmul(): jnp.dot(a, w, preferred_element_type=jnp.float32).astype(jnp.bfloat16)  75.6 us
    dot_general x34, starting transfers between devices, layer(): gate = jnp.dot(a, w['w_gate'], preferred_element_type=jnp.float32)  73 us
    dot_general x34, starting transfers between devices, layer(): up = jnp.dot(a, w['w_up'], preferred_element_type=jnp.float32)  73 us
    dot_general x19, matrix products, matmul(): jnp.dot(a, w, preferred_element_type=jnp.float32).astype(jnp.bfloat16)  69.5 us
    dot_general x34, waiting for transfers between devices, matmul(): jnp.dot(a, w, preferred_element_type=jnp.float32).astype(jnp.bfloat16)  65.1 us
  transfers between devices with their start and end apart: 105, of which 64 were waited for; matrix products, arithmetic and copies ran while one was open for 27% of the time, Pallas kernels for 0%

commit v1 on v0

v1 whole, which is shorter than its diff:
```python
import jax
import jax.numpy as jnp
from jax import lax
from jax.sharding import PartitionSpec as P

F32, BF16 = jnp.float32, jnp.bfloat16


def dot(a, b, dims):
    return lax.dot_general(a, b, (dims, ((), ())), preferred_element_type=F32)


def normed(h):
    wide = h.astype(F32)
    scale = lax.rsqrt(jnp.mean(wide**2, -1, keepdims=True) + 1e-6)
    return (wide * scale).astype(BF16), scale


def adamw(w, m, v, g):
    m = 0.9 * m + 0.1 * g
    v = 0.95 * v + 0.05 * g * g
    step = m * lax.rsqrt(v + 1e-8) + 0.1 * w
    return (w - 0.02 * step).astype(BF16), m, v


def gated_grads(gate, up, d):
    s = jax.nn.sigmoid(gate)
    silu = gate * s
    return (silu * up).astype(BF16), (d * up * (s + silu * (1 - s))).astype(BF16), (d * silu).astype(BF16)


def solution(mesh):
    n = mesh.shape["dp"]

    def body(x, dy, wg, wu, wd, mg, mu, md, vg, vu, vd):
        x, dy = x[0], dy[0]
        me = lax.axis_index("dp")

        def scatter(g):
            return lax.psum_scatter(g.astype(BF16), "dp", scatter_dimension=0, tiled=True)

        a0, _ = normed(x)
        gate0, up0 = dot(a0, wg[0], ((1,), (0,))), dot(a0, wu[0], ((1,), (0,)))
        inner0 = (jax.nn.silu(gate0) * up0).astype(BF16)
        h1 = x + dot(inner0, wd[0], ((1,), (0,))).astype(BF16)
        a1, s1 = normed(h1)
        gate1, up1 = dot(a1, wg[1], ((1,), (0,))), dot(a1, wu[1], ((1,), (0,)))
        d1 = dot(dy, wd[1], ((1,), (1,))).astype(BF16).astype(F32)
        inner1, dg1, du1 = gated_grads(gate1, up1, d1)
        g_d1 = scatter(dot(inner1, dy, ((0,), (0,))))
        g_g1 = scatter(dot(a1, dg1, ((0,), (0,))))
        g_u1 = scatter(dot(a1, du1, ((0,), (0,))))
        da = (dot(dg1, wg[1], ((1,), (1,))) + dot(du1, wu[1], ((1,), (1,)))).astype(BF16).astype(F32)
        wide = h1.astype(F32)
        dwide = s1 * da - wide * (s1**3 * jnp.mean(da * wide, -1, keepdims=True))
        dh = dy + dwide.astype(BF16)
        g_d0 = scatter(dot(inner0, dh, ((0,), (0,))))
        d0 = dot(dh, wd[0], ((1,), (1,))).astype(BF16).astype(F32)
        _, dg0, du0 = gated_grads(gate0, up0, d0)
        g_g0 = scatter(dot(a0, dg0, ((0,), (0,))))
        g_u0 = scatter(dot(a0, du0, ((0,), (0,))))

        grads = [jnp.stack(p).astype(F32) for p in ((g_g0, g_g1), (g_u0, g_u1), (g_d0, g_d1))]
        count = n * sum(g.size for g in grads)
        squares = lax.psum(sum(jnp.sum(g * g) for g in grads), "dp")
        factor = jnp.minimum(1.0, 0.5 * lax.rsqrt(squares / count + 1e-30))
        new = []
        for w, m, v, g in zip((wg, wu, wd), (mg, mu, md), (vg, vu, vd), grads, strict=True):
            rows = g.shape[1]
            own = lax.dynamic_slice_in_dim(w, me * rows, rows, 1).astype(F32)
            w, m, v = adamw(own, m, v, g * factor)
            new.append((lax.all_gather(w, "dp", axis=1, tiled=True), m, v))
        return tuple(one[which] for which in range(3) for one in new)

    whole, rows = P(), P(None, "dp", None)
    seq, mine = P(("rep", "dp")), P("rep", "dp", None)
    return jax.shard_map(
        body,
        mesh=mesh,
        in_specs=(seq, seq) + (whole,) * 3 + (rows,) * 6,
        out_specs=(P("rep"),) * 3 + (mine,) * 6,
        check_vma=False,
    )
```

time: 1140 us -> 748 us (0.66)
  starting transfers between devices: 222 us -> 0.37 us
  other arithmetic: 137 us -> 17.6 us
  waiting for transfers between devices: 338 us -> 450 us
  matrix products: 270 us -> 200 us
  loops' own time: 44.9 us -> 0 us
  local copies, waits for them, and re-layouts: 64.2 us -> 23.2 us
    reduce_scatter x0 -> x6, waiting for transfers between devices: none -> 287 us  [scatter(): lax.psum_scatter(g.astype(BF16), 'dp', scatter_dimension=0, tiled=True)]
    dot_general x102 -> x0, starting transfers between devices: 222 us -> none  [the longest x34 75.6 us: matmul(): jnp.dot(a, w, preferred_element_type=jnp.float32).astype(jnp.bfloat16)]
    dot_general x102 -> x0, waiting for transfers between devices: 172 us -> none  [the longest x34 65.1 us: matmul(): jnp.dot(a, w, preferred_element_type=jnp.float32).astype(jnp.bfloat16)]
    reshape x3 -> x0, waiting for transfers between devices: 166 us -> none  [step(): t.reshape(-1, *t.shape[2:])]
    all_gather x0 -> x3, waiting for transfers between devices: none -> 163 us  [body(): new.append((lax.all_gather(w, 'dp', axis=1, tiled=True), m, v))]
    dot_general x112 -> x0, other arithmetic: 96.7 us -> none
    dot_general x57 -> x15, matrix products: 270 us -> 200 us  [dot(): return lax.dot_general(a, b, (dims, ((), ())), preferred_element_type=F32)]
    another operation x6 -> x0, loops' own time: 44.9 us -> none  [the longest x2 16 us: matmul(): jnp.dot(a, w, preferred_element_type=jnp.float32).astype(jnp.bfloat16)]
  transfers between devices with their start and end apart: 105 -> 9, of which waited for: 64 -> 8; matrix products, arithmetic and copies ran while one was open for 27% -> 16% of each run, Pallas kernels for 0% -> 0%
where the time goes in v1:
time: 748 us; the launch traced here: 739 us
  waiting for transfers between devices  450 us (60%)
  matrix products  200 us (27%)
  blocking collectives  30 us (4%)
  local copies, waits for them, and re-layouts  23.2 us (3%)
  other arithmetic  17.6 us (2%)
  between operations  17.2 us (2%)
    reduce_scatter x6, waiting for transfers between devices, scatter(): lax.psum_scatter(g.astype(BF16), 'dp', scatter_dimension=0, tiled=True)  287 us
    dot_general x15, matrix products, dot(): return lax.dot_general(a, b, (dims, ((), ())), preferred_element_type=F32)  200 us
    all_gather x3, waiting for transfers between devices, body(): new.append((lax.all_gather(w, 'dp', axis=1, tiled=True), m, v))  163 us
    psum x1, blocking collectives, body(): squares = lax.psum(sum((jnp.sum(g * g) for g in grads)), 'dp')  30 us
    unnamed x53, local copies, waits for them, and re-layouts  23.2 us
  transfers between devices with their start and end apart: 9, of which 8 were waited for; matrix products, arithmetic and copies ran while one was open for 16% of the time, Pallas kernels for 0%

profile of v1, /device:TPU:0, one launch (start us, length us, event | category | flops | bytes accessed | tf_op | source)
XLA Modules:
  0.0 738.8 jit_solution(17333127865492277231)
XLA Ops:
  7.2 0.0 reduce-scatter.17.cloned.1.call-start
  7.2 3.0 copy.20
  10.2 0.0 slice-start.2
  10.2 0.6 fusion.13
  10.8 0.0 copy-start.7
  10.8 0.0 slice-start.3
  10.8 12.4 %convolution_convert_fusion.1 = bf16[2048,2048]{1,0:T(8,128)(2,1)} fusion(bf16[1,2048,640]{2,1,0:T(8,128)(2,1)} %param.12, bf16[2,2048,640]{2,1,0:T(8,128)(2,1)} %param.15), kind=kOutput, calls=%fused_computation.24 | convolution fusion | flops 5372903424 | bytes 13631488 | tf_op jit(solution)/shard_map/dot_general | solution.py:10
  23.3 9.9 %fusion.43 = f32[2048,2048]{1,0:T(8,128)} fusion(bf16[2,640,2048]{2,1,0:T(8,128)(2,1)S(1)} %bitcast.81, bf16[1,2048,640]{2,1,0:T(8,128)(2,1)S(1)} %copy-done.7, f32[2048]{0:T(1024)S(1)} %add_rsqrt_fusion.1), kind=kOutput, calls=%fused_computation.60 | convolution fusion | flops 5372641280 | bytes 22028288 | tf_op jit(solution)/shard_map/dot_general | solution.py:10
  33.2 16.8 %multiply_convert_fusion.1 = (bf16[2048,2048]{1,0:T(8,128)(2,1)}, f32[2048,2048]{1,0:T(8,128)}) fusion(f32[2048,2048]{1,0:T(8,128)} %fusion.43, bf16[2,640,2048]{2,1,0:T(8,128)(2,1)} %param.14, bf16[1,2048,640]{2,1,0:T(8,128)(2,1)} %param.11, f32[2048]{0:T(1024)S(1)} %add_rsqrt_fusion.1), kind=kOutput, calls=%fused_computation.12 | convolution fusion | flops 5397807104 | bytes 47194112 | tf_op jit(solution)/shard_map/dot_general | solution.py:10
  50.0 9.2 %fusion.17 = (f32[2048]{0:T(1024)S(1)}, bf16[2048,640]{0,1:T(8,128)(2,1)S(1)}) fusion(bf16[2048,2048]{1,0:T(8,128)(2,1)} %get-tuple-element.18, bf16[2,2048,640]{2,1,0:T(8,128)(2,1)} %param.15, bf16[1,2048,640]{1,2,0:T(8,128)(2,1)S(1)} %copy.20), kind=kOutput, calls=%fused_computation.32 | convolution fusion | flops 5375260672 | bytes 16261120 | tf_op jit(solution)/shard_map/dot_general | solution.py:10
  59.2 1.5 copy-done.3
  60.6 12.3 %fusion.33 = f32[2048,2048]{1,0:T(8,128)} fusion(bf16[2,640,2048]{2,1,0:T(8,128)(2,1)} %param.13, bf16[2048,640]{0,1:T(8,128)(2,1)S(1)} %get-tuple-element.21, f32[2048]{0:T(1024)S(1)} %add_rsqrt_fusion), kind=kOutput, calls=%fused_computation.50 | convolution fusion | flops 5372641280 | bytes 22028288 | tf_op jit(solution)/shard_map/dot_general | solution.py:10
  72.9 23.3 %fusion.1 = (bf16[2048,2048]{1,0:T(8,128)(2,1)}, f32[2048,2048]{1,0:T(8,128)}) fusion(bf16[2048,2048]{1,0:T(8,128)(2,1)} %convolution_convert_fusion.1, f32[2048,2048]{1,0:T(8,128)} %fusion.33, bf16[2,640,2048]{2,1,0:T(8,128)(2,1)} %param.14, bf16[2048,640]{0,1:T(8,128)(2,1)} %copy-done.3, f32[2048]{0:T(1024)S(1)} %add_rsqrt_fusion), kind=kOutput, calls=%fused_computation.5 | convolution fusion | flops 5418778624 | bytes 55582720 | tf_op jit(solution)/shard_map/dot_general | solution.py:10
  96.2 15.5 %fusion.26 = bf16[2048,640]{1,0:T(8,128)(2,1)} fusion(f32[2048,2048]{1,0:T(8,128)} %get-tuple-element.23, bf16[1,2048,640]{2,1,0:T(8,128)(2,1)S(1)} %copy-done.8, f32[2048,2048]{1,0:T(8,128)} %fusion.33), kind=kOutput, calls=%fused_computation.39 | convolution fusion | flops 5395185664 | bytes 38797312 | tf_op jit(solution)/shard_map/dot_general | solution.py:10
  111.8 0.0 reduce-scatter.17.cloned.1.call-update
  111.8 0.0 reduce-scatter.15.cloned.1.call-start
  111.8 11.4 %fusion.31 = f32[2048,640]{0,1:T(8,128)} fusion(bf16[2048,2048]{1,0:T(8,128)(2,1)} %get-tuple-element.22, bf16[2,640,2048]{2,1,0:T(8,128)(2,1)} %param.13), kind=kOutput, calls=%fused_computation.48 | convolution fusion | flops 5368709120 | bytes 16252928 | tf_op jit(solution)/shard_map/dot_general | solution.py:10
  123.3 16.0 %fusion.19 = (f32[2048]{0:T(1024)S(1)}, bf16[2048,640]{0,1:T(8,128)(2,1)}) fusion(bf16[2048,640]{0,1:T(8,128)(2,1)S(1)} %copy-done.4, f32[2048,640]{0,1:T(8,128)} %fusion.31, bf16[2,640,2048]{2,1,0:T(8,128)(2,1)} %param.14, bf16[2048,2048]{1,0:T(8,128)(2,1)} %convolution_convert_fusion.1, f32[2048,2048]{1,0:T(8,128)} %fusion.33), kind=kOutput, calls=%fused_computation.34 | convolution fusion | flops 5405931520 | bytes 38281216 | tf_op jit(solution)/shard_map/dot_general | solution.py:10
  139.3 3.0 copy.21
  142.3 4.3 fusion.28
  146.6 0.0 copy-start.6
  146.6 1.5 copy-done.6
  148.1 10.5 %convolution_convert_fusion.2 = bf16[2048,640]{1,0:T(8,128)(2,1)} fusion(bf16[2048,2048]{1,0:T(8,128)(2,1)} %get-tuple-element.18, bf16[2048,640]{0,1:T(8,128)(2,1)S(1)} %fusion.28), kind=kOutput, calls=%fused_computation.40 | convolution fusion | flops 5370019840 | bytes 13631488 | tf_op jit(solution)/shard_map/dot_general | solution.py:10
  158.5 0.0 reduce-scatter.15.cloned.1.call-update
  158.6 0.0 reduce-scatter.13.cloned.1.call-start
  158.6 12.7 %convolution_convert_fusion.3 = bf16[640,2048]{1,0:T(8,128)(2,1)} fusion(bf16[2048,640]{0,1:T(8,128)(2,1)S(1)} %copy-done.5, f32[2048]{0:T(1024)S(1)} %add_rsqrt_fusion, bf16[2048,2048]{1,0:T(8,128)(2,1)} %convolution_convert_fusion.1, f32[2048,2048]{1,0:T(8,128)} %fusion.33), kind=kOutput, calls=%fused_computation.41 | convolution fusion | flops 5403312128 | bytes 30416896 | tf_op jit(solution)/shard_map/dot_general | solution.py:10
  171.3 0.0 reduce-scatter.13.cloned.1.call-update
  171.4 0.0 reduce-scatter.11.cloned.1.call-start
  171.4 9.3 %convolution_convert_fusion = bf16[2048,2048]{1,0:T(8,128)(2,1)S(1)} fusion(bf16[2048,640]{0,1:T(8,128)(2,1)} %copy-done.6, bf16[2,2048,640]{2,1,0:T(8,128)(2,1)} %param.15), kind=kOutput, calls=%fused_computation.23 | convolution fusion | flops 5372903424 | bytes 13631488 | tf_op jit(solution)/shard_map/dot_general | solution.py:10
  180.7 3.2 copy-done.19
  184.0 11.0 %fusion.23 = bf16[640,2048]{1,0:T(8,128)(2,1)} fusion(bf16[2048,2048]{1,0:T(8,128)(2,1)S(1)} %convolution_convert_fusion, bf16[1,2048,640]{1,2,0:T(8,128)(2,1)S(1)} %copy-done.1, f32[2048]{0:T(1024)S(1)} %copy-done.18, f32[2048,2048]{1,0:T(8,128)} %fusion.43), kind=kOutput, calls=%fused_computation.38 | convolution fusion | flops 5403312128 | bytes 30416896 | tf_op jit(solution)/shard_map/dot_general | solution.py:10
  195.0 0.0 reduce-scatter.11.cloned.1.call-update
  195.0 0.0 reduce-scatter.9.cloned.1.call-start
  195.0 10.9 %convolution_convert_fusion.4 = bf16[640,2048]{1,0:T(8,128)(2,1)} fusion(bf16[2048,2048]{1,0:T(8,128)(2,1)} %get-tuple-element.22, bf16[2048,640]{0,1:T(8,128)(2,1)} %copy-done.3, f32[2048]{0:T(1024)S(1)} %add_rsqrt_fusion), kind=kOutput, calls=%fused_computation.42 | convolution fusion | flops 5373952000 | bytes 13639680 | tf_op jit(solution)/shard_map/dot_general | solution.py:10
  205.9 0.0 reduce-scatter.9.cloned.1.call-update
  205.9 0.0 reduce-scatter.7.cloned.1.call-start
  206.0 0.0 copy-start.9
  206.0 19.2 %fusion.20 = bf16[640,2048]{1,0:T(8,128)(2,1)} fusion(f32[2048,2048]{1,0:T(8,128)} %get-tuple-element.19, bf16[2048,2048]{1,0:T(8,128)(2,1)} %copy-done.19, f32[2048,2048]{1,0:T(8,128)} %fusion.43, bf16[1,2048,640]{1,2,0:T(8,128)(2,1)S(1)} %copy-done.1, f32[2048]{0:T(1024)S(1)} %copy-done.18), kind=kOutput, calls=%fused_computation.37 | convolution fusion | flops 5420089344 | bytes 47194112 | tf_op jit(solution)/shard_map/dot_general | solution.py:10
  225.2 0.0 reduce-scatter.7.cloned.1.call-update
  225.2 0.0 all-gather.8.cloned.1.call-start
  225.3 0.0 reduce-scatter.17.cloned.1.call-done
  225.3 20.9 %reduce-scatter.15.cloned.1.call-done = bf16[128,640]{1,0:T(8,128)(2,1)} async-done(((bf16[2048,640]{1,0:T(8,128)(2,1)}), bf16[128,640]{1,0:T(8,128)(2,1)}) %reduce-scatter.15.cloned.1.call-update) | async-done | bytes 163856 | tf_op jit(solution)/shard_map/reduce_scatter | solution.py:40
  246.3 1.8 fusion.75
  248.0 65.9 %reduce-scatter.13.cloned.1.call-done = bf16[40,2048]{1,0:T(8,128)(2,1)} async-done(((bf16[640,2048]{1,0:T(8,128)(2,1)}), bf16[40,2048]{1,0:T(8,128)(2,1)}) %reduce-scatter.13.cloned.1.call-update) | async-done | bytes 163856 | tf_op jit(solution)/shard_map/reduce_scatter | solution.py:40
  313.9 66.8 %reduce-scatter.11.cloned.1.call-done = bf16[40,2048]{1,0:T(8,128)(2,1)} async-done(((bf16[640,2048]{1,0:T(8,128)(2,1)}), bf16[40,2048]{1,0:T(8,128)(2,1)}) %reduce-scatter.11.cloned.1.call-update) | async-done | bytes 163856 | tf_op jit(solution)/shard_map/reduce_scatter | solution.py:40
  380.7 1.8 fusion.74
  382.5 65.6 %reduce-scatter.9.cloned.1.call-done = bf16[40,2048]{1,0:T(8,128)(2,1)} async-done(((bf16[640,2048]{1,0:T(8,128)(2,1)}), bf16[40,2048]{1,0:T(8,128)(2,1)}) %reduce-scatter.9.cloned.1.call-update) | async-done | bytes 163856 | tf_op jit(solution)/shard_map/reduce_scatter | solution.py:40
  448.0 67.3 %reduce-scatter.7.cloned.1.call-done = bf16[40,2048]{1,0:T(8,128)(2,1)} async-done(((bf16[640,2048]{1,0:T(8,128)(2,1)}), bf16[40,2048]{1,0:T(8,128)(2,1)}) %reduce-scatter.7.cloned.1.call-update) | async-done | bytes 163856 | tf_op jit(solution)/shard_map/reduce_scatter | solution.py:40
  515.4 1.8 fusion.73
  519.1 30.0 %psum.7 = f32[]{:T(128)} all-reduce(f32[]{:T(128)S(6)} %add.122), channel_id=1, replica_groups=mesh['rep'=2,'dp'=16] {'dp'}, use_global_device_ids=true, to_apply=%region_12.13 | all-reduce | flops 1 | bytes 8 | tf_op jit(solution)/shard_map/psum | solution.py:65
  549.8 2.7 fusion.81
  552.5 0.0 all-gather.8.cloned.1.call-update
  552.5 0.0 all-gather.4.cloned.1.call-start
  552.6 2.4 fusion.72
  555.0 0.0 all-gather.4.cloned.1.call-update
  555.0 0.0 all-gather.6.cloned.1.call-start
  555.1 2.4 fusion.78
  557.5 0.0 all-gather.6.cloned.1.call-update
  557.5 48.7 %all-gather.8.cloned.1.call-done = bf16[2,2048,640]{2,1,0:T(8,128)(2,1)} async-done(((bf16[2,128,640]{2,1,0:T(8,128)(2,1)}), bf16[2,2048,640]{2,1,0:T(8,128)(2,1)}) %all-gather.8.cloned.1.call-update) | async-done | bytes 5242896 | tf_op jit(solution)/shard_map/all_gather | solution.py:72
  606.2 57.4 %all-gather.4.cloned.1.call-done = bf16[2,640,2048]{2,1,0:T(8,128)(2,1)} async-done(((bf16[2,40,2048]{2,1,0:T(8,128)(2,1)}), bf16[2,640,2048]{2,1,0:T(8,128)(2,1)}) %all-gather.4.cloned.1.call-update) | async-done | bytes 5242896 | tf_op jit(solution)/shard_map/all_gather | solution.py:72
  663.6 57.4 %all-gather.6.cloned.1.call-done = bf16[2,640,2048]{2,1,0:T(8,128)(2,1)} async-done(((bf16[2,40,2048]{2,1,0:T(8,128)(2,1)}), bf16[2,640,2048]{2,1,0:T(8,128)(2,1)}) %all-gather.6.cloned.1.call-update) | async-done | bytes 5242896 | tf_op jit(solution)/shard_map/all_gather | solution.py:72
  721.0 6.2 copy.25
  727.1 2.4 copy.26
  729.5 2.4 copy.27
  (45 shorter events, 0.1 us)
Async XLA Ops:
  7.2 218.1 %reduce-scatter.17.cloned.1.call-start = ((), (), s32[]{:S(2)}) async-start(), calls=%async_computation.11 | async-start | bytes 2785280 | tf_op jit(solution)/shard_map/reduce_scatter | solution.py:40
  10.2 39.7 %copy-start = (bf16[1,2048,640]{1,2,0:T(8,128)(2,1)}, bf16[1,2048,640]{1,2,0:T(8,128)(2,1)S(1)}, u32[]{:S(2)}) copy-start(bf16[1,2048,640]{1,2,0:T(8,128)(2,1)S(1)} %copy.20) | copy-start | bytes 7864324
  10.2 13.0 %slice-start.2 = ((s8[5242880]{0:T(1024)(128)(4,1)}), s8[4194304]{0:T(1024)(128)(4,1)S(1)}, s32[]{:S(2)}) async-start(s8[5242880]{0:T(1024)(128)(4,1)} %bitcast.80), calls=%async_computation.17 | async-start | bytes 8388608
  10.8 22.4 %copy-start.17 = (f32[2048]{0:T(1024)}, f32[2048]{0:T(1024)S(1)}, u32[]{:S(2)}) copy-start(f32[2048]{0:T(1024)S(1)} %add_rsqrt_fusion.1) | copy-start | bytes 24580
  10.8 12.4 %copy-start.7 = (bf16[1,2048,640]{2,1,0:T(8,128)(2,1)S(1)}, bf16[1,2048,640]{2,1,0:T(8,128)(2,1)}, u32[]{:S(2)}) copy-start(bf16[1,2048,640]{2,1,0:T(8,128)(2,1)} %param.11) | copy-start | bytes 7864324
  10.8 12.4 %slice-start.3 = ((s8[5242880]{0:T(1024)(128)(4,1)}), s8[1048576]{0:T(1024)(128)(4,1)S(1)}, s32[]{:S(2)}) async-start(s8[5242880]{0:T(1024)(128)(4,1)} %bitcast.80), calls=%async_computation.18 | async-start | bytes 2097152
  59.1 1.5 copy-start.3
  59.1 1.5 copy-start.15
  72.9 23.3 %copy-start.8 = (bf16[1,2048,640]{2,1,0:T(8,128)(2,1)S(1)}, bf16[1,2048,640]{2,1,0:T(8,128)(2,1)}, u32[]{:S(2)}) copy-start(bf16[1,2048,640]{2,1,0:T(8,128)(2,1)} %param.12) | copy-start | bytes 7864324
  111.8 134.5 %reduce-scatter.15.cloned.1.call-start = ((), (), s32[]{:S(2)}) async-start(), calls=%async_computation.10 | async-start | bytes 2785280 | tf_op jit(solution)/shard_map/reduce_scatter | solution.py:40
  111.8 11.4 %copy-start.4 = (bf16[2048,640]{0,1:T(8,128)(2,1)S(1)}, bf16[2048,640]{0,1:T(8,128)(2,1)}, u32[]{:S(2)}) copy-start(bf16[2048,640]{0,1:T(8,128)(2,1)} %copy-done.3) | copy-start | bytes 7864324
  139.3 3.0 copy-start.16
  146.6 1.5 copy-start.6
  148.1 10.5 %copy-start.5 = (bf16[2048,640]{0,1:T(8,128)(2,1)S(1)}, bf16[2048,640]{0,1:T(8,128)(2,1)}, u32[]{:S(2)}) copy-start(bf16[2048,640]{0,1:T(8,128)(2,1)} %copy-done.3) | copy-start | bytes 7864324
  158.6 155.4 %reduce-scatter.13.cloned.1.call-start = ((), (), s32[]{:S(2)}) async-start(), calls=%async_computation.9 | async-start | bytes 2785280 | tf_op jit(solution)/shard_map/reduce_scatter | solution.py:40
  171.3 12.7 %copy-start.1 = (bf16[1,2048,640]{1,2,0:T(8,128)(2,1)S(1)}, bf16[1,2048,640]{1,2,0:T(8,128)(2,1)}, u32[]{:S(2)}) copy-start(bf16[1,2048,640]{1,2,0:T(8,128)(2,1)} %copy-done) | copy-start | bytes 7864324
  171.3 12.6 %copy-start.18 = (f32[2048]{0:T(1024)S(1)}, f32[2048]{0:T(1024)}, u32[]{:S(2)}) copy-start(f32[2048]{0:T(1024)} %copy-done.17) | copy-start | bytes 24580
  171.4 209.3 %reduce-scatter.11.cloned.1.call-start = ((), (), s32[]{:S(2)}) async-start(), calls=%async_computation.8 | async-start | bytes 2785280 | tf_op jit(solution)/shard_map/reduce_scatter | solution.py:40
  180.7 3.2 copy-start.19
  195.0 253.1 %reduce-scatter.9.cloned.1.call-start = ((), (), s32[]{:S(2)}) async-start(), calls=%async_computation.7 | async-start | bytes 2785280 | tf_op jit(solution)/shard_map/reduce_scatter | solution.py:40
  205.9 309.4 %reduce-scatter.7.cloned.1.call-start = ((), (), s32[]{:S(2)}) async-start(), calls=%async_computation.6 | async-start | bytes 2785280 | tf_op jit(solution)/shard_map/reduce_scatter | solution.py:40
  206.0 343.8 %copy-start.9 = (f32[2,128,640]{2,1,0:T(8,128)S(1)}, f32[2,128,640]{2,1,0:T(8,128)}, u32[]{:S(2)}) copy-start(f32[2,128,640]{2,1,0:T(8,128)} %param.21) | copy-start | bytes 1966084
  225.2 327.3 %copy-start.10 = (f32[2,40,2048]{2,1,0:T(8,128)S(1)}, f32[2,40,2048]{2,1,0:T(8,128)}, u32[]{:S(2)}) copy-start(f32[2,40,2048]{2,1,0:T(8,128)} %param.19) | copy-start | bytes 1966084
  225.2 327.4 %copy-start.11 = (f32[2,40,2048]{2,1,0:T(8,128)S(1)}, f32[2,40,2048]{2,1,0:T(8,128)}, u32[]{:S(2)}) copy-start(f32[2,40,2048]{2,1,0:T(8,128)} %param.16) | copy-start | bytes 1966084
  225.2 329.9 %copy-start.12 = (f32[2,40,2048]{2,1,0:T(8,128)S(1)}, f32[2,40,2048]{2,1,0:T(8,128)}, u32[]{:S(2)}) copy-start(f32[2,40,2048]{2,1,0:T(8,128)} %param.20) | copy-start | bytes 1966084
  225.2 329.9 %copy-start.13 = (f32[2,40,2048]{2,1,0:T(8,128)S(1)}, f32[2,40,2048]{2,1,0:T(8,128)}, u32[]{:S(2)}) copy-start(f32[2,40,2048]{2,1,0:T(8,128)} %param.17) | copy-start | bytes 1966084
  225.2 380.9 %all-gather.8.cloned.1.call-start = ((), (), s32[]{:S(2)}) async-start(), calls=%async_computation.14 | async-start | bytes 5570560 | tf_op jit(solution)/shard_map/all_gather | solution.py:72
  313.9 241.2 %copy-start.14 = (bf16[40,2048]{1,0:T(8,128)(2,1)S(1)}, bf16[40,2048]{1,0:T(8,128)(2,1)}, u32[]{:S(2)}) copy-start(bf16[40,2048]{1,0:T(8,128)(2,1)} %reduce-scatter.13.cloned.1.call-done) | copy-start | bytes 491524
  552.5 111.1 %all-gather.4.cloned.1.call-start = ((), (), s32[]{:S(2)}) async-start(), calls=%async_computation.12 | async-start | bytes 5570560 | tf_op jit(solution)/shard_map/all_gather | solution.py:72
  555.0 165.9 %all-gather.6.cloned.1.call-start = ((), (), s32[]{:S(2)}) async-start(), calls=%async_computation.13 | async-start | bytes 5570560 | tf_op jit(solution)/shard_map/all_gather | solution.py:72
  721.0 6.2 copy-start.2
  721.0 8.5 %slice-start = ((s8[5242880]{0:T(1024)(128)(4,1)}), s8[4194304]{0:T(1024)(128)(4,1)S(1)}, s32[]{:S(2)}) async-start(s8[5242880]{0:T(1024)(128)(4,1)} %bitcast.66), calls=%async_computation.15 | async-start | bytes 8388608
  727.1 2.4 slice-start.1
Sparse Core Ops, SparseCore 0:
  111.9 67.1 reduce-scatter.16
  182.9 63.2 reduce-scatter.14
  250.6 63.2 reduce-scatter.12
  317.6 63.1 reduce-scatter.10
  384.9 63.1 reduce-scatter.8
  452.2 63.1 reduce-scatter.6
  552.6 53.5 all-gather.7
  609.0 54.5 all-gather.3
  666.4 54.5 all-gather.5

commit v2 on v1

v2 whole, which is shorter than its diff:
```python
import jax
import jax.numpy as jnp
from jax import lax
from jax.experimental import pallas as pl
from jax.experimental.pallas import tpu as pltpu
from jax.sharding import PartitionSpec as P

F32, BF16 = jnp.float32, jnp.bfloat16
MESH = pl.DeviceIdType.MESH
ANY = pl.BlockSpec(memory_space=pl.ANY)
CHIPS = 8
HOPS = CHIPS - 1


def dot(a, b, dims):
    return lax.dot_general(a, b, (dims, ((), ())), preferred_element_type=F32)


def normed(h):
    wide = h.astype(F32)
    scale = lax.rsqrt(jnp.mean(wide**2, -1, keepdims=True) + 1e-6)
    return (wide * scale).astype(BF16), scale


def adamw(w, m, v, g):
    m = 0.9 * m + 0.1 * g
    v = 0.95 * v + 0.05 * g * g
    step = m * lax.rsqrt(v + 1e-8) + 0.1 * w
    return (w - 0.02 * step).astype(BF16), m, v


def gated_grads(gate, up, d):
    s = jax.nn.sigmoid(gate)
    silu = gate * s
    return (silu * up).astype(BF16), (d * up * (s + silu * (1 - s))).astype(BF16), (d * silu).astype(BF16)


class Place:
    def __init__(self):
        self.me = lax.axis_index("dp")
        self.chip, self.core = lax.div(self.me, 2), lax.rem(self.me, 2)
        self.at = self.flip(self.chip)
        self.partner = self.chip * 2 + 1 - self.core

    @staticmethod
    def flip(c):
        half = CHIPS // 2
        return c + lax.div(c, half) * (3 * half - 1 - 2 * c)

    def chip_at(self, offset):
        return self.flip(lax.rem(self.at + offset + 2 * CHIPS, CHIPS))

    def device_at(self, offset):
        return self.chip_at(offset) * 2 + self.core


def remote(src, dst, send, recv, device):
    return pltpu.make_async_remote_copy(src, dst, send, recv, device_id={"dp": device}, device_id_type=MESH)


def greet(n):
    me = lax.axis_index("dp")
    barrier = pltpu.get_barrier_semaphore()

    @pl.loop(1, n)
    def _(j):
        pl.semaphore_signal(barrier, inc=1, device_id={"dp": lax.rem(me + j, n)}, device_id_type=MESH)

    pl.semaphore_wait(barrier, n - 1)


def wide(ref):
    return ref[...].astype(F32)


def comm_kernel(n, count, *refs):
    it = iter(refs)
    take = lambda k: [next(it) for _ in range(k)]
    grads = take(6)
    ws, ms, vs = take(3), take(3), take(3)
    w_out, m_out, v_out = take(3), take(3), take(3)
    own40, peer40, got40, own64, peer64, got64 = take(6)
    w40, w64, m40, m64, v40, v64, squares = take(7)
    local_sem, pair_send, pair_recv, ring_send, ring_recv = take(5)
    sq_send, sq_recv, gat_send, gat_recv, cross_send, cross_recv = take(6)

    here = Place()
    me, core = here.me, here.core
    streams = [(layer, kind) for kind in range(4) for layer in (1, 0)]
    sign = lambda kind: 1 - 2 * (kind % 2)

    def own(layer, kind):
        return (own40 if kind < 2 else own64).at[layer, kind % 2]

    def peer(layer, kind):
        return (peer40 if kind < 2 else peer64).at[layer, kind % 2]

    def got(layer, kind):
        return (got40 if kind < 2 else got64).at[layer, kind % 2]

    def source(layer, kind, of_core):
        g = grads[3 * layer + min(kind, 2)]
        return g.at[:, of_core] if kind < 2 else g.at[:, of_core, kind - 2]

    loads = []

    def load(src, dst):
        c = pltpu.make_async_copy(src, dst, local_sem.at[len(loads)])
        c.start()
        loads.append(c)

    for layer, kind in streams:
        load(source(layer, kind, core), own(layer, kind))
    for side, x40, x64, per in ((ws, w40, w64, True), (ms, m40, m64, False), (vs, v40, v64, False)):
        for i in range(2):
            load(side[i].at[:, me] if per else side[i], x40.at[i])
        load(side[2].at[:, me] if per else side[2], x64)

    greet(n)
    pairs = []
    for i, (layer, kind) in enumerate(streams):
        c = remote(source(layer, kind, 1 - core), peer(layer, kind), pair_send.at[i], pair_recv.at[i], here.partner)
        c.start()
        pairs.append(c)

    def hop(i, layer, kind, t):
        q = here.chip_at(-sign(kind) * (1 + t))
        return remote(own(layer, kind).at[q], got(layer, kind).at[t], ring_send.at[i, t], ring_recv.at[i, t], here.device_at(sign(kind)))

    for i, (layer, kind) in enumerate(streams):
        loads[i].wait()
        pairs[i].wait_recv()
        q = here.chip_at(-sign(kind))
        mine = own(layer, kind).at[q]
        mine[...] = (wide(mine) + wide(peer(layer, kind).at[q])).astype(BF16)
        hop(i, layer, kind, 0).start()

    @pl.loop(1, HOPS)
    def _(t):
        for i, (layer, kind) in enumerate(streams):
            hop(i, layer, kind, t - 1).wait_recv()
            q = here.chip_at(-sign(kind) * (1 + t))
            mine = own(layer, kind).at[q]
            mine[...] = (wide(mine) + wide(peer(layer, kind).at[q]) + wide(got(layer, kind).at[t - 1])).astype(BF16)
            hop(i, layer, kind, t).start()

    total = jnp.zeros((1, 1), F32)
    for i, (layer, kind) in enumerate(streams):
        hop(i, layer, kind, HOPS - 1).wait_recv()
        mine = own(layer, kind).at[here.chip]
        g = (wide(mine) + wide(peer(layer, kind).at[here.chip]) + wide(got(layer, kind).at[HOPS - 1])).astype(BF16)
        mine[...] = g
        g = g.astype(F32)
        total += jnp.sum(g * g, keepdims=True)

    squares[me] = jnp.broadcast_to(total, squares.shape[1:])

    def tell(j):
        return remote(squares.at[me], squares.at[me], sq_send.at[j], sq_recv.at[me], lax.rem(me + j, n))

    def told(j):
        o = lax.rem(me + n - j, n)
        return remote(squares.at[o], squares.at[o], sq_send.at[j], sq_recv.at[o], o)

    @pl.loop(1, n)
    def _(j):
        tell(j).start()

    for c in loads[len(streams) :]:
        c.wait()

    @pl.loop(1, n)
    def _(j):
        told(j).wait_recv()

    total = jnp.sum(squares[...], axis=0)[:1, :1]
    factor = jnp.minimum(1.0, 0.5 * lax.rsqrt(total / count + 1e-30))

    def whole(layer, kind, owner):
        return w_out[kind].at[layer, owner] if kind < 2 else w_out[2].at[layer, owner, kind - 2]

    def pass_on(i, layer, kind, t):
        o = here.device_at(-sign(kind) * t)
        block = whole(layer, kind, o)
        return remote(block, block, gat_send.at[i, t], gat_recv.at[i, t], here.device_at(sign(kind)))

    def across(i, layer, kind, t):
        o = here.device_at(-sign(kind) * t)
        block = whole(layer, kind, o)
        return remote(block, block, cross_send.at[i, t], cross_recv.at[i, t], here.partner)

    def across_in(i, layer, kind, t):
        o = here.chip_at(-sign(kind) * t) * 2 + 1 - core
        block = whole(layer, kind, o)
        return remote(block, block, cross_send.at[i, t], cross_recv.at[i, t], here.partner)

    for i, (layer, kind) in enumerate(streams):
        sel = (lambda r40, r64: r40.at[kind, layer] if kind < 2 else r64.at[layer, kind - 2])
        out = (lambda r: r[kind].at[layer] if kind < 2 else r[2].at[layer, kind - 2])
        g = wide(own(layer, kind).at[here.chip]) * factor
        w, m, v = adamw(wide(sel(w40, w64)), sel(m40, m64)[...], sel(v40, v64)[...], g)
        whole(layer, kind, me)[...] = w
        pass_on(i, layer, kind, 0).start()
        across(i, layer, kind, 0).start()
        out(m_out)[...] = m
        out(v_out)[...] = v

    @pl.loop(1, HOPS)
    def _(t):
        for i, (layer, kind) in enumerate(streams):
            pass_on(i, layer, kind, t - 1).wait_recv()
            pass_on(i, layer, kind, t).start()
            across(i, layer, kind, t).start()

    for i, (layer, kind) in enumerate(streams):
        pass_on(i, layer, kind, HOPS - 1).wait_recv()
        across(i, layer, kind, HOPS).start()

    for i, (layer, kind) in enumerate(streams):
        pairs[i].wait_send()

    @pl.loop(0, HOPS)
    def _(t):
        for i, (layer, kind) in enumerate(streams):
            hop(i, layer, kind, t).wait_send()
            pass_on(i, layer, kind, t).wait_send()

    @pl.loop(1, n)
    def _(j):
        tell(j).wait_send()

    @pl.loop(0, CHIPS)
    def _(t):
        for i, (layer, kind) in enumerate(streams):
            across(i, layer, kind, t).wait_send()
            across_in(i, layer, kind, t).wait_recv()


def comm(n, count, grads, ws, ms, vs):
    dma = pltpu.SemaphoreType.DMA
    two = lambda k: [pltpu.VMEM((2, 2, k, 40, 2048), BF16), pltpu.VMEM((2, 2, k, 64, 640), BF16)]
    own, peer, got = two(CHIPS), two(CHIPS), two(HOPS)
    scratch = [own[0], peer[0], got[0], own[1], peer[1], got[1]]
    scratch += [pltpu.VMEM((2, 2, 40, 2048), BF16), pltpu.VMEM((2, 2, 64, 640), BF16)]
    scratch += [pltpu.VMEM((2, 2, 40, 2048), F32), pltpu.VMEM((2, 2, 64, 640), F32)] * 2
    scratch += [pltpu.VMEM((n, 8, 128), F32)]
    scratch += [dma((17,)), dma((8,)), dma((8,)), dma((8, HOPS)), dma((8, HOPS)), dma((n,)), dma((n,))]
    scratch += [dma((8, HOPS)), dma((8, HOPS)), dma((8, CHIPS)), dma((8, CHIPS))]
    out_shape = [pltpu.VMEM((2, n, 40, 2048), BF16)] * 2 + [pltpu.VMEM((2, n, 2, 64, 640), BF16)]
    out_shape += ([pltpu.VMEM((2, 40, 2048), F32)] * 2 + [pltpu.VMEM((2, 2, 64, 640), F32)]) * 2
    return pl.pallas_call(
        lambda *refs: comm_kernel(n, count, *refs),
        out_shape=out_shape,
        in_specs=[ANY] * 15,
        out_specs=[pl.BlockSpec(memory_space=pltpu.VMEM)] * 9,
        scratch_shapes=scratch,
        compiler_params=pltpu.CompilerParams(collective_id=0, has_side_effects=True, vmem_limit_bytes=40 * 2**20),
        name="comm",
    )(*grads, *ws, *ms, *vs)


def write_kernel(*refs):
    k = (len(refs) - 1) // 2
    copies = [pltpu.make_async_copy(refs[i], refs[k + i], refs[-1].at[i]) for i in range(k)]
    for c in copies:
        c.start()
    for c in copies:
        c.wait()


def write(arrays):
    return pl.pallas_call(
        write_kernel,
        out_shape=[jax.ShapeDtypeStruct(a.shape, a.dtype) for a in arrays],
        in_specs=[pl.BlockSpec(memory_space=pltpu.VMEM)] * len(arrays),
        out_specs=[ANY] * len(arrays),
        scratch_shapes=[pltpu.SemaphoreType.DMA((len(arrays),))],
        compiler_params=pltpu.CompilerParams(vmem_limit_bytes=2**20),
        name="write",
    )(*arrays)


def solution(mesh):
    n = mesh.shape["dp"]

    def body(x, dy, wg, wu, wd, mg, mu, md, vg, vu, vd):
        x, dy = x[0], dy[0]
        a0, _ = normed(x)
        gate0, up0 = dot(a0, wg[0], ((1,), (0,))), dot(a0, wu[0], ((1,), (0,)))
        inner0 = (jax.nn.silu(gate0) * up0).astype(BF16)
        h1 = x + dot(inner0, wd[0], ((1,), (0,))).astype(BF16)
        a1, s1 = normed(h1)
        gate1, up1 = dot(a1, wg[1], ((1,), (0,))), dot(a1, wu[1], ((1,), (0,)))
        d1 = dot(dy, wd[1], ((1,), (1,))).astype(BF16).astype(F32)
        inner1, dg1, du1 = gated_grads(gate1, up1, d1)
        g_d1 = dot(inner1, dy, ((0,), (0,))).astype(BF16)
        g_g1 = dot(a1, dg1, ((0,), (0,))).astype(BF16)
        g_u1 = dot(a1, du1, ((0,), (0,))).astype(BF16)
        da = (dot(dg1, wg[1], ((1,), (1,))) + dot(du1, wu[1], ((1,), (1,)))).astype(BF16).astype(F32)
        h = h1.astype(F32)
        dh = dy + (s1 * da - h * (s1**3 * jnp.mean(da * h, -1, keepdims=True))).astype(BF16)
        g_d0 = dot(inner0, dh, ((0,), (0,))).astype(BF16)
        d0 = dot(dh, wd[0], ((1,), (1,))).astype(BF16).astype(F32)
        _, dg0, du0 = gated_grads(gate0, up0, d0)
        g_g0 = dot(a0, dg0, ((0,), (0,))).astype(BF16)
        g_u0 = dot(a0, du0, ((0,), (0,))).astype(BF16)

        flat = lambda g: g.reshape(CHIPS, 2, 40, 2048)
        grads = [flat(g_g0), flat(g_u0), g_d0.reshape(CHIPS, 2, 2, 64, 640)]
        grads += [flat(g_g1), flat(g_u1), g_d1.reshape(CHIPS, 2, 2, 64, 640)]
        rows = lambda w: w.reshape(2, n, 40, 2048)
        ws = [rows(wg), rows(wu), wd.reshape(2, n, 2, 64, 640)]
        split = lambda t: t.reshape(2, 2, 64, 640)
        count = wg.size + wu.size + wd.size
        outs = write(comm(n, count, grads, ws, [mg, mu, split(md)], [vg, vu, split(vd)]))
        shapes = [wg, wu, wd, mg, mu, md, vg, vu, vd]
        return tuple(o.reshape(s.shape) for o, s in zip(outs, shapes, strict=True))

    whole, mine = P(), P(None, "dp", None)
    seq, out = P(("rep", "dp")), P("rep", "dp", None)
    return jax.shard_map(
        body,
        mesh=mesh,
        in_specs=(seq, seq) + (whole,) * 3 + (mine,) * 6,
        out_specs=(P("rep"),) * 3 + (out,) * 6,
        check_vma=False,
    )
```

time: 748 us -> 400 us (0.53)
  waiting for transfers between devices: 450 us -> 0 us
  Pallas kernels: 0 us -> 180 us
  blocking collectives: 30 us -> 0 us
  local copies, waits for them, and re-layouts: 23.2 us -> 6.06 us
  between operations: 17.2 us -> 1.08 us
  other arithmetic: 17.6 us -> 4.96 us
    reduce_scatter x6 -> x0, waiting for transfers between devices: 287 us -> none  [scatter(): lax.psum_scatter(g.astype(BF16), 'dp', scatter_dimension=0, tiled=True)]
    pallas_call x0 -> x2, Pallas kernels: none -> 180 us  [the longest x1 173 us: comm(): pl.pallas_call(lambda *refs: comm_kernel(n, count, *refs), out_shape=out_...]
    all_gather x3 -> x0, waiting for transfers between devices: 163 us -> none  [body(): new.append((lax.all_gather(w, 'dp', axis=1, tiled=True), m, v))]
    psum x1 -> x0, blocking collectives: 30 us -> none  [body(): squares = lax.psum(sum((jnp.sum(g * g) for g in grads)), 'dp')]
    unnamed x53 -> x34, local copies, waits for them, and re-layouts: 23.2 us -> 6.06 us
  transfers between devices with their start and end apart: 9 -> 0, of which waited for: 8 -> 0; matrix products, arithmetic and copies ran while one was open for 16% -> 0% of each run, Pallas kernels for 0% -> 0%
where the time goes in v2:
time: 400 us; the launch traced here: 393 us
  matrix products  200 us (50%)
  Pallas kernels  180 us (45%)
  local copies, waits for them, and re-layouts  6.06 us (2%)
  other arithmetic  4.96 us (1%)
    dot_general x15, matrix products, dot(): return lax.dot_general(a, b, (dims, ((), ())), preferred_element_type=F32)  200 us
    pallas_call x1, Pallas kernels, comm(): pl.pallas_call(lambda *refs: comm_kernel(n, count, *refs), out_shape=out_...  173 us

profile of v2, /device:TPU:0, one launch (start us, length us, event | category | flops | bytes accessed | tf_op | source)
XLA Modules:
  0.0 392.7 jit_solution(939801324019074782)
XLA Ops:
  0.6 3.0 copy.20
  3.6 0.0 copy-start
  3.7 0.6 fusion.13
  4.2 0.0 copy-start.6
  4.2 12.7 %fusion.43 = f32[2048,2048]{1,0:T(8,128)} fusion(bf16[2,640,2048]{2,1,0:T(8,128)(2,1)} %param.13, bf16[1,2048,640]{2,1,0:T(8,128)(2,1)} %param.11, f32[2048]{0:T(1024)S(1)} %add_rsqrt_fusion.1), kind=kOutput, calls=%fused_computation.60 | convolution fusion | flops 5372641280 | bytes 22028288 | tf_op jit(solution)/shard_map/dot_general | solution.py:16
  16.9 0.0 copy-done.6
  16.9 16.7 %multiply_convert_fusion.1 = (bf16[2048,2048]{1,0:T(8,128)(2,1)}, f32[2048,2048]{1,0:T(8,128)}) fusion(f32[2048,2048]{1,0:T(8,128)} %fusion.43, bf16[2,640,2048]{2,1,0:T(8,128)(2,1)} %param.14, bf16[1,2048,640]{2,1,0:T(8,128)(2,1)} %param.11, f32[2048]{0:T(1024)S(1)} %add_rsqrt_fusion.1), kind=kOutput, calls=%fused_computation.12 | convolution fusion | flops 5397807104 | bytes 47194112 | tf_op jit(solution)/shard_map/dot_general | solution.py:16
  33.7 0.0 copy-done
  33.7 9.2 %fusion.17 = (f32[2048]{0:T(1024)S(1)}, bf16[2048,640]{0,1:T(8,128)(2,1)S(1)}) fusion(bf16[2048,2048]{1,0:T(8,128)(2,1)} %get-tuple-element.45, bf16[2,2048,640]{2,1,0:T(8,128)(2,1)} %param.15, bf16[1,2048,640]{1,2,0:T(8,128)(2,1)S(1)} %copy.20), kind=kOutput, calls=%fused_computation.32 | convolution fusion | flops 5375260672 | bytes 16261120 | tf_op jit(solution)/shard_map/dot_general | solution.py:16
  42.8 0.0 copy-start.2
  42.8 0.0 copy-start.4
  42.9 0.0 copy-start.3
  42.9 13.2 %fusion.33 = f32[2048,2048]{1,0:T(8,128)} fusion(bf16[2,640,2048]{2,1,0:T(8,128)(2,1)} %param.13, bf16[2048,640]{0,1:T(8,128)(2,1)S(1)} %get-tuple-element.48, f32[2048]{0:T(1024)S(1)} %add_rsqrt_fusion), kind=kOutput, calls=%fused_computation.50 | convolution fusion | flops 5372641280 | bytes 22028288 | tf_op jit(solution)/shard_map/dot_general | solution.py:16
  56.1 0.0 copy-done.2
  56.1 0.0 copy-done.4
  56.1 0.0 copy-done.3
  56.1 10.7 %convolution_convert_fusion.1 = bf16[2048,2048]{1,0:T(8,128)(2,1)} fusion(bf16[1,2048,640]{2,1,0:T(8,128)(2,1)S(1)} %copy-done.3, bf16[2,2048,640]{2,1,0:T(8,128)(2,1)} %param.15), kind=kOutput, calls=%fused_computation.24 | convolution fusion | flops 5372903424 | bytes 13631488 | tf_op jit(solution)/shard_map/dot_general | solution.py:16
  66.8 23.1 %fusion.1 = (bf16[2048,2048]{1,0:T(8,128)(2,1)}, f32[2048,2048]{1,0:T(8,128)}) fusion(bf16[2048,2048]{1,0:T(8,128)(2,1)} %convolution_convert_fusion.1, f32[2048,2048]{1,0:T(8,128)} %fusion.33, bf16[2,640,2048]{2,1,0:T(8,128)(2,1)} %param.14, bf16[2048,640]{0,1:T(8,128)(2,1)} %copy-done.2, f32[2048]{0:T(1024)S(1)} %add_rsqrt_fusion), kind=kOutput, calls=%fused_computation.5 | convolution fusion | flops 5418778624 | bytes 55582720 | tf_op jit(solution)/shard_map/dot_general | solution.py:16
  89.9 0.0 slice-start
  89.9 0.0 slice-start.2
  89.9 16.8 %fusion.26 = bf16[2048,640]{1,0:T(8,128)(2,1)} fusion(f32[2048,2048]{1,0:T(8,128)} %get-tuple-element.50, bf16[1,2048,640]{2,1,0:T(8,128)(2,1)} %param.12, f32[2048,2048]{1,0:T(8,128)} %fusion.33), kind=kOutput, calls=%fused_computation.39 | convolution fusion | flops 5395185664 | bytes 38797312 | tf_op jit(solution)/shard_map/dot_general | solution.py:16
  106.7 0.0 slice-start.1
  106.7 0.0 slice-start.3
  106.7 13.4 %convolution_convert_fusion.2 = bf16[640,2048]{1,0:T(8,128)(2,1)} fusion(bf16[2048,640]{0,1:T(8,128)(2,1)} %copy-done.2, f32[2048]{0:T(1024)S(1)} %add_rsqrt_fusion, bf16[2048,2048]{1,0:T(8,128)(2,1)} %convolution_convert_fusion.1, f32[2048,2048]{1,0:T(8,128)} %fusion.33), kind=kOutput, calls=%fused_computation.40 | convolution fusion | flops 5403312128 | bytes 30416896 | tf_op jit(solution)/shard_map/dot_general | solution.py:16
  120.1 0.0 copy-start.8
  120.1 10.7 %convolution_convert_fusion.3 = bf16[640,2048]{1,0:T(8,128)(2,1)} fusion(bf16[2048,2048]{1,0:T(8,128)(2,1)} %get-tuple-element.49, bf16[2048,640]{0,1:T(8,128)(2,1)} %copy-done.2, f32[2048]{0:T(1024)S(1)} %add_rsqrt_fusion), kind=kOutput, calls=%fused_computation.41 | convolution fusion | flops 5373952000 | bytes 13639680 | tf_op jit(solution)/shard_map/dot_general | solution.py:16
  130.9 0.0 slice-done
  130.9 0.0 slice-done.1
  130.9 0.0 copy-done.8
  130.9 7.4 %fusion.31 = f32[2048,640]{0,1:T(8,128)} fusion(bf16[2048,2048]{1,0:T(8,128)(2,1)S(1)} %copy-done.8, bf16[2,640,2048]{2,1,0:T(8,128)(2,1)S(1)} %bitcast.78), kind=kOutput, calls=%fused_computation.48 | convolution fusion | flops 5368709120 | bytes 16252928 | tf_op jit(solution)/shard_map/dot_general | solution.py:16
  138.3 0.0 slice-done.2
  138.3 0.0 slice-done.3
  138.3 0.0 copy-start.5
  138.3 15.6 %fusion.19 = (f32[2048]{0:T(1024)S(1)}, bf16[2048,640]{0,1:T(8,128)(2,1)}) fusion(bf16[2048,640]{0,1:T(8,128)(2,1)} %copy-done.2, f32[2048,640]{0,1:T(8,128)} %fusion.31, bf16[2,640,2048]{2,1,0:T(8,128)(2,1)S(1)} %bitcast.81, bf16[2048,2048]{1,0:T(8,128)(2,1)} %convolution_convert_fusion.1, f32[2048,2048]{1,0:T(8,128)} %fusion.33), kind=kOutput, calls=%fused_computation.34 | convolution fusion | flops 5405931520 | bytes 38281216 | tf_op jit(solution)/shard_map/dot_general | solution.py:16
  153.9 0.0 copy-done.5
  153.9 3.0 copy.21
  156.9 0.0 slice-start.4
  156.9 4.4 %fusion.28 = bf16[2048,640]{0,1:T(8,128)(2,1)S(1)} fusion(bf16[2048,640]{0,1:T(8,128)(2,1)} %copy-done.2, bf16[2048,640]{0,1:T(8,128)(2,1)} %get-tuple-element.52, bf16[1,2048,640]{1,2,0:T(8,128)(2,1)S(1)} %copy.21, f32[2048]{0:T(1024)S(1)} %fusion.64, f32[2048]{0:T(1024)S(1)} %add_rsqrt_fusion), kind=kLoop, calls=%fused_computation.45 | loop fusion | flops 9175040 | bytes 10502144 | tf_op jit(solution)/shard_map/add | solution.py:301
  161.3 0.0 slice-start.5
  161.3 10.5 %convolution_convert_fusion.4 = bf16[2048,640]{1,0:T(8,128)(2,1)} fusion(bf16[2048,2048]{1,0:T(8,128)(2,1)} %get-tuple-element.45, bf16[2048,640]{0,1:T(8,128)(2,1)S(1)} %fusion.28), kind=kOutput, calls=%fused_computation.42 | convolution fusion | flops 5370019840 | bytes 13631488 | tf_op jit(solution)/shard_map/dot_general | solution.py:16
  171.8 0.0 slice-done.4
  171.8 0.0 slice-done.5
  171.8 0.0 copy-start.1
  171.8 0.0 copy-start.7
  171.8 7.2 %convolution_convert_fusion = bf16[2048,2048]{1,0:T(8,128)(2,1)S(1)} fusion(bf16[2048,640]{0,1:T(8,128)(2,1)S(1)} %fusion.28, bf16[2,2048,640]{2,1,0:T(8,128)(2,1)S(1)} %bitcast.84), kind=kOutput, calls=%fused_computation.23 | convolution fusion | flops 5372903424 | bytes 13631488 | tf_op jit(solution)/shard_map/dot_general | solution.py:16
  179.0 0.0 copy-done.1
  179.0 0.0 copy-done.7
  179.0 0.0 copy-start.9
  179.1 14.0 %fusion.23 = bf16[640,2048]{1,0:T(8,128)(2,1)} fusion(bf16[2048,2048]{1,0:T(8,128)(2,1)S(1)} %convolution_convert_fusion, bf16[1,2048,640]{1,2,0:T(8,128)(2,1)S(1)} %copy-done.1, f32[2048]{0:T(1024)S(1)} %copy-done.7, f32[2048,2048]{1,0:T(8,128)} %fusion.43), kind=kOutput, calls=%fused_computation.38 | convolution fusion | flops 5403312128 | bytes 30416896 | tf_op jit(solution)/shard_map/dot_general | solution.py:16
  193.0 0.0 copy-done.9
  193.0 19.2 %fusion.20 = bf16[640,2048]{1,0:T(8,128)(2,1)} fusion(f32[2048,2048]{1,0:T(8,128)} %get-tuple-element.46, bf16[2048,2048]{1,0:T(8,128)(2,1)} %copy-done.9, f32[2048,2048]{1,0:T(8,128)} %fusion.43, bf16[1,2048,640]{1,2,0:T(8,128)(2,1)S(1)} %copy-done.1, f32[2048]{0:T(1024)S(1)} %copy-done.7), kind=kOutput, calls=%fused_computation.37 | convolution fusion | flops 5420089344 | bytes 47194112 | tf_op jit(solution)/shard_map/dot_general | solution.py:16
  212.2 173.5 %comm.1 = (bf16[2,16,40,2048]{3,2,1,0:T(8,128)(2,1)S(1)}, bf16[2,16,40,2048]{3,2,1,0:T(8,128)(2,1)S(1)}, bf16[2,16,2,64,640]{4,3,2,1,0:T(8,128)(2,1)S(1)}, f32[2...) custom-call(bf16[8,2,40,2048]{3,2,1,0:T(8,128)(2,1)} %bitcast.90, ...), custom_call_target="tpu_custom_call" | custom-call | tf_op jit(solution)/shard_map/comm/pallas_call | solution.py:251
  385.7 6.8 %write.1 = (bf16[2,16,40,2048]{3,2,1,0:T(8,128)(2,1)}, bf16[2,16,40,2048]{3,2,1,0:T(8,128)(2,1)}, bf16[2,16,2,64,640]{4,3,2,1,0:T(8,128)(2,1)}, f32[2,40,2048]{2...) custom-call(bf16[2,16,40,2048]{3,2,1,0:T(8,128)(2,1)S(1)} %get-tuple, ...), custom_call_target="tpu_custom_call" | custom-call | tf_op jit(solution)/shard_map/write/pallas_call | solution.py:272
  (6 shorter events, 0.0 us)
Async XLA Ops:
  3.6 30.0 %copy-start = (bf16[1,2048,640]{1,2,0:T(8,128)(2,1)}, bf16[1,2048,640]{1,2,0:T(8,128)(2,1)S(1)}, u32[]{:S(2)}) copy-start(bf16[1,2048,640]{1,2,0:T(8,128)(2,1)S(1)} %copy.20) | copy-start | bytes 7864324
  4.2 12.7 %copy-start.6 = (f32[2048]{0:T(1024)}, f32[2048]{0:T(1024)S(1)}, u32[]{:S(2)}) copy-start(f32[2048]{0:T(1024)S(1)} %add_rsqrt_fusion.1) | copy-start | bytes 24580
  42.8 13.3 %copy-start.2 = (bf16[2048,640]{0,1:T(8,128)(2,1)}, bf16[2048,640]{0,1:T(8,128)(2,1)S(1)}, u32[]{:S(2)}) copy-start(bf16[2048,640]{0,1:T(8,128)(2,1)S(1)} %get-tuple-element.48) | copy-start | bytes 7864324
  42.8 13.2 %copy-start.4 = (f32[2048]{0:T(1024)}, f32[2048]{0:T(1024)S(1)}, u32[]{:S(2)}) copy-start(f32[2048]{0:T(1024)S(1)} %get-tuple-element.47) | copy-start | bytes 24580
  42.9 13.2 %copy-start.3 = (bf16[1,2048,640]{2,1,0:T(8,128)(2,1)S(1)}, bf16[1,2048,640]{2,1,0:T(8,128)(2,1)}, u32[]{:S(2)}) copy-start(bf16[1,2048,640]{2,1,0:T(8,128)(2,1)} %param.12) | copy-start | bytes 7864324
  89.9 40.9 %slice-start = ((s8[5242880]{0:T(1024)(128)(4,1)}), s8[1048576]{0:T(1024)(128)(4,1)S(1)}, s32[]{:S(2)}) async-start(s8[5242880]{0:T(1024)(128)(4,1)} %bitcast.77), calls=%async_computation | async-start | bytes 2097152
  89.9 48.3 %slice-start.2 = ((s8[5242880]{0:T(1024)(128)(4,1)}), s8[4194304]{0:T(1024)(128)(4,1)S(1)}, s32[]{:S(2)}) async-start(s8[5242880]{0:T(1024)(128)(4,1)} %bitcast.80), calls=%async_computation.2 | async-start | bytes 8388608
  106.7 24.2 %slice-start.1 = ((s8[5242880]{0:T(1024)(128)(4,1)}), s8[4194304]{0:T(1024)(128)(4,1)S(1)}, s32[]{:S(2)}) async-start(s8[5242880]{0:T(1024)(128)(4,1)} %bitcast.77), calls=%async_computation.1 | async-start | bytes 8388608
  106.7 31.6 %slice-start.3 = ((s8[5242880]{0:T(1024)(128)(4,1)}), s8[1048576]{0:T(1024)(128)(4,1)S(1)}, s32[]{:S(2)}) async-start(s8[5242880]{0:T(1024)(128)(4,1)} %bitcast.80), calls=%async_computation.3 | async-start | bytes 2097152
  120.1 10.8 %copy-start.8 = (bf16[2048,2048]{1,0:T(8,128)(2,1)S(1)}, bf16[2048,2048]{1,0:T(8,128)(2,1)}, u32[]{:S(2)}) copy-start(bf16[2048,2048]{1,0:T(8,128)(2,1)} %get-tuple-element.49) | copy-start | bytes 25165828
  138.3 15.6 %copy-start.5 = (f32[2048]{0:T(1024)S(1)}, f32[2048]{0:T(1024)}, u32[]{:S(2)}) copy-start(f32[2048]{0:T(1024)} %copy-done.4) | copy-start | bytes 24580
  156.9 14.9 %slice-start.4 = ((s8[5242880]{0:T(1024)(128)(4,1)}), s8[1048576]{0:T(1024)(128)(4,1)S(1)}, s32[]{:S(2)}) async-start(s8[5242880]{0:T(1024)(128)(4,1)} %bitcast.83), calls=%async_computation.4 | async-start | bytes 2097152
  161.3 10.5 %slice-start.5 = ((s8[5242880]{0:T(1024)(128)(4,1)}), s8[4194304]{0:T(1024)(128)(4,1)S(1)}, s32[]{:S(2)}) async-start(s8[5242880]{0:T(1024)(128)(4,1)} %bitcast.83), calls=%async_computation.5 | async-start | bytes 8388608
  171.8 7.3 %copy-start.1 = (bf16[1,2048,640]{1,2,0:T(8,128)(2,1)S(1)}, bf16[1,2048,640]{1,2,0:T(8,128)(2,1)}, u32[]{:S(2)}) copy-start(bf16[1,2048,640]{1,2,0:T(8,128)(2,1)} %copy-done) | copy-start | bytes 7864324
  171.8 7.3 %copy-start.7 = (f32[2048]{0:T(1024)S(1)}, f32[2048]{0:T(1024)}, u32[]{:S(2)}) copy-start(f32[2048]{0:T(1024)} %copy-done.6) | copy-start | bytes 24580
  179.0 14.0 %copy-start.9 = (bf16[2048,2048]{1,0:T(8,128)(2,1)}, bf16[2048,2048]{1,0:T(8,128)(2,1)S(1)}, u32[]{:S(2)}) copy-start(bf16[2048,2048]{1,0:T(8,128)(2,1)S(1)} %convolution_convert_fusion) | copy-start | bytes 25165828

commit v3 on v2

--- a/solution.py
+++ b/solution.py
@@ -29,10 +29,169 @@
     return (w - 0.02 * step).astype(BF16), m, v
 
 
-def gated_grads(gate, up, d):
-    s = jax.nn.sigmoid(gate)
+TILE = 512
+FB = 256
+
+
+def tiles(tokens):
+    return [pl.ds(r, TILE) for r in range(0, tokens, TILE)]
+
+
+def nn(a, b):
+    return dot(a, b, ((1,), (0,)))
+
+
+def nt(a, b):
+    return dot(a, b, ((1,), (1,)))
+
+
+def gates(a, wg, wu):
+    gate, up = nn(a, wg), nn(a, wu)
+    s = 0.5 + 0.5 * jnp.tanh(0.5 * gate)
     silu = gate * s
-    return (silu * up).astype(BF16), (d * up * (s + silu * (1 - s))).astype(BF16), (d * silu).astype(BF16)
+    return silu, up * (s + silu * (1 - s)), (silu * up).astype(BF16)
+
+
+def forward_kernel(x, dy, wg, wu, wd, silu_out, slope_out, inner_out, at_out, dyt_out, h_out, a_out, a, acc):
+    j = pl.program_id(0)
+    tokens = x.shape[0]
+
+    @pl.when(j == 0)
+    def _():
+        for r in tiles(tokens):
+            a[r] = normed(x[r])[0]
+            acc[r] = jnp.zeros((TILE, x.shape[1]), F32)
+
+    part = pl.ds(pl.multiple_of(j * FB, FB), FB)
+    at_out[...] = a[part].T
+    dyt_out[...] = dy[part].T
+    for r in tiles(tokens):
+        silu, slope, inner = gates(a[r], wg[...], wu[...])
+        silu_out[r], slope_out[r], inner_out[r] = silu, slope, inner
+        acc[r] += nn(inner, wd[...])
+
+    @pl.when(j == pl.num_programs(0) - 1)
+    def _():
+        for r in tiles(tokens):
+            h = x[r] + acc[r].astype(BF16)
+            h_out[r] = h
+            a_out[r] = normed(h)[0]
+
+
+def forward(x, dy, wg, wu, wd):
+    tokens, d = x.shape
+    steps = tokens // FB
+    whole = lambda s: pl.BlockSpec(s, lambda j: (0, 0))
+    cols = lambda rows: pl.BlockSpec((rows, FB), lambda j: (0, j))
+    wcols = pl.BlockSpec((None, d, FB), lambda j: (0, 0, j))
+    wrows = pl.BlockSpec((None, FB, d), lambda j: (0, j, 0))
+    ff = wg.shape[2]
+    shape = jax.ShapeDtypeStruct
+    return pl.pallas_call(
+        forward_kernel,
+        grid=(ff // FB,),
+        in_specs=[whole(x.shape), whole(x.shape), wcols, wcols, wrows],
+        out_specs=[cols(tokens), cols(tokens), cols(tokens), cols(d), cols(d), whole(x.shape), whole(x.shape)],
+        out_shape=[shape((tokens, ff), F32)] * 2
+        + [shape((tokens, ff), BF16)]
+        + [shape((d, tokens), BF16)] * 2
+        + [shape(x.shape, BF16)] * 2,
+        scratch_shapes=[pltpu.VMEM(x.shape, BF16), pltpu.VMEM(x.shape, F32)],
+        compiler_params=pltpu.CompilerParams(vmem_limit_bytes=60 * 2**20),
+        name="forward",
+    )(x, dy, wg, wu, wd)
+
+
+def store_gradients(outs, dyt, at, inner, dg, du):
+    gate_out, up_out, down_out = outs
+    down_out[...] = nn(dyt[...], inner[...]).T.reshape(down_out.shape).astype(BF16)
+    gate_out[...] = nn(at[...], dg[...]).reshape(gate_out.shape).astype(BF16)
+    up_out[...] = nn(at[...], du[...]).reshape(up_out.shape).astype(BF16)
+
+
+def backward_kernel(dy_in, a_in, h_in, dyt_in, a0t_in, wg, wu, wd, silu, slope, inner0, *refs):
+    outs1, outs0 = refs[0:3], refs[3:6]
+    d, a, h, dt, at, da, inner, dg, du, sems = refs[6:]
+    step = pl.program_id(0)
+    half = pl.num_programs(0) // 2
+    tokens = d.shape[0]
+
+    def load(src, dst, i):
+        return pltpu.make_async_copy(src, dst, sems.at[i])
+
+    @pl.when(step == 0)
+    def _():
+        first = [load(dy_in, d, 0), load(a_in, a, 1), load(dyt_in, dt, 2), load(h_in, h, 3)]
+        for c in first:
+            c.start()
+        for r in tiles(tokens):
+            da[r] = jnp.zeros((TILE, d.shape[1]), F32)
+        for c in first:
+            c.wait()
+        at[...] = a[...].T
+
+    @pl.when(step < half)
+    def _():
+        both = jnp.concatenate([wg[...], wu[...]], axis=1)
+        for r in tiles(tokens):
+            by_inner = nt(d[r], wd[...]).astype(BF16).astype(F32)
+            silu, slope, product = gates(a[r], wg[...], wu[...])
+            by_gate, by_up = (by_inner * slope).astype(BF16), (by_inner * silu).astype(BF16)
+            inner[r], dg[r], du[r] = product, by_gate, by_up
+            da[r] += nt(jnp.concatenate([by_gate, by_up], axis=1), both)
+        store_gradients(outs1, dt, at, inner, dg, du)
+
+    @pl.when(step == half - 1)
+    def _():
+        c = load(a0t_in, at, 0)
+        c.start()
+        for r in tiles(tokens):
+            wide = h[r].astype(F32)
+            scale = lax.rsqrt(jnp.mean(wide**2, -1, keepdims=True) + 1e-6)
+            by_a = da[r].astype(BF16).astype(F32)
+            by_h = scale * by_a - wide * (scale**3 * jnp.mean(by_a * wide, -1, keepdims=True))
+            d[r] = d[r] + by_h.astype(BF16)
+        dt[...] = d[...].T
+        c.wait()
+
+    @pl.when(step >= half)
+    def _():
+        for r in tiles(tokens):
+            by_inner = nt(d[r], wd[...]).astype(BF16).astype(F32)
+            dg[r], du[r] = (by_inner * slope[r]).astype(BF16), (by_inner * silu[r]).astype(BF16)
+        store_gradients(outs0, dt, at, inner0, dg, du)
+
+
+def backward(n, dy, a1, h1, dyt, a0t, wg, wu, wd, silu, slope, inner0):
+    tokens, d = dy.shape
+    ff = wg.shape[2]
+    half = ff // FB
+    early = lambda s: jnp.minimum(s, half - 1)
+    late = lambda s: jnp.maximum(s - half, 0)
+    layer = lambda s: 1 - s // half
+    wcols = pl.BlockSpec((None, d, FB), lambda s: (1, 0, early(s)))
+    wrows = pl.BlockSpec((None, FB, d), lambda s: (layer(s), s % half, 0))
+    saved = pl.BlockSpec((tokens, FB), lambda s: (0, late(s)))
+
+    def outs(at):
+        cols = pl.BlockSpec((n, d // n, FB), lambda s: (0, 0, at(s)))
+        return [cols, cols, pl.BlockSpec((FB * n // ff, 2, ff // n // 2, d), lambda s: (at(s), 0, 0, 0))]
+
+    shape = lambda *s: jax.ShapeDtypeStruct(s, BF16)
+    shapes = [shape(n, d // n, ff)] * 2 + [shape(n, 2, ff // n // 2, d)]
+    rows, block = pltpu.VMEM((tokens, d), BF16), pltpu.VMEM((tokens, FB), BF16)
+    flipped = pltpu.VMEM((d, tokens), BF16)
+    return pl.pallas_call(
+        backward_kernel,
+        grid=(2 * half,),
+        in_specs=[ANY] * 5 + [wcols, wcols, wrows, saved, saved, saved],
+        out_specs=outs(early) + outs(late),
+        out_shape=shapes * 2,
+        scratch_shapes=[rows, rows, rows, flipped, flipped, pltpu.VMEM((tokens, d), F32), block, block, block]
+        + [pltpu.SemaphoreType.DMA((4,))],
+        compiler_params=pltpu.CompilerParams(vmem_limit_bytes=60 * 2**20),
+        name="backward",
+    )(dy, a1, h1, dyt, a0t, wg, wu, wd, silu, slope, inner0)
 
 
 class Place:
@@ -285,29 +444,10 @@
 
     def body(x, dy, wg, wu, wd, mg, mu, md, vg, vu, vd):
         x, dy = x[0], dy[0]
-        a0, _ = normed(x)
-        gate0, up0 = dot(a0, wg[0], ((1,), (0,))), dot(a0, wu[0], ((1,), (0,)))
-        inner0 = (jax.nn.silu(gate0) * up0).astype(BF16)
-        h1 = x + dot(inner0, wd[0], ((1,), (0,))).astype(BF16)
-        a1, s1 = normed(h1)
-        gate1, up1 = dot(a1, wg[1], ((1,), (0,))), dot(a1, wu[1], ((1,), (0,)))
-        d1 = dot(dy, wd[1], ((1,), (1,))).astype(BF16).astype(F32)
-        inner1, dg1, du1 = gated_grads(gate1, up1, d1)
-        g_d1 = dot(inner1, dy, ((0,), (0,))).astype(BF16)
-        g_g1 = dot(a1, dg1, ((0,), (0,))).astype(BF16)
-        g_u1 = dot(a1, du1, ((0,), (0,))).astype(BF16)
-        da = (dot(dg1, wg[1], ((1,), (1,))) + dot(du1, wu[1], ((1,), (1,)))).astype(BF16).astype(F32)
-        h = h1.astype(F32)
-        dh = dy + (s1 * da - h * (s1**3 * jnp.mean(da * h, -1, keepdims=True))).astype(BF16)
-        g_d0 = dot(inner0, dh, ((0,), (0,))).astype(BF16)
-        d0 = dot(dh, wd[0], ((1,), (1,))).astype(BF16).astype(F32)
-        _, dg0, du0 = gated_grads(gate0, up0, d0)
-        g_g0 = dot(a0, dg0, ((0,), (0,))).astype(BF16)
-        g_u0 = dot(a0, du0, ((0,), (0,))).astype(BF16)
-
-        flat = lambda g: g.reshape(CHIPS, 2, 40, 2048)
-        grads = [flat(g_g0), flat(g_u0), g_d0.reshape(CHIPS, 2, 2, 64, 640)]
-        grads += [flat(g_g1), flat(g_u1), g_d1.reshape(CHIPS, 2, 2, 64, 640)]
+        silu, slope, inner0, a0t, dyt, h1, a1 = forward(x, dy, wg, wu, wd)
+        grads = backward(n, dy, a1, h1, dyt, a0t, wg, wu, wd, silu, slope, inner0)
+        by = lambda g: g.reshape(CHIPS, 2, *g.shape[1:])
+        grads = [by(g) for g in grads[3:] + grads[:3]]
         rows = lambda w: w.reshape(2, n, 40, 2048)
         ws = [rows(wg), rows(wu), wd.reshape(2, n, 2, 64, 640)]
         split = lambda t: t.reshape(2, 2, 64, 640)

time: 400 us -> 315 us (0.79); the launches traced: 393 us -> 315 us
  matrix products: 200 us -> 0 us
  Pallas kernels: 180 us -> 314 us
  local copies, waits for them, and re-layouts: 6.06 us -> 0 us
  other arithmetic: 4.96 us -> 0 us
    dot_general x15 -> x0, matrix products: 200 us -> none  [dot(): return lax.dot_general(a, b, (dims, ((), ())), preferred_element_type=F32)]
    pallas_call x0 -> x2, Pallas kernels: none -> 134 us  [the longest x1 100 us: backward(): pl.pallas_call(backward_kernel, grid=(2 * half,), in_specs=[ANY] * 5 + [w...]
    unnamed x34 -> x0, local copies, waits for them, and re-layouts: 6.06 us -> none
    add x1 -> x0, other arithmetic: 4.38 us -> none  [body(): dy + (s1 * da - h * (s1 ** 3 * jnp.mean(da * h, -1, keepdims=True))).asty...]
where the time goes in v3:
time: 315 us
  Pallas kernels  314 us (100%)
    pallas_call x1, Pallas kernels, comm(): pl.pallas_call(lambda *refs: comm_kernel(n, count, *refs), out_shape=out_...  174 us
    pallas_call x1, Pallas kernels, backward(): pl.pallas_call(backward_kernel, grid=(2 * half,), in_specs=[ANY] * 5 + [w...  100 us
    pallas_call x1, Pallas kernels, forward(): pl.pallas_call(forward_kernel, grid=(ff // FB,), in_specs=[whole(x.shape)...  33.6 us
    pallas_call x1, Pallas kernels, write(): pl.pallas_call(write_kernel, out_shape=[jax.ShapeDtypeStruct(a.shape, a.d...  6.79 us

profile of v3, /device:TPU:0, one launch (start us, length us, event | category | flops | bytes accessed | tf_op | source)
XLA Modules:
  0.0 315.0 jit_solution(15052190871946827659)
XLA Ops:
  0.6 33.6 %forward.1 = (f32[2048,2048]{1,0:T(8,128)}, f32[2048,2048]{1,0:T(8,128)}, bf16[2048,2048]{1,0:T(8,128)(2,1)}, bf16[640,2048]{1,0:T(8,128)(2,1)}, bf16[640,2048]{...) custom-call(bf16[2048,640]{1,0:T(8,128)(2,1)} %bitcast.29, bf16[2048,640]{1,0:T(8,128)(2,1)} %bitcast.21, ...), custom_call_target="tpu_custom_call" | custom-call | tf_op jit(solution)/shard_map/forward/pallas_call | solution.py:90
  34.2 100.2 %backward.1 = (bf16[16,40,2048]{2,1,0:T(8,128)(2,1)}, bf16[16,40,2048]{2,1,0:T(8,128)(2,1)}, bf16[16,2,64,640]{3,2,1,0:T(8,128)(2,1)}, bf16[16,40,2048]{2,1,0:T(...) custom-call(bf16[2048,640]{1,0:T(8,128)(2,1)} %bitcast.22, ...), custom_call_target="tpu_custom_call" | custom-call | tf_op jit(solution)/shard_map/backward/pallas_call | solution.py:184
  134.5 173.6 %comm.1 = (bf16[2,16,40,2048]{3,2,1,0:T(8,128)(2,1)S(1)}, bf16[2,16,40,2048]{3,2,1,0:T(8,128)(2,1)S(1)}, bf16[2,16,2,64,640]{4,3,2,1,0:T(8,128)(2,1)S(1)}, f32[2...) custom-call(bf16[8,2,40,2048]{3,2,1,0:T(8,128)(2,1)} %bitcast.26, ...), custom_call_target="tpu_custom_call" | custom-call | tf_op jit(solution)/shard_map/comm/pallas_call | solution.py:410
  308.0 6.8 %write.1 = (bf16[2,16,40,2048]{3,2,1,0:T(8,128)(2,1)}, bf16[2,16,40,2048]{3,2,1,0:T(8,128)(2,1)}, bf16[2,16,2,64,640]{4,3,2,1,0:T(8,128)(2,1)}, f32[2,40,2048]{2...) custom-call(bf16[2,16,40,2048]{3,2,1,0:T(8,128)(2,1)S(1)} %get-tuple, ...), custom_call_target="tpu_custom_call" | custom-call | tf_op jit(solution)/shard_map/write/pallas_call | solution.py:431

commit v4 on v2

v4 whole, which is shorter than its diff:
```python
import jax
import jax.numpy as jnp
from jax import lax
from jax.experimental import pallas as pl
from jax.experimental.pallas import tpu as pltpu
from jax.sharding import PartitionSpec as P

F32, BF16 = jnp.float32, jnp.bfloat16
MESH = pl.DeviceIdType.MESH
ANY = pl.BlockSpec(memory_space=pl.ANY)
CHIPS = 8
HOPS = CHIPS - 1


def dot(a, b, dims):
    return lax.dot_general(a, b, (dims, ((), ())), preferred_element_type=F32)


def normed(h):
    wide = h.astype(F32)
    scale = lax.rsqrt(jnp.mean(wide**2, -1, keepdims=True) + 1e-6)
    return (wide * scale).astype(BF16), scale


def adamw(w, m, v, g):
    m = 0.9 * m + 0.1 * g
    v = 0.95 * v + 0.05 * g * g
    step = m * lax.rsqrt(v + 1e-8) + 0.1 * w
    return (w - 0.02 * step).astype(BF16), m, v


TILE = 512
FB = 256


def tiles(tokens):
    return [pl.ds(r, TILE) for r in range(0, tokens, TILE)]


def nn(a, b):
    return dot(a, b, ((1,), (0,)))


def nt(a, b):
    return dot(a, b, ((1,), (1,)))


def gates(a, wg, wu):
    gate, up = nn(a, wg), nn(a, wu)
    s = 0.5 + 0.5 * jnp.tanh(0.5 * gate)
    silu = gate * s
    return silu, up * (s + silu * (1 - s)), (silu * up).astype(BF16)


def forward_kernel(x, dy, wg, wu, wd, silu_out, slope_out, inner_out, at_out, dyt_out, h_out, a_out, a, acc):
    j = pl.program_id(0)
    tokens = x.shape[0]

    @pl.when(j == 0)
    def _():
        for r in tiles(tokens):
            a[r] = normed(x[r])[0]
            acc[r] = jnp.zeros((TILE, x.shape[1]), F32)

    part = pl.ds(pl.multiple_of(j * FB, FB), FB)
    at_out[...] = a[part].T
    dyt_out[...] = dy[part].T
    for r in tiles(tokens):
        silu, slope, inner = gates(a[r], wg[...], wu[...])
        silu_out[r], slope_out[r], inner_out[r] = silu, slope, inner
        acc[r] += nn(inner, wd[...])

    @pl.when(j == pl.num_programs(0) - 1)
    def _():
        for r in tiles(tokens):
            h = x[r] + acc[r].astype(BF16)
            h_out[r] = h
            a_out[r] = normed(h)[0]


def forward(x, dy, wg, wu, wd):
    tokens, d = x.shape
    steps = tokens // FB
    whole = lambda s: pl.BlockSpec(s, lambda j: (0, 0))
    cols = lambda rows: pl.BlockSpec((rows, FB), lambda j: (0, j))
    wcols = pl.BlockSpec((None, d, FB), lambda j: (0, 0, j))
    wrows = pl.BlockSpec((None, FB, d), lambda j: (0, j, 0))
    ff = wg.shape[2]
    shape = jax.ShapeDtypeStruct
    return pl.pallas_call(
        forward_kernel,
        grid=(ff // FB,),
        in_specs=[whole(x.shape), whole(x.shape), wcols, wcols, wrows],
        out_specs=[cols(tokens), cols(tokens), cols(tokens), cols(d), cols(d), whole(x.shape), whole(x.shape)],
        out_shape=[shape((tokens, ff), F32)] * 2
        + [shape((tokens, ff), BF16)]
        + [shape((d, tokens), BF16)] * 2
        + [shape(x.shape, BF16)] * 2,
        scratch_shapes=[pltpu.VMEM(x.shape, BF16), pltpu.VMEM(x.shape, F32)],
        compiler_params=pltpu.CompilerParams(vmem_limit_bytes=60 * 2**20),
        name="forward",
    )(x, dy, wg, wu, wd)


class Place:
    def __init__(self):
        self.me = lax.axis_index("dp")
        self.chip, self.core = lax.div(self.me, 2), lax.rem(self.me, 2)
        self.at = self.flip(self.chip)
        self.partner = self.chip * 2 + 1 - self.core

    @staticmethod
    def flip(c):
        half = CHIPS // 2
        return c + lax.div(c, half) * (3 * half - 1 - 2 * c)

    def chip_at(self, offset):
        return self.flip(lax.rem(self.at + offset + 2 * CHIPS, CHIPS))

    def device_at(self, offset):
        return self.chip_at(offset) * 2 + self.core


def remote(src, dst, send, recv, device):
    return pltpu.make_async_remote_copy(src, dst, send, recv, device_id={"dp": device}, device_id_type=MESH)


def greet(n):
    me = lax.axis_index("dp")
    barrier = pltpu.get_barrier_semaphore()

    @pl.loop(1, n)
    def _(j):
        pl.semaphore_signal(barrier, inc=1, device_id={"dp": lax.rem(me + j, n)}, device_id_type=MESH)

    pl.semaphore_wait(barrier, n - 1)


def wide(ref):
    return ref[...].astype(F32)


class Stream:
    def __init__(self, refs):
        self.own40, self.peer40, self.got40, self.stage40, self.own64, self.peer64, self.got64, self.stage64 = refs[:8]
        self.sq40, self.sq64 = refs[8:10]
        self.pair40_send, self.pair40_recv, self.pair64_send, self.pair64_recv = refs[10:14]
        self.ring40_send, self.ring40_recv, self.ring64_send, self.ring64_recv = refs[14:18]
        self.here = Place()

    def keep(self, step, gate, up, down):
        c, part = lax.div(step, 2), lax.rem(step, 2)
        slot = lax.rem(c, 2)
        first = self.here.core == 0
        cols = pl.ds(pl.multiple_of(part * FB, FB), FB)
        for kind, g in enumerate((gate, up)):
            g = g.reshape(CHIPS, 2, -1, FB)
            self.own40[kind, c, :, :, cols] = jnp.where(first, g[:, 0], g[:, 1]).astype(BF16)
            self.stage40[slot, kind, :, :, cols] = jnp.where(first, g[:, 1], g[:, 0]).astype(BF16)
        g = down.reshape(2, *self.own64.shape[2:])
        self.own64[c, part] = jnp.where(first, g[0], g[1]).astype(BF16)
        self.stage64[slot, part] = jnp.where(first, g[1], g[0]).astype(BF16)

    def pair40(self, kind, c):
        return remote(self.stage40.at[lax.rem(c, 2), kind], self.peer40.at[kind, c], self.pair40_send.at[kind, c], self.pair40_recv.at[kind, c], self.here.partner)

    def pair64(self, c):
        return remote(self.stage64.at[lax.rem(c, 2)], self.peer64.at[c], self.pair64_send.at[c], self.pair64_recv.at[c], self.here.partner)

    def swap(self, c):
        self.pair64(c).start()
        self.pair40(0, c).start()
        self.pair40(1, c).start()

    def swapped_out(self, c):
        self.pair64(c).wait_send()
        self.pair40(0, c).wait_send()
        self.pair40(1, c).wait_send()

    def hop40(self, kind, c, h):
        sign = 1 - 2 * kind
        q = self.here.chip_at(-sign * (1 + h))
        return remote(self.own40.at[kind, c, q], self.got40.at[kind, c, h], self.ring40_send.at[kind, c, h], self.ring40_recv.at[kind, c, h], self.here.device_at(sign))

    def hop64(self, c, part, side):
        return remote(self.own64.at[c, part, side], self.got64.at[c, part, side], self.ring64_send.at[c, part, side], self.ring64_recv.at[c, part, side], self.here.device_at(1 - 2 * side))

    def turn64(self, c, part, side):
        to = self.here.flip(lax.rem(2 * c + part, CHIPS))
        return lax.rem((1 - 2 * side) * (self.here.at - to) - 1 + 2 * CHIPS, CHIPS)

    def advance(self, c, h, g40, g64):
        layer, quarter = 1 - lax.div(c, 4), lax.rem(c, 4)
        here = self.here

        @pl.when(h == 0)
        def _():
            self.pair64(c).wait_recv()
            for kind in range(2):
                self.pair40(kind, c).wait_recv()
                q = here.chip_at(-(1 - 2 * kind))
                mine = self.own40.at[kind, c, q]
                mine[...] = (wide(mine) + wide(self.peer40.at[kind, c, q])).astype(BF16)
                self.hop40(kind, c, 0).start()

        @pl.when((h > 0) & (h < HOPS))
        def _():
            for kind in range(2):
                self.hop40(kind, c, h - 1).wait_recv()
                q = here.chip_at(-(1 - 2 * kind) * (1 + h))
                mine = self.own40.at[kind, c, q]
                mine[...] = (wide(mine) + wide(self.peer40.at[kind, c, q]) + wide(self.got40.at[kind, c, h - 1])).astype(BF16)
                self.hop40(kind, c, h).start()

        @pl.when(h == HOPS)
        def _():
            for kind in range(2):
                self.hop40(kind, c, HOPS - 1).wait_recv()
                q = here.chip
                g = (wide(self.own40.at[kind, c, q]) + wide(self.peer40.at[kind, c, q]) + wide(self.got40.at[kind, c, HOPS - 1])).astype(BF16)
                g40[kind, layer, :, pl.ds(pl.multiple_of(quarter * 2 * FB, 2 * FB), 2 * FB)] = g
                g = g.astype(F32)
                self.sq40[...] += g * g

        for part in range(2):
            for side in range(2):
                turn = self.turn64(c, part, side)
                mine, theirs, got = (r.at[c, part, side] for r in (self.own64, self.peer64, self.got64))

                @pl.when((h == turn) & (h == 0))
                def _():
                    mine[...] = (wide(mine) + wide(theirs)).astype(BF16)
                    self.hop64(c, part, side).start()

                @pl.when((h == turn) & (h > 0) & (h < HOPS))
                def _():
                    self.hop64(c, part, side).wait_recv()
                    mine[...] = (wide(mine) + wide(theirs) + wide(got)).astype(BF16)
                    self.hop64(c, part, side).start()

                @pl.when((h == turn) & (h == HOPS))
                def _():
                    self.hop64(c, part, side).wait_recv()
                    g = (wide(mine) + wide(theirs) + wide(got)).astype(BF16)
                    g64[layer, side] = g
                    g = g.astype(F32)
                    self.sq64[...] += g * g

    def tick(self, tick, g40, g64):
        @pl.loop(0, 8)
        def _(c):
            early = 1 - lax.div(lax.div(c, 3) + 2, 3)
            h = tick - (2 * c + 10 - early * (5 - 2 * c))

            @pl.when((h >= 0) & (h <= HOPS))
            def _():
                self.advance(c, h, g40, g64)

    def drain(self):
        self.swapped_out(6)
        self.swapped_out(7)

        @pl.loop(0, 8)
        def _(c):
            for kind in range(2):

                @pl.loop(0, HOPS)
                def _(h):
                    self.hop40(kind, c, h).wait_send()

            for part in range(2):
                for side in range(2):

                    @pl.when(self.turn64(c, part, side) < HOPS)
                    def _():
                        self.hop64(c, part, side).wait_send()


def backward_kernel(dy_in, a_in, h_in, dyt_in, a0t_in, wg, wu, wd, silu, slope, inner0, g40, g64, squares, *refs):
    d, a, dt, at, da, inner, dg, du, sems = refs[:9]
    stream = Stream(refs[9:])
    step = pl.program_id(0)
    half = pl.num_programs(0) // 2
    tokens = d.shape[0]

    def load(src, dst, i):
        return pltpu.make_async_copy(src, dst, sems.at[i])

    def gradients(inner):
        @pl.when((lax.rem(step, 2) == 0) & (step >= 4))
        def _():
            stream.swapped_out(lax.div(step, 2) - 2)

        stream.keep(step, nn(at[...], dg[...]), nn(at[...], du[...]), nn(dt[...], inner[...]).T)

        @pl.when(lax.rem(step, 2) == 1)
        def _():
            stream.swap(lax.div(step, 2))

    @pl.when(step == 0)
    def _():
        here = stream.here
        for device in (here.device_at(1), here.device_at(-1), here.partner):
            pl.semaphore_signal(pltpu.get_barrier_semaphore(), inc=1, device_id={"dp": device}, device_id_type=MESH)
        first = [load(dy_in, d, 0), load(a_in, a, 1), load(dyt_in, dt, 2)]
        for c in first:
            c.start()
        for r in tiles(tokens):
            da[r] = jnp.zeros((TILE, d.shape[1]), F32)
        stream.sq40[...] = jnp.zeros_like(stream.sq40)
        stream.sq64[...] = jnp.zeros_like(stream.sq64)
        for c in first:
            c.wait()
        at[...] = a[...].T

    @pl.when(step == 1)
    def _():
        pl.semaphore_wait(pltpu.get_barrier_semaphore(), 3)

    @pl.when(step < half)
    def _():
        stream.tick(2 * step, g40, g64)
        both = jnp.concatenate([wg[...], wu[...]], axis=1)
        for r in tiles(tokens):
            by_inner = nt(d[r], wd[...]).astype(BF16).astype(F32)
            silu, slope, product = gates(a[r], wg[...], wu[...])
            by_gate, by_up = (by_inner * slope).astype(BF16), (by_inner * silu).astype(BF16)
            inner[r], dg[r], du[r] = product, by_gate, by_up
            da[r] += nt(jnp.concatenate([by_gate, by_up], axis=1), both)
        stream.tick(2 * step + 1, g40, g64)

        @pl.when(step == half - 1)
        def _():
            load(h_in, a, 1).start()

        gradients(inner)

    @pl.when(step == half - 1)
    def _():
        c = load(a0t_in, at, 0)
        c.start()
        load(h_in, a, 1).wait()
        for r in tiles(tokens):
            h = a[r].astype(F32)
            scale = lax.rsqrt(jnp.mean(h**2, -1, keepdims=True) + 1e-6)
            by_a = da[r].astype(BF16).astype(F32)
            by_h = scale * by_a - h * (scale**3 * jnp.mean(by_a * h, -1, keepdims=True))
            d[r] = d[r] + by_h.astype(BF16)
        dt[...] = d[...].T
        c.wait()

    @pl.when(step >= half)
    def _():
        for r in tiles(tokens):
            by_inner = nt(d[r], wd[...]).astype(BF16).astype(F32)
            dg[r], du[r] = (by_inner * slope[r]).astype(BF16), (by_inner * silu[r]).astype(BF16)
        stream.tick(step + half, g40, g64)
        gradients(inner0)

    @pl.when(step == 2 * half - 1)
    def _():
        @pl.loop(0, CHIPS)
        def _(t):
            stream.tick(3 * half + t, g40, g64)

        stream.drain()
        total = jnp.sum(stream.sq40[...], keepdims=True) + jnp.sum(stream.sq64[...], keepdims=True)
        squares[...] = jnp.broadcast_to(total, squares.shape)


def backward(dy, a1, h1, dyt, a0t, wg, wu, wd, silu, slope, inner0):
    tokens, d = dy.shape
    ff = wg.shape[2]
    half = ff // FB
    early = lambda s: jnp.minimum(s, half - 1)
    late = lambda s: jnp.maximum(s - half, 0)
    layer = lambda s: 1 - s // half
    wcols = pl.BlockSpec((None, d, FB), lambda s: (1, 0, early(s)))
    wrows = pl.BlockSpec((None, FB, d), lambda s: (layer(s), s % half, 0))
    saved = pl.BlockSpec((tokens, FB), lambda s: (0, late(s)))
    rows, block = pltpu.VMEM((tokens, d), BF16), pltpu.VMEM((tokens, FB), BF16)
    flipped = pltpu.VMEM((d, tokens), BF16)
    dma = pltpu.SemaphoreType.DMA
    of40 = lambda *s: pltpu.VMEM((*s, 40, 2 * FB), BF16)
    of64 = lambda *s: pltpu.VMEM((*s, 2, 64, 640), BF16)
    comms = [of40(2, 8, CHIPS), of40(2, 8, CHIPS), of40(2, 8, HOPS), of40(2, 2, CHIPS)]
    comms += [of64(8, 2), of64(8, 2), of64(8, 2), of64(2, 2)]
    comms += [pltpu.VMEM((40, 2 * FB), F32), pltpu.VMEM((64, 640), F32)]
    comms += [dma((2, 8)), dma((2, 8)), dma((8,)), dma((8,)), dma((2, 8, HOPS)), dma((2, 8, HOPS)), dma((8, 2, 2)), dma((8, 2, 2))]
    return pl.pallas_call(
        backward_kernel,
        grid=(2 * half,),
        in_specs=[ANY] * 5 + [wcols, wcols, wrows, saved, saved, saved],
        out_specs=[pl.BlockSpec(memory_space=pltpu.VMEM)] * 3,
        out_shape=[pltpu.VMEM((2, 2, 40, ff), BF16), pltpu.VMEM((2, 2, 64, 640), BF16), pltpu.VMEM((8, 128), F32)],
        scratch_shapes=[rows, rows, flipped, flipped, pltpu.VMEM((tokens, d), F32), block, block, block, dma((3,))] + comms,
        compiler_params=pltpu.CompilerParams(collective_id=1, has_side_effects=True, vmem_limit_bytes=62 * 2**20),
        name="backward",
    )(dy, a1, h1, dyt, a0t, wg, wu, wd, silu, slope, inner0)


def comm_kernel(n, count, *refs):
    it = iter(refs)
    take = lambda k: [next(it) for _ in range(k)]
    g40, g64, own_squares = take(3)
    ws, ms, vs = take(3), take(3), take(3)
    w_out, m_out, v_out = take(3), take(3), take(3)
    w40, w64, m40, m64, v40, v64, squares, local_sem = take(8)
    sq_send, sq_recv, gat_send, gat_recv, cross_send, cross_recv = take(6)

    here = Place()
    me, core = here.me, here.core
    streams = [(layer, kind) for kind in range(4) for layer in (1, 0)]
    sign = lambda kind: 1 - 2 * (kind % 2)
    loads = []

    def load(src, dst):
        c = pltpu.make_async_copy(src, dst, local_sem.at[len(loads)])
        c.start()
        loads.append(c)

    for side, x40, x64, per in ((ws, w40, w64, True), (ms, m40, m64, False), (vs, v40, v64, False)):
        for i in range(2):
            load(side[i].at[:, me] if per else side[i], x40.at[i])
        load(side[2].at[:, me] if per else side[2], x64)

    greet(n)
    squares[me] = own_squares[...]

    def tell(j):
        return remote(squares.at[me], squares.at[me], sq_send.at[j], sq_recv.at[me], lax.rem(me + j, n))

    def told(j):
        o = lax.rem(me + n - j, n)
        return remote(squares.at[o], squares.at[o], sq_send.at[j], sq_recv.at[o], o)

    @pl.loop(1, n)
    def _(j):
        tell(j).start()

    for c in loads:
        c.wait()

    @pl.loop(1, n)
    def _(j):
        told(j).wait_recv()

    total = jnp.sum(squares[...], axis=0)[:1, :1]
    factor = jnp.minimum(1.0, 0.5 * lax.rsqrt(total / count + 1e-30))

    def whole(layer, kind, owner):
        return w_out[kind].at[layer, owner] if kind < 2 else w_out[2].at[layer, owner, kind - 2]

    def pass_on(i, layer, kind, t):
        o = here.device_at(-sign(kind) * t)
        block = whole(layer, kind, o)
        return remote(block, block, gat_send.at[i, t], gat_recv.at[i, t], here.device_at(sign(kind)))

    def across(i, layer, kind, t):
        o = here.device_at(-sign(kind) * t)
        block = whole(layer, kind, o)
        return remote(block, block, cross_send.at[i, t], cross_recv.at[i, t], here.partner)

    def across_in(i, layer, kind, t):
        o = here.chip_at(-sign(kind) * t) * 2 + 1 - core
        block = whole(layer, kind, o)
        return remote(block, block, cross_send.at[i, t], cross_recv.at[i, t], here.partner)

    for i, (layer, kind) in enumerate(streams):
        sel = (lambda r40, r64: r40.at[kind, layer] if kind < 2 else r64.at[layer, kind - 2])
        out = (lambda r: r[kind].at[layer] if kind < 2 else r[2].at[layer, kind - 2])
        g = wide(g40.at[kind, layer] if kind < 2 else g64.at[layer, kind - 2]) * factor
        w, m, v = adamw(wide(sel(w40, w64)), sel(m40, m64)[...], sel(v40, v64)[...], g)
        whole(layer, kind, me)[...] = w
        pass_on(i, layer, kind, 0).start()
        across(i, layer, kind, 0).start()
        out(m_out)[...] = m
        out(v_out)[...] = v

    @pl.loop(1, HOPS)
    def _(t):
        for i, (layer, kind) in enumerate(streams):
            pass_on(i, layer, kind, t - 1).wait_recv()
            pass_on(i, layer, kind, t).start()
            across(i, layer, kind, t).start()

    for i, (layer, kind) in enumerate(streams):
        pass_on(i, layer, kind, HOPS - 1).wait_recv()
        across(i, layer, kind, HOPS).start()

    @pl.loop(0, HOPS)
    def _(t):
        for i, (layer, kind) in enumerate(streams):
            pass_on(i, layer, kind, t).wait_send()

    @pl.loop(1, n)
    def _(j):
        tell(j).wait_send()

    @pl.loop(0, CHIPS)
    def _(t):
        for i, (layer, kind) in enumerate(streams):
            across(i, layer, kind, t).wait_send()
            across_in(i, layer, kind, t).wait_recv()


def comm(n, count, grads, ws, ms, vs):
    dma = pltpu.SemaphoreType.DMA
    scratch = [pltpu.VMEM((2, 2, 40, 2048), BF16), pltpu.VMEM((2, 2, 64, 640), BF16)]
    scratch += [pltpu.VMEM((2, 2, 40, 2048), F32), pltpu.VMEM((2, 2, 64, 640), F32)] * 2
    scratch += [pltpu.VMEM((n, 8, 128), F32), dma((9,)), dma((n,)), dma((n,))]
    scratch += [dma((8, HOPS)), dma((8, HOPS)), dma((8, CHIPS)), dma((8, CHIPS))]
    out_shape = [pltpu.VMEM((2, n, 40, 2048), BF16)] * 2 + [pltpu.VMEM((2, n, 2, 64, 640), BF16)]
    out_shape += ([pltpu.VMEM((2, 40, 2048), F32)] * 2 + [pltpu.VMEM((2, 2, 64, 640), F32)]) * 2
    return pl.pallas_call(
        lambda *refs: comm_kernel(n, count, *refs),
        out_shape=out_shape,
        in_specs=[pl.BlockSpec(memory_space=pltpu.VMEM)] * 3 + [ANY] * 9,
        out_specs=[pl.BlockSpec(memory_space=pltpu.VMEM)] * 9,
        scratch_shapes=scratch,
        compiler_params=pltpu.CompilerParams(collective_id=0, has_side_effects=True, vmem_limit_bytes=16 * 2**20),
        name="comm",
    )(*grads, *ws, *ms, *vs)


def write_kernel(*refs):
    k = (len(refs) - 1) // 2
    copies = [pltpu.make_async_copy(refs[i], refs[k + i], refs[-1].at[i]) for i in range(k)]
    for c in copies:
        c.start()
    for c in copies:
        c.wait()


def write(arrays):
    return pl.pallas_call(
        write_kernel,
        out_shape=[jax.ShapeDtypeStruct(a.shape, a.dtype) for a in arrays],
        in_specs=[pl.BlockSpec(memory_space=pltpu.VMEM)] * len(arrays),
        out_specs=[ANY] * len(arrays),
        scratch_shapes=[pltpu.SemaphoreType.DMA((len(arrays),))],
        compiler_params=pltpu.CompilerParams(vmem_limit_bytes=2**20),
        name="write",
    )(*arrays)


def solution(mesh):
    n = mesh.shape["dp"]

    def body(x, dy, wg, wu, wd, mg, mu, md, vg, vu, vd):
        x, dy = x[0], dy[0]
        silu, slope, inner0, a0t, dyt, h1, a1 = forward(x, dy, wg, wu, wd)
        grads = backward(dy, a1, h1, dyt, a0t, wg, wu, wd, silu, slope, inner0)
        rows = lambda w: w.reshape(2, n, 40, 2048)
        ws = [rows(wg), rows(wu), wd.reshape(2, n, 2, 64, 640)]
        split = lambda t: t.reshape(2, 2, 64, 640)
        count = wg.size + wu.size + wd.size
        outs = write(comm(n, count, grads, ws, [mg, mu, split(md)], [vg, vu, split(vd)]))
        shapes = [wg, wu, wd, mg, mu, md, vg, vu, vd]
        return tuple(o.reshape(s.shape) for o, s in zip(outs, shapes, strict=True))

    whole, mine = P(), P(None, "dp", None)
    seq, out = P(("rep", "dp")), P("rep", "dp", None)
    return jax.shard_map(
        body,
        mesh=mesh,
        in_specs=(seq, seq) + (whole,) * 3 + (mine,) * 6,
        out_specs=(P("rep"),) * 3 + (out,) * 6,
        check_vma=False,
    )
```

time: 400 us -> 314 us (0.79); the launches traced: 393 us -> 314 us
  matrix products: 200 us -> 0 us
  Pallas kernels: 180 us -> 302 us
  other arithmetic: 4.96 us -> 0 us
  local copies, waits for them, and re-layouts: 6.06 us -> 10.4 us
    pallas_call x0 -> x2, Pallas kernels: none -> 205 us  [the longest x1 172 us: backward(): pl.pallas_call(backward_kernel, grid=(2 * half,), in_specs=[ANY] * 5 + [w...]
    dot_general x15 -> x0, matrix products: 200 us -> none  [dot(): return lax.dot_general(a, b, (dims, ((), ())), preferred_element_type=F32)]
    pallas_call x1, Pallas kernels: 173 us -> 90.5 us  [comm(): pl.pallas_call(lambda *refs: comm_kernel(n, count, *refs), out_shape=out_...]
    add x1 -> x0, other arithmetic: 4.38 us -> none  [body(): dy + (s1 * da - h * (s1 ** 3 * jnp.mean(da * h, -1, keepdims=True))).asty...]
    unnamed x34 -> x16, local copies, waits for them, and re-layouts: 6.06 us -> 10.4 us
where the time goes in v4:
time: 314 us
  Pallas kernels  302 us (96%)
  local copies, waits for them, and re-layouts  10.4 us (3%)
    pallas_call x1, Pallas kernels, backward(): pl.pallas_call(backward_kernel, grid=(2 * half,), in_specs=[ANY] * 5 + [w...  172 us
    pallas_call x1, Pallas kernels, comm(): pl.pallas_call(lambda *refs: comm_kernel(n, count, *refs), out_shape=out_...  90.5 us
    pallas_call x1, Pallas kernels, forward(): pl.pallas_call(forward_kernel, grid=(ff // FB,), in_specs=[whole(x.shape)...  33.6 us
    unnamed x16, local copies, waits for them, and re-layouts  10.4 us
    pallas_call x1, Pallas kernels, write(): pl.pallas_call(write_kernel, out_shape=[jax.ShapeDtypeStruct(a.shape, a.d...  6.79 us

profile of v4, /device:TPU:0, one launch (start us, length us, event | category | flops | bytes accessed | tf_op | source)
XLA Modules:
  0.0 313.7 jit_solution(9787060501543227571)
XLA Ops:
  0.6 33.6 %forward.1 = (f32[2048,2048]{1,0:T(8,128)}, f32[2048,2048]{1,0:T(8,128)}, bf16[2048,2048]{1,0:T(8,128)(2,1)}, bf16[640,2048]{1,0:T(8,128)(2,1)}, bf16[640,2048]{...) custom-call(bf16[2048,640]{1,0:T(8,128)(2,1)} %bitcast.19, bf16[2048,640]{1,0:T(8,128)(2,1)} %bitcast.17, ...), custom_call_target="tpu_custom_call" | custom-call | tf_op jit(solution)/shard_map/forward/pallas_call | solution.py:90
  34.2 0.0 copy-start.2
  34.2 171.6 %backward.1 = (bf16[2,2,40,2048]{3,2,1,0:T(8,128)(2,1)S(1)}, bf16[2,2,64,640]{3,2,1,0:T(8,128)(2,1)S(1)}, f32[8,128]{1,0:T(8,128)S(1)}) custom-call(bf16[2048,640]{1,0:T(8,128)(2,1)} %bitcast.18, bf16[2048,640]{1,0:T(8,128)(2,1)} %get-tuple-element.37.a_in, bf16[2048,640]{1,0:T(8,128)(2,1)} %get-tuple-element.38.h_in, ...), custom_call_target="tpu_custom_call" | custom-call | tf_op jit(solution)/shard_map/backward/pallas_call | solution.py:390
  205.9 0.0 copy-done.2
  205.9 0.0 copy-start
  205.9 2.5 copy-done
  208.4 0.0 copy-start.1
  208.4 2.5 copy-done.1
  210.9 0.0 copy-start.3
  210.9 1.1 copy-done.3
  211.9 0.0 copy-start.4
  212.0 1.1 copy-done.4
  213.0 0.0 copy-start.5
  213.0 1.1 copy-done.5
  214.1 0.0 copy-start.6
  214.1 1.1 copy-done.6
  215.2 0.0 copy-start.7
  215.2 1.1 copy-done.7
  216.3 90.5 %comm.1 = (bf16[2,16,40,2048]{3,2,1,0:T(8,128)(2,1)S(1)}, bf16[2,16,40,2048]{3,2,1,0:T(8,128)(2,1)S(1)}, bf16[2,16,2,64,640]{4,3,2,1,0:T(8,128)(2,1)S(1)}, f32[2...) custom-call(bf16[2,2,40,2048]{3,2,1,0:T(8,128)(2,1)S(1)} %get-tuple-, ...), custom_call_target="tpu_custom_call" | custom-call | tf_op jit(solution)/shard_map/comm/pallas_call | solution.py:515
  306.8 6.8 %write.1 = (bf16[2,16,40,2048]{3,2,1,0:T(8,128)(2,1)}, bf16[2,16,40,2048]{3,2,1,0:T(8,128)(2,1)}, bf16[2,16,2,64,640]{4,3,2,1,0:T(8,128)(2,1)}, f32[2,40,2048]{2...) custom-call(bf16[2,16,40,2048]{3,2,1,0:T(8,128)(2,1)S(1)} %get-tuple, ...), custom_call_target="tpu_custom_call" | custom-call | tf_op jit(solution)/shard_map/write/pallas_call | solution.py:536
Async XLA Ops:
  34.2 171.6 %copy-start.2 = (f32[2,40,2048]{2,1,0:T(8,128)S(1)}, f32[2,40,2048]{2,1,0:T(8,128)}, u32[]{:S(2)}) copy-start(f32[2,40,2048]{2,1,0:T(8,128)} %refs_6_.1) | copy-start | bytes 1966084
  205.9 2.5 copy-start
  208.4 2.5 copy-start.1
  210.9 1.1 copy-start.3
  211.9 1.1 copy-start.4
  213.0 1.1 copy-start.5
  214.1 1.1 copy-start.6
  215.2 1.1 copy-start.7

commit v5 on v4

v5 whole, which is shorter than its diff:
```python
import jax
import jax.numpy as jnp
from jax import lax
from jax.experimental import pallas as pl
from jax.experimental.pallas import tpu as pltpu
from jax.sharding import PartitionSpec as P

F32, BF16 = jnp.float32, jnp.bfloat16
MESH = pl.DeviceIdType.MESH
ANY = pl.BlockSpec(memory_space=pl.ANY)
CHIPS = 8
HOPS = CHIPS - 1


def dot(a, b, dims):
    return lax.dot_general(a, b, (dims, ((), ())), preferred_element_type=F32)


def normed(h):
    wide = h.astype(F32)
    scale = lax.rsqrt(jnp.mean(wide**2, -1, keepdims=True) + 1e-6)
    return (wide * scale).astype(BF16), scale


def adamw(w, m, v, g):
    m = 0.9 * m + 0.1 * g
    v = 0.95 * v + 0.05 * g * g
    step = m * lax.rsqrt(v + 1e-8) + 0.1 * w
    return (w - 0.02 * step).astype(BF16), m, v


TILE = 512
FB = 256
WIDE = 512
LAST = 1
ROW = 4
MIB = 2**20


def tiles(tokens):
    return [pl.ds(r, TILE) for r in range(0, tokens, TILE)]


def nn(a, b):
    return dot(a, b, ((1,), (0,)))


def nt(a, b):
    return dot(a, b, ((1,), (1,)))


def gates(a, wg, wu):
    gate, up = nn(a, wg), nn(a, wu)
    s = 0.5 + 0.5 * jnp.tanh(0.5 * gate)
    silu = gate * s
    return silu, up * (s + silu * (1 - s)), (silu * up).astype(BF16)


def forward_kernel(x, dy, wg, wu, wd, silu_out, slope_out, inner_out, at_out, dyt_out, h_out, a_out, a, acc):
    j = pl.program_id(0)
    tokens = x.shape[0]

    @pl.when(j == 0)
    def _():
        for r in tiles(tokens):
            a[r] = normed(x[r])[0]
            acc[r] = jnp.zeros((TILE, x.shape[1]), F32)

    part = pl.ds(pl.multiple_of(j * WIDE, WIDE), WIDE)
    at_out[...] = a[part].T
    dyt_out[...] = dy[part].T
    for r in tiles(tokens):
        silu, slope, inner = gates(a[r], wg[...], wu[...])
        silu_out[r], slope_out[r], inner_out[r] = silu, slope, inner
        acc[r] += nn(inner, wd[...])

    @pl.when(j == pl.num_programs(0) - 1)
    def _():
        for r in tiles(tokens):
            h = x[r] + acc[r].astype(BF16)
            h_out[r] = h
            a_out[r] = normed(h)[0]


def forward(x, dy, wg, wu, wd):
    tokens, d = x.shape
    whole = lambda s: pl.BlockSpec(s, lambda j: (0, 0))
    cols = lambda rows: pl.BlockSpec((rows, WIDE), lambda j: (0, j))
    wcols = pl.BlockSpec((None, d, WIDE), lambda j: (0, 0, j))
    wrows = pl.BlockSpec((None, WIDE, d), lambda j: (0, j, 0))
    ff = wg.shape[2]
    shape = jax.ShapeDtypeStruct
    return pl.pallas_call(
        forward_kernel,
        grid=(ff // WIDE,),
        in_specs=[whole(x.shape), whole(x.shape), wcols, wcols, wrows],
        out_specs=[cols(tokens), cols(tokens), cols(tokens), cols(d), cols(d), whole(x.shape), whole(x.shape)],
        out_shape=[shape((tokens, ff), F32)] * 2
        + [shape((tokens, ff), BF16)]
        + [shape((d, tokens), BF16)] * 2
        + [shape(x.shape, BF16)] * 2,
        scratch_shapes=[pltpu.VMEM(x.shape, BF16), pltpu.VMEM(x.shape, F32)],
        compiler_params=pltpu.CompilerParams(vmem_limit_bytes=60 * MIB),
        name="forward",
    )(x, dy, wg, wu, wd)


class Place:
    def __init__(self):
        self.me = lax.axis_index("dp")
        self.chip, self.core = lax.div(self.me, 2), lax.rem(self.me, 2)
        self.at = self.flip(self.chip)
        self.partner = self.chip * 2 + 1 - self.core

    @staticmethod
    def flip(c):
        half = CHIPS // 2
        return c + lax.div(c, half) * (3 * half - 1 - 2 * c)

    def chip_at(self, offset):
        return self.flip(lax.rem(self.at + offset + 2 * CHIPS, CHIPS))

    def device_at(self, offset):
        return self.chip_at(offset) * 2 + self.core


def remote(src, dst, send, recv, device):
    return pltpu.make_async_remote_copy(src, dst, send, recv, device_id={"dp": device}, device_id_type=MESH)


def greet(n):
    me = lax.axis_index("dp")
    barrier = pltpu.get_barrier_semaphore()

    @pl.loop(1, n)
    def _(j):
        pl.semaphore_signal(barrier, inc=1, device_id={"dp": lax.rem(me + j, n)}, device_id_type=MESH)

    pl.semaphore_wait(barrier, n - 1)


def wide(ref):
    return ref[...].astype(F32)


class Stream:
    def __init__(self, refs):
        self.own40, self.peer40, self.across40, self.along40, self.stage40 = refs[:5]
        self.own64, self.peer64, self.across64, self.along64, self.stage64 = refs[5:10]
        self.sq40, self.sq64, self.both64 = refs[10:13]
        self.sems = dict(zip(("pair40", "pair64", "y40", "y64", "z40", "z64", "far40", "far64"), zip(refs[13::2], refs[14::2])))
        self.me = lax.axis_index("dp")
        self.chip, self.core = lax.div(self.me, 2), lax.rem(self.me, 2)
        self.y, self.z = lax.div(self.chip, ROW), lax.rem(self.chip, ROW)
        self.partner = self.device(self.y, self.z, 1 - self.core)
        self.facing = self.device(1 - self.y, self.z, self.core)
        self.mate_z = self.z + 1 - 2 * lax.rem(self.z, 2)
        self.mate, self.far = self.device(self.y, self.mate_z, self.core), self.device(self.y, 3 - self.z, self.core)

    @staticmethod
    def device(y, z, core):
        return (y * ROW + z) * 2 + core

    def copy(self, name, src, dst, send, recv, device):
        out, into = self.sems[name]
        return remote(src, dst, out.at[send], into.at[recv], device)

    def keep40(self, c, part, gate, up):
        first = self.core == 0
        cols = pl.ds(pl.multiple_of(part * FB, FB), FB)
        for kind, g in enumerate((gate, up)):
            g = g.reshape(CHIPS, 2, -1, FB)
            self.own40[c, :, kind, :, cols] = jnp.where(first, g[:, 0], g[:, 1]).astype(BF16)
            self.stage40[lax.rem(c, 2), :, kind, :, cols] = jnp.where(first, g[:, 1], g[:, 0]).astype(BF16)

    def keep64(self, c, part, down):
        first = self.core == 0
        g = down.reshape(2, *self.own64.shape[2:])
        self.own64[c, part] = jnp.where(first, g[0], g[1]).astype(BF16)
        self.stage64[lax.rem(c, 2), part] = jnp.where(first, g[1], g[0]).astype(BF16)

    def pair40(self, c):
        return self.copy("pair40", self.stage40.at[lax.rem(c, 2)], self.peer40.at[c], c, c, self.partner)

    def pair64(self, c):
        return self.copy("pair64", self.stage64.at[lax.rem(c, 2)], self.peer64.at[c], c, c, self.partner)

    def y40(self, c):
        return self.copy("y40", self.own40.at[c, pl.ds((1 - self.y) * ROW, 4)], self.across40.at[c], c, c, self.facing)

    def y64(self, c):
        return self.copy("y64", self.own64.at[c, 1 - self.y], self.across64.at[c], c, c, self.facing)

    def z40(self, c, i):
        to = (self.mate_z, 3 - self.mate_z)[i]
        return self.copy("z40", self.own40.at[c, self.y * ROW + to], self.along40.at[c, i], (c, i), (c, i), self.mate)

    def far40(self, c):
        return self.copy("far40", self.own40.at[c, self.y * ROW + 3 - self.z], self.along40.at[c, 2], c, c, self.far)

    def z64(self, c, i):
        return self.copy("z64", self.own64.at[c, self.y], self.along64.at[i], (0, i), (0, i), self.mate)

    def far64(self, c):
        return self.copy("far64", self.own64.at[c, self.y], self.along64.at[2], 0, 0, self.far)

    def first_copy(self, c, i):
        at = (LAST, i)
        return self.copy("z64", self.own64.at[c], self.both64.at[i], at, at, self.mate)

    def second_copy(self, c):
        return self.copy("far64", self.own64.at[c], self.both64.at[2], LAST, LAST, self.far)

    def pair_sum(self, c, row):
        return wide(self.own64.at[c, row]) + wide(self.peer64.at[c, row])

    def row_sum(self, c, row):
        return self.pair_sum(c, row) + wide(self.both64.at[0, row]) + wide(self.both64.at[2, row])

    def first64(self, c):
        self.pair64(c).wait_recv()
        for i, owner in enumerate((self.mate_z, 3 - self.mate_z)):

            @pl.when(owner == lax.rem(c, ROW))
            def _():
                for row in range(2):
                    self.own64[c, row] = self.pair_sum(c, row).astype(BF16)
                self.first_copy(c, i).start()

    def second64(self, c):
        @pl.when(3 - self.z == lax.rem(c, ROW))
        def _():
            self.first_copy(c, 1).wait_recv()
            for row in range(2):
                self.own64[c, row] = (self.pair_sum(c, row) + wide(self.both64.at[1, row])).astype(BF16)
            self.second_copy(c).start()

    def third64(self):
        c = ROW + self.z
        self.first_copy(c, 0).wait_recv()
        self.second_copy(c).wait_recv()
        self.own64[c, 1 - self.y] = self.row_sum(c, 1 - self.y).astype(BF16)
        self.y64(c).start()

    def last64(self, g64):
        c = ROW + self.z
        self.y64(c).wait_recv()
        total = (self.row_sum(c, self.y) + wide(self.across64.at[c])).astype(BF16)
        g64[0] = total
        total = total.astype(F32)
        self.sq64[...] += total * total

    def over40(self, c):
        self.pair40(c).wait_recv()

        @pl.loop(0, ROW)
        def _(z):
            q = (1 - self.y) * ROW + z
            mine = self.own40.at[c, q]
            mine[...] = (wide(mine) + wide(self.peer40.at[c, q])).astype(BF16)

        self.y40(c).start()

    def over64(self, c):
        self.pair64(c).wait_recv()
        mine = self.own64.at[c, 1 - self.y]
        mine[...] = (wide(mine) + wide(self.peer64.at[c, 1 - self.y])).astype(BF16)
        self.y64(c).start()

    def sum40(self, c, z):
        q = self.y * ROW + z
        return wide(self.own40.at[c, q]) + wide(self.peer40.at[c, q]) + wide(self.across40.at[c, z])

    def sum64(self, c):
        return wide(self.own64.at[c, self.y]) + wide(self.peer64.at[c, self.y]) + wide(self.across64.at[c])

    def on40(self, c):
        self.y40(c).wait_recv()
        for i, to in enumerate((self.mate_z, 3 - self.mate_z)):
            self.own40[c, self.y * ROW + to] = self.sum40(c, to).astype(BF16)
            self.z40(c, i).start()

    def on64(self, c):
        self.y64(c).wait_recv()
        for i, owner in enumerate((self.mate_z, 3 - self.mate_z)):

            @pl.when(owner == lax.rem(c, ROW))
            def _():
                self.own64[c, self.y] = self.sum64(c).astype(BF16)
                self.z64(c, i).start()

    def out40(self, c):
        self.z40(c, 1).wait_recv()
        to = 3 - self.z
        self.own40[c, self.y * ROW + to] = (self.sum40(c, to) + wide(self.along40.at[c, 1])).astype(BF16)
        self.far40(c).start()

    def out64(self, c):
        @pl.when(3 - self.z == lax.rem(c, ROW))
        def _():
            self.z64(c, 1).wait_recv()
            self.own64[c, self.y] = (self.sum64(c) + wide(self.along64.at[1])).astype(BF16)
            self.far64(c).start()

    def end40(self, c, g40):
        self.z40(c, 0).wait_recv()
        self.far40(c).wait_recv()
        total = (self.sum40(c, self.z) + wide(self.along40.at[c, 0]) + wide(self.along40.at[c, 2])).astype(BF16)
        for part in range(2):
            cols = pl.ds(pl.multiple_of((lax.rem(c, ROW) + 4 * part) * FB, FB), FB)
            g40[:, 1 - lax.div(c, ROW), :, cols] = total[:, :, part * FB : (part + 1) * FB]
        total = total.astype(F32)
        self.sq40[...] += total * total

    def end64(self, c, g64):
        @pl.when(self.z == lax.rem(c, ROW))
        def _():
            self.z64(c, 0).wait_recv()
            self.far64(c).wait_recv()
            total = (self.sum64(c) + wide(self.along64.at[0]) + wide(self.along64.at[2])).astype(BF16)
            g64[1] = total
            total = total.astype(F32)
            self.sq64[...] += total * total

    def drain(self):
        for c in (6, 7):
            self.pair40(c).wait_send()
            self.pair64(c).wait_send()

        @pl.loop(0, 8)
        def _(c):
            self.far40(c).wait_send()
            self.y40(c).wait_send()
            for i in range(2):
                self.z40(c, i).wait_send()

        @pl.loop(0, ROW)
        def _(c):
            self.y64(c).wait_send()

        self.y64(ROW + self.z).wait_send()
        self.far64(0).wait_send()
        self.second_copy(4).wait_send()
        for i in range(2):
            self.z64(0, i).wait_send()
            self.first_copy(4, i).wait_send()


def backward_kernel(dy_in, a_in, h_in, dyt_in, a0t_in, wg, wu, wd, silu, slope, inner0, g40, g64, squares, *refs):
    d, a, dt, at, da, inner, dg, du, sems = refs[:9]
    stream = Stream(refs[9:])
    step = pl.program_id(0)
    half = pl.num_programs(0) // 3
    tokens = d.shape[0]

    def load(src, dst, i):
        return pltpu.make_async_copy(src, dst, sems.at[i])

    part, block = lax.rem(step, 2), lax.rem(lax.div(step, 2), 4)

    def gate_up(c):
        @pl.when((part == 0) & (c >= 2))
        def _():
            stream.pair40(c - 2).wait_send()

        stream.keep40(c, part, nn(at[...], dg[...]), nn(at[...], du[...]))

        @pl.when(part == 1)
        def _():
            stream.pair40(c).start()

    def down(c, inner):
        @pl.when((part == 0) & (c >= 2))
        def _():
            stream.pair64(c - 2).wait_send()

        stream.keep64(c, part, nn(dt[...], inner[...]).T)

        @pl.when(part == 1)
        def _():
            stream.pair64(c).start()

    @pl.when(step == 0)
    def _():
        for device in (stream.mate, stream.far, stream.partner, stream.facing):
            pl.semaphore_signal(pltpu.get_barrier_semaphore(), inc=1, device_id={"dp": device}, device_id_type=MESH)
        first = [load(dy_in, d, 0), load(a_in, a, 1), load(dyt_in, dt, 2)]
        for c in first:
            c.start()
        for r in tiles(tokens):
            da[r] = jnp.zeros((TILE, d.shape[1]), F32)
        stream.sq40[...] = jnp.zeros_like(stream.sq40)
        stream.sq64[...] = jnp.zeros_like(stream.sq64)
        for c in first:
            c.wait()
        at[...] = a[...].T

    @pl.when(step == 1)
    def _():
        pl.semaphore_wait(pltpu.get_barrier_semaphore(), 4)

    @pl.when(step < half)
    def _():
        both = jnp.concatenate([wg[...], wu[...]], axis=1)
        for r in tiles(tokens):
            by_inner = nt(d[r], wd[...]).astype(BF16).astype(F32)
            silu, slope, product = gates(a[r], wg[...], wu[...])
            by_gate, by_up = (by_inner * slope).astype(BF16), (by_inner * silu).astype(BF16)
            inner[r], dg[r], du[r] = product, by_gate, by_up
            da[r] += nt(jnp.concatenate([by_gate, by_up], axis=1), both)
        c = lax.div(step, 2) - 1

        @pl.when((part == 0) & (c >= 0))
        def _():
            stream.over64(c)
            stream.over40(c)

        @pl.when((part == 1) & (c >= 0))
        def _():
            stream.on64(c)
            stream.on40(c)

        @pl.when((part == 0) & (c >= 1))
        def _():
            stream.out64(c - 1)
            stream.out40(c - 1)

        @pl.when((part == 0) & (c >= 2))
        def _():
            stream.end64(c - 2, g64)
            stream.end40(c - 2, g40)

        @pl.when(step == half - 1)
        def _():
            load(h_in, a, 1).start()

        down(block, inner)
        gate_up(block)

    @pl.when(step == half - 1)
    def _():
        c = load(a0t_in, at, 0)
        c.start()
        load(h_in, a, 1).wait()
        for r in tiles(tokens):
            h = a[r].astype(F32)
            scale = lax.rsqrt(jnp.mean(h**2, -1, keepdims=True) + 1e-6)
            by_a = da[r].astype(BF16).astype(F32)
            by_h = scale * by_a - h * (scale**3 * jnp.mean(by_a * h, -1, keepdims=True))
            d[r] = d[r] + by_h.astype(BF16)
        dt[...] = d[...].T
        c.wait()

    @pl.when((step >= half) & (step < 2 * half))
    def _():
        @pl.when(step == half)
        def _():
            stream.out64(2)
            stream.out40(2)

        @pl.when(step == half + 1)
        def _():
            stream.over64(3)
            stream.over40(3)

        @pl.when(step == half + 2)
        def _():
            stream.end64(1, g64)
            stream.end40(1, g40)

        @pl.when((part == 1) & (block >= 1))
        def _():
            stream.first64(3 + block)

        @pl.when(step == half + 5)
        def _():
            stream.on64(3)
            stream.on40(3)

        down(ROW + block, inner0)

    @pl.when(step >= 2 * half)
    def _():
        for r in tiles(tokens):
            by_inner = nt(d[r], wd[...]).astype(BF16).astype(F32)
            dg[r], du[r] = (by_inner * slope[r]).astype(BF16), (by_inner * silu[r]).astype(BF16)

        @pl.when(step == 2 * half)
        def _():
            stream.first64(7)
            stream.end64(2, g64)
            stream.end40(2, g40)

        @pl.when((block >= 1) & (part == 0))
        def _():
            stream.over40(3 + block)

        @pl.when(step == 2 * half + 1)
        def _():
            stream.out64(3)
            stream.out40(3)

        @pl.when((step > 2 * half + 2) & (step <= 2 * half + 6))
        def _():
            stream.second64(1 + step - 2 * half)

        @pl.when(step == 2 * half + 5)
        def _():
            stream.end64(3, g64)
            stream.end40(3, g40)

        @pl.when((block >= 2) & (part == 1))
        def _():
            stream.on40(2 + block)

        gate_up(ROW + block)

    @pl.when(step == 3 * half - 1)
    def _():
        stream.over40(7)
        stream.out40(4)
        stream.on40(6)

        stream.third64()
        stream.out40(5)
        stream.end40(4, g40)
        stream.on40(7)
        stream.out40(6)
        stream.end40(5, g40)
        stream.last64(g64)
        stream.out40(7)
        stream.end40(6, g40)
        stream.end40(7, g40)
        stream.drain()
        total = jnp.sum(jnp.sum(stream.sq40[...], axis=0), keepdims=True) + jnp.sum(stream.sq64[...], keepdims=True)
        squares[...] = jnp.broadcast_to(total, squares.shape)


def backward(dy, a1, h1, dyt, a0t, wg, wu, wd, silu, slope, inner0):
    tokens, d = dy.shape
    ff = wg.shape[2]
    half = ff // FB
    early = lambda s: jnp.minimum(s, half - 1)
    late = lambda s: jnp.maximum(s - 2 * half, 0)
    middle = lambda s: jnp.clip(s - half, 0, half - 1)
    turn = lambda s: s // 2 + half // 2 * (s % 2)
    wcols = pl.BlockSpec((None, d, FB), lambda s: (1, 0, turn(early(s))))
    wrows = pl.BlockSpec((None, FB, d), lambda s: (1 - jnp.minimum(s // half, 1), turn(jnp.where(s < half, s, late(s))), 0))
    saved = pl.BlockSpec((tokens, FB), lambda s: (0, turn(late(s))))
    product = pl.BlockSpec((tokens, FB), lambda s: (0, turn(middle(s))))
    rows, block = pltpu.VMEM((tokens, d), BF16), pltpu.VMEM((tokens, FB), BF16)
    flipped = pltpu.VMEM((d, tokens), BF16)
    dma = pltpu.SemaphoreType.DMA
    of40 = lambda *s: pltpu.VMEM((*s, 2, 40, 2 * FB), BF16)
    of64 = lambda *s: pltpu.VMEM((*s, 128, 640), BF16)
    comms = [of40(8, CHIPS), of40(8, CHIPS), of40(8, 4), of40(8, 3), of40(2, CHIPS)]
    comms += [of64(8, 2), of64(8, 2), of64(8), of64(3), of64(2, 2)]
    comms += [pltpu.VMEM((2, 40, 2 * FB), F32), pltpu.VMEM((128, 640), F32), of64(3, 2)]
    comms += [dma((8,))] * 8 + [dma((8, 2))] * 2 + [dma((2, 2))] * 2 + [dma((8,))] * 2 + [dma((2,))] * 2
    return pl.pallas_call(
        backward_kernel,
        grid=(3 * half,),
        in_specs=[ANY] * 5 + [wcols, wcols, wrows, saved, saved, product],
        out_specs=[pl.BlockSpec(memory_space=pltpu.VMEM)] * 3,
        out_shape=[pltpu.VMEM((2, 2, 40, ff), BF16), pltpu.VMEM((2, 128, 640), BF16), pltpu.VMEM((8, 128), F32)],
        scratch_shapes=[rows, rows, flipped, flipped, pltpu.VMEM((tokens, d), F32), block, block, block, dma((3,))] + comms,
        compiler_params=pltpu.CompilerParams(collective_id=1, has_side_effects=True, vmem_limit_bytes=62 * MIB),
        name="backward",
    )(dy, a1, h1, dyt, a0t, wg, wu, wd, silu, slope, inner0)


def comm_kernel(n, count, *refs):
    it = iter(refs)
    take = lambda k: [next(it) for _ in range(k)]
    g40, g64, own_squares = take(3)
    ws, ms, vs = take(3), take(3), take(3)
    w_out, m_out, v_out = take(3), take(3), take(3)
    w40, w64, m40, m64, v40, v64, squares, local_sem = take(8)
    sq_send, sq_recv, gat_send, gat_recv, cross_send, cross_recv = take(6)

    here = Place()
    me, core = here.me, here.core
    streams = [(layer, kind) for kind in range(4) for layer in (1, 0)]
    sign = lambda kind: 1 - 2 * (kind % 2)
    loads = []

    def load(src, dst):
        c = pltpu.make_async_copy(src, dst, local_sem.at[len(loads)])
        c.start()
        loads.append(c)

    for side, x40, x64, per in ((ws, w40, w64, True), (ms, m40, m64, False), (vs, v40, v64, False)):
        for i in range(2):
            load(side[i].at[:, me] if per else side[i], x40.at[i])
        load(side[2].at[:, me] if per else side[2], x64)

    greet(n)
    squares[me] = own_squares[...]

    def tell(j):
        return remote(squares.at[me], squares.at[me], sq_send.at[j], sq_recv.at[me], lax.rem(me + j, n))

    def told(j):
        o = lax.rem(me + n - j, n)
        return remote(squares.at[o], squares.at[o], sq_send.at[j], sq_recv.at[o], o)

    @pl.loop(1, n)
    def _(j):
        tell(j).start()

    for c in loads:
        c.wait()

    @pl.loop(1, n)
    def _(j):
        told(j).wait_recv()

    total = jnp.sum(squares[...], axis=0)[:1, :1]
    factor = jnp.minimum(1.0, 0.5 * lax.rsqrt(total / count + 1e-30))

    def whole(layer, kind, owner):
        return w_out[kind].at[layer, owner] if kind < 2 else w_out[2].at[layer, owner, kind - 2]

    def pass_on(i, layer, kind, t):
        o = here.device_at(-sign(kind) * t)
        block = whole(layer, kind, o)
        return remote(block, block, gat_send.at[i, t], gat_recv.at[i, t], here.device_at(sign(kind)))

    def across(i, layer, kind, t):
        o = here.device_at(-sign(kind) * t)
        block = whole(layer, kind, o)
        return remote(block, block, cross_send.at[i, t], cross_recv.at[i, t], here.partner)

    def across_in(i, layer, kind, t):
        o = here.chip_at(-sign(kind) * t) * 2 + 1 - core
        block = whole(layer, kind, o)
        return remote(block, block, cross_send.at[i, t], cross_recv.at[i, t], here.partner)

    for i, (layer, kind) in enumerate(streams):
        sel = (lambda r40, r64: r40.at[kind, layer] if kind < 2 else r64.at[layer, kind - 2])
        out = (lambda r: r[kind].at[layer] if kind < 2 else r[2].at[layer, kind - 2])
        g = wide(g40.at[kind, layer] if kind < 2 else g64.at[layer, pl.ds((kind - 2) * 64, 64)]) * factor
        w, m, v = adamw(wide(sel(w40, w64)), sel(m40, m64)[...], sel(v40, v64)[...], g)
        whole(layer, kind, me)[...] = w
        pass_on(i, layer, kind, 0).start()
        across(i, layer, kind, 0).start()
        out(m_out)[...] = m
        out(v_out)[...] = v

    @pl.loop(1, HOPS)
    def _(t):
        for i, (layer, kind) in enumerate(streams):
            pass_on(i, layer, kind, t - 1).wait_recv()
            pass_on(i, layer, kind, t).start()
            across(i, layer, kind, t).start()

    for i, (layer, kind) in enumerate(streams):
        pass_on(i, layer, kind, HOPS - 1).wait_recv()
        across(i, layer, kind, HOPS).start()

    @pl.loop(0, HOPS)
    def _(t):
        for i, (layer, kind) in enumerate(streams):
            pass_on(i, layer, kind, t).wait_send()

    @pl.loop(1, n)
    def _(j):
        tell(j).wait_send()

    @pl.loop(0, CHIPS)
    def _(t):
        for i, (layer, kind) in enumerate(streams):
            across(i, layer, kind, t).wait_send()
            across_in(i, layer, kind, t).wait_recv()


def comm(n, count, grads, ws, ms, vs):
    dma = pltpu.SemaphoreType.DMA
    scratch = [pltpu.VMEM((2, 2, 40, 2048), BF16), pltpu.VMEM((2, 2, 64, 640), BF16)]
    scratch += [pltpu.VMEM((2, 2, 40, 2048), F32), pltpu.VMEM((2, 2, 64, 640), F32)] * 2
    scratch += [pltpu.VMEM((n, 8, 128), F32), dma((9,)), dma((n,)), dma((n,))]
    scratch += [dma((8, HOPS)), dma((8, HOPS)), dma((8, CHIPS)), dma((8, CHIPS))]
    out_shape = [pltpu.VMEM((2, n, 40, 2048), BF16)] * 2 + [pltpu.VMEM((2, n, 2, 64, 640), BF16)]
    out_shape += [pltpu.VMEM(a.shape, F32) for a in (*ms, *vs)]
    return pl.pallas_call(
        lambda *refs: comm_kernel(n, count, *refs),
        out_shape=out_shape,
        in_specs=[pl.BlockSpec(memory_space=pltpu.VMEM)] * 3 + [ANY] * 9,
        out_specs=[pl.BlockSpec(memory_space=pltpu.VMEM)] * 9,
        scratch_shapes=scratch,
        compiler_params=pltpu.CompilerParams(collective_id=0, has_side_effects=True, vmem_limit_bytes=40 * MIB),
        name="comm",
    )(*grads, *ws, *ms, *vs)


def write_kernel(*refs):
    k = (len(refs) - 1) // 2
    copies = [pltpu.make_async_copy(refs[i], refs[k + i], refs[-1].at[i]) for i in range(k)]
    for c in copies:
        c.start()
    for c in copies:
        c.wait()


def write(arrays):
    return pl.pallas_call(
        write_kernel,
        out_shape=[jax.ShapeDtypeStruct(a.shape, a.dtype) for a in arrays],
        in_specs=[pl.BlockSpec(memory_space=pltpu.VMEM)] * len(arrays),
        out_specs=[ANY] * len(arrays),
        scratch_shapes=[pltpu.SemaphoreType.DMA((len(arrays),))],
        compiler_params=pltpu.CompilerParams(vmem_limit_bytes=MIB),
        name="write",
    )(*arrays)


def solution(mesh):
    n = mesh.shape["dp"]

    def body(x, dy, wg, wu, wd, mg, mu, md, vg, vu, vd):
        x, dy = x[0], dy[0]
        silu, slope, inner0, a0t, dyt, h1, a1 = forward(x, dy, wg, wu, wd)
        grads = backward(dy, a1, h1, dyt, a0t, wg, wu, wd, silu, slope, inner0)
        rows = lambda w: w.reshape(w.shape[0], n, -1, w.shape[2])
        ws = [rows(wg), rows(wu), wd.reshape(2, n, 2, 64, 640)]
        split = lambda t: t.reshape(2, 2, 64, 640)
        count = wg.size + wu.size + wd.size
        outs = write(comm(n, count, grads, ws, [mg, mu, split(md)], [vg, vu, split(vd)]))
        shapes = [wg, wu, wd, mg, mu, md, vg, vu, vd]
        return tuple(o.reshape(s.shape) for o, s in zip(outs, shapes, strict=True))

    whole, mine = P(), P(None, "dp", None)
    seq, out = P(("rep", "dp")), P("rep", "dp", None)
    return jax.shard_map(
        body,
        mesh=mesh,
        in_specs=(seq, seq) + (whole,) * 3 + (mine,) * 6,
        out_specs=(P("rep"),) * 3 + (out,) * 6,
        check_vma=False,
    )
```

time: 314 us -> 290 us (0.924)
  Pallas kernels: 302 us -> 287 us
  local copies, waits for them, and re-layouts: 10.4 us -> 2.15 us
    pallas_call x2, Pallas kernels: 205 us -> 193 us  [the longest x1 159 us: backward(): pl.pallas_call(backward_kernel, grid=(3 * half,), in_specs=[ANY] * 5 + [w...]
    unnamed x16 -> x6, local copies, waits for them, and re-layouts: 10.4 us -> 2.15 us
where the time goes in v5:
time: 290 us
  Pallas kernels  287 us (99%)
    pallas_call x1, Pallas kernels, backward(): pl.pallas_call(backward_kernel, grid=(3 * half,), in_specs=[ANY] * 5 + [w...  159 us
    pallas_call x1, Pallas kernels, comm(): pl.pallas_call(lambda *refs: comm_kernel(n, count, *refs), out_shape=out_...  87.5 us
    pallas_call x1, Pallas kernels, forward(): pl.pallas_call(forward_kernel, grid=(ff // WIDE,), in_specs=[whole(x.shap...  33.4 us
    pallas_call x1, Pallas kernels, write(): pl.pallas_call(write_kernel, out_shape=[jax.ShapeDtypeStruct(a.shape, a.d...  6.79 us

profile of v5, /device:TPU:0, one launch (start us, length us, event | category | flops | bytes accessed | tf_op | source)
XLA Modules:
  0.0 290.1 jit_solution(13557610123943275950)
XLA Ops:
  0.6 33.4 %forward.1 = (f32[2048,2048]{1,0:T(8,128)}, f32[2048,2048]{1,0:T(8,128)}, bf16[2048,2048]{1,0:T(8,128)(2,1)}, bf16[640,2048]{1,0:T(8,128)(2,1)}, bf16[640,2048]{...) custom-call(bf16[2048,640]{1,0:T(8,128)(2,1)} %bitcast.17, bf16[2048,640]{1,0:T(8,128)(2,1)} %bitcast.15, ...), custom_call_target="tpu_custom_call" | custom-call | tf_op jit(solution)/shard_map/forward/pallas_call | solution.py:93
  34.1 159.4 %backward.1 = (bf16[2,2,40,2048]{3,2,1,0:T(8,128)(2,1)S(1)}, bf16[2,128,640]{2,1,0:T(8,128)(2,1)S(1)}, f32[8,128]{1,0:T(8,128)S(1)}) custom-call(bf16[2048,640]{1,0:T(8,128)(2,1)} %bitcast.16, bf16[2048,640]{1,0:T(8,128)(2,1)} %get-tuple-element.37.a_in, bf16[2048,640]{1,0:T(8,128)(2,1)} %get-tuple-element.38.h_in, ...), custom_call_target="tpu_custom_call" | custom-call | tf_op jit(solution)/shard_map/backward/pallas_call | solution.py:560
  193.5 0.0 copy-start
  193.5 0.8 copy-done
  194.3 0.0 copy-start.1
  194.3 0.7 copy-done.1
  195.1 0.0 copy-start.2
  195.1 0.6 copy-done.2
  195.7 87.5 %comm.1 = (bf16[2,16,40,2048]{3,2,1,0:T(8,128)(2,1)S(1)}, bf16[2,16,40,2048]{3,2,1,0:T(8,128)(2,1)S(1)}, bf16[2,16,2,64,640]{4,3,2,1,0:T(8,128)(2,1)S(1)}, f32[2...) custom-call(bf16[2,2,40,2048]{3,2,1,0:T(8,128)(2,1)} %copy-done, ...), custom_call_target="tpu_custom_call" | custom-call | tf_op jit(solution)/shard_map/comm/pallas_call | solution.py:685
  283.2 6.8 %write.1 = (bf16[2,16,40,2048]{3,2,1,0:T(8,128)(2,1)}, bf16[2,16,40,2048]{3,2,1,0:T(8,128)(2,1)}, bf16[2,16,2,64,640]{4,3,2,1,0:T(8,128)(2,1)}, f32[2,40,2048]{2...) custom-call(bf16[2,16,40,2048]{3,2,1,0:T(8,128)(2,1)S(1)} %get-tuple, ...), custom_call_target="tpu_custom_call" | custom-call | tf_op jit(solution)/shard_map/write/pallas_call | solution.py:706
Async XLA Ops:
  193.5 0.8 copy-start
  194.3 0.7 copy-start.1
  195.1 0.6 copy-start.2

commit v6 on v5

--- a/solution.py
+++ b/solution.py
@@ -526,10 +526,10 @@
         stream.end40(4, g40)
         stream.on40(7)
         stream.out40(6)
+        stream.out40(7)
         stream.end40(5, g40)
+        stream.end40(6, g40)
         stream.last64(g64)
-        stream.out40(7)
-        stream.end40(6, g40)
         stream.end40(7, g40)
         stream.drain()
         total = jnp.sum(jnp.sum(stream.sq40[...], axis=0), keepdims=True) + jnp.sum(stream.sq64[...], keepdims=True)

time: 290 us -> 290 us (level)
  no operation moved by 1% of the time
where the time goes in v6:
time: 290 us
  Pallas kernels  287 us (99%)
    pallas_call x1, Pallas kernels, backward(): pl.pallas_call(backward_kernel, grid=(3 * half,), in_specs=[ANY] * 5 + [w...  159 us
    pallas_call x1, Pallas kernels, comm(): pl.pallas_call(lambda *refs: comm_kernel(n, count, *refs), out_shape=out_...  87.5 us
    pallas_call x1, Pallas kernels, forward(): pl.pallas_call(forward_kernel, grid=(ff // WIDE,), in_specs=[whole(x.shap...  33.4 us
    pallas_call x1, Pallas kernels, write(): pl.pallas_call(write_kernel, out_shape=[jax.ShapeDtypeStruct(a.shape, a.d...  6.79 us

profile of v6, /device:TPU:0, one launch (start us, length us, event | category | flops | bytes accessed | tf_op | source)
XLA Modules:
  0.0 290.1 jit_solution(2194085526757201977)
XLA Ops:
  0.6 33.4 %forward.1 = (f32[2048,2048]{1,0:T(8,128)}, f32[2048,2048]{1,0:T(8,128)}, bf16[2048,2048]{1,0:T(8,128)(2,1)}, bf16[640,2048]{1,0:T(8,128)(2,1)}, bf16[640,2048]{...) custom-call(bf16[2048,640]{1,0:T(8,128)(2,1)} %bitcast.17, bf16[2048,640]{1,0:T(8,128)(2,1)} %bitcast.15, ...), custom_call_target="tpu_custom_call" | custom-call | tf_op jit(solution)/shard_map/forward/pallas_call | solution.py:93
  34.1 159.4 %backward.1 = (bf16[2,2,40,2048]{3,2,1,0:T(8,128)(2,1)S(1)}, bf16[2,128,640]{2,1,0:T(8,128)(2,1)S(1)}, f32[8,128]{1,0:T(8,128)S(1)}) custom-call(bf16[2048,640]{1,0:T(8,128)(2,1)} %bitcast.16, bf16[2048,640]{1,0:T(8,128)(2,1)} %get-tuple-element.37.a_in, bf16[2048,640]{1,0:T(8,128)(2,1)} %get-tuple-element.38.h_in, ...), custom_call_target="tpu_custom_call" | custom-call | tf_op jit(solution)/shard_map/backward/pallas_call | solution.py:560
  193.5 0.0 copy-start
  193.5 0.8 copy-done
  194.3 0.0 copy-start.1
  194.3 0.7 copy-done.1
  195.1 0.0 copy-start.2
  195.1 0.6 copy-done.2
  195.7 87.5 %comm.1 = (bf16[2,16,40,2048]{3,2,1,0:T(8,128)(2,1)S(1)}, bf16[2,16,40,2048]{3,2,1,0:T(8,128)(2,1)S(1)}, bf16[2,16,2,64,640]{4,3,2,1,0:T(8,128)(2,1)S(1)}, f32[2...) custom-call(bf16[2,2,40,2048]{3,2,1,0:T(8,128)(2,1)} %copy-done, ...), custom_call_target="tpu_custom_call" | custom-call | tf_op jit(solution)/shard_map/comm/pallas_call | solution.py:685
  283.2 6.8 %write.1 = (bf16[2,16,40,2048]{3,2,1,0:T(8,128)(2,1)}, bf16[2,16,40,2048]{3,2,1,0:T(8,128)(2,1)}, bf16[2,16,2,64,640]{4,3,2,1,0:T(8,128)(2,1)}, f32[2,40,2048]{2...) custom-call(bf16[2,16,40,2048]{3,2,1,0:T(8,128)(2,1)S(1)} %get-tuple, ...), custom_call_target="tpu_custom_call" | custom-call | tf_op jit(solution)/shard_map/write/pallas_call | solution.py:706
Async XLA Ops:
  193.5 0.8 copy-start
  194.3 0.7 copy-start.1
  195.1 0.6 copy-start.2
